TPU v7x, 32 devices: a whole 2x2x4 slice. The times are simulated.
32 devices in a mesh: dp: 4 (over x, core), ctx: 2 (over y), head: 4 (over z).
Axes of the slice: x: 2, y: 2, z: 4, core: 2. Of those that a mesh axis runs over, the one named last changes fastest.
Arguments:
- latent: bfloat16 [4, 256, 512], P('dp', 'ctx'), may hold values from -6 to 6
- rope: bfloat16 [4, 256, 64], P('dp', 'ctx'), may hold values from -6 to 6
- query: bfloat16 [4, 256, 12288], P('dp', 'ctx', 'head'), may hold values from -9 to 9
- grad_out: bfloat16 [4, 256, 8192], P('dp', 'ctx', 'head'), may hold values from -6 to 6
- attn_out: bfloat16 [4, 256, 8192], P('dp', 'ctx', 'head'), may hold values from -40 to 40
- lse: float32 [4, 64, 256], P('dp', 'head', 'ctx'), may hold values from -100 to 100, as said below
- positions: int32 [4, 256], P('dp'), may hold values from 0 to 255, as said below
- w_uk: bfloat16 [512, 8192], P(None, 'head'), may hold values from -2 to 2
- w_uv: bfloat16 [512, 8192], P(None, 'head'), may hold values from -2 to 2
Outputs:
- grad_query: bfloat16 [4, 256, 12288], P('dp', 'ctx', 'head')
- grad_latent: float32 [4, 256, 512], P('dp', 'ctx')
- grad_rope: float32 [4, 256, 64], P('dp', 'ctx')
- grad_wuk: bfloat16 [512, 8192], P(('dp', 'ctx'), 'head')
- grad_wuv: bfloat16 [512, 8192], P(('dp', 'ctx'), 'head')
Inputs may be any that keep to these rules, and one draw needn't show every extreme that they name: Each sequence's row is a permutation of 0 to 255 made of runs of 64 consecutive positions, each run filling an aligned run of 64 rows in rising order; which run goes to which rows is drawn. lse[h, i] is the log of the sum of exp(scores[i, j]) over the keys j with positions[j] <= positions[i].
All inputs are finite; a program needn't handle non-finite values.
Results may differ from a plain program's by a relative error of at most 0.02.
Values may be sent and summed in bfloat16 or wider, within the bound.
No kernel may reach another device: no remote copies, remote signals or barrier semaphores. Data moves between devices by JAX's collectives and lax.ppermute only.
A program may use at most 64 MiB of HBM per device.

v0:
```python
import math

import jax
import jax.numpy as jnp
from jax import lax
from jax.sharding import PartitionSpec as P

DR = 64
DN = 128
DV = 128


MASKED = -1e30


def shortened(shard):
    return jax.tree.map(lambda a: a.astype(jnp.bfloat16) if a.dtype == jnp.float32 else a, shard)


def shifted(value, axis, steps):
    count = lax.axis_size(axis)
    pairs = [(source, (source + steps) % count) for source in range(count)]
    return lax.ppermute(value, axis, pairs)


def block_grads(
    queries, grads, lse_rows, delta_rows, query_pos, key_rows, value_rows, key_pos, score_scale
):
    scores = (
        jnp.einsum("grd,gsd->grs", queries, key_rows, preferred_element_type=jnp.float32)
        * score_scale
    )
    allowed = key_pos[None, None, :] <= query_pos[None, :, None]
    weights = jnp.exp(jnp.where(allowed, scores - lse_rows[:, :, None], MASKED))
    dots = jnp.einsum("grd,gsd->grs", grads, value_rows, preferred_element_type=jnp.float32)
    score_grad = (weights * (dots - delta_rows[:, :, None]) * score_scale).astype(jnp.bfloat16)
    weights_b = weights.astype(jnp.bfloat16)
    return (score_grad, weights_b)


def head_grads(
    queries, grads, lse_rows, delta_rows, query_pos, key_rows, value_rows, key_pos, score_scale
):
    score_grad, weights_b = block_grads(
        queries, grads, lse_rows, delta_rows, query_pos, key_rows, value_rows, key_pos, score_scale
    )
    query_grad = jnp.einsum(
        "grs,gsd->grd", score_grad, key_rows, preferred_element_type=jnp.float32
    )
    key_grad = jnp.einsum("grs,grd->gsd", score_grad, queries, preferred_element_type=jnp.float32)
    value_grad = jnp.einsum("grs,grd->gsd", weights_b, grads, preferred_element_type=jnp.float32)
    return (query_grad, key_grad, value_grad)


def guarded_grads(
    queries, grads, lse_rows, delta_rows, query_pos, key_rows, value_rows, key_pos, score_scale
):

    def skipped():
        return (
            jnp.zeros(queries.shape, jnp.float32),
            jnp.zeros(key_rows.shape, jnp.float32),
            jnp.zeros(value_rows.shape, jnp.float32),
        )

    def computed():
        return head_grads(
            queries,
            grads,
            lse_rows,
            delta_rows,
            query_pos,
            key_rows,
            value_rows,
            key_pos,
            score_scale,
        )

    return lax.cond(jnp.min(key_pos) > jnp.max(query_pos), skipped, computed)


def rotate(blocks, stat_rows, direction, last_step):
    if not last_step:
        blocks = jax.tree.map(
            lambda part, own: part.astype(own.dtype),
            shifted(shortened(blocks), "ctx", direction),
            blocks,
        )
    stat_rows = shifted(stat_rows, "ctx", direction)
    return (blocks, stat_rows)


def head_major(flat, row_count, head_count, width):
    return flat.reshape(row_count, head_count, width).transpose(1, 0, 2)


def row_major(stacked):
    return stacked.transpose(1, 0, 2).reshape(stacked.shape[1], stacked.shape[0] * stacked.shape[2])


def on_device(latent, rope, query, grad_out, attn_out, lse, positions, w_uk, w_uv):
    latent_rows = latent[0]
    row_count = latent_rows.shape[0]
    head_count = w_uk.shape[1] // DN
    score_scale = 1.0 / math.sqrt(DN + DR)
    highest = lax.Precision.HIGHEST
    cycle_size = lax.axis_size("ctx")
    my_index = lax.axis_index("ctx")
    seq_order = positions[0]
    key_pos = lax.dynamic_slice_in_dim(seq_order, my_index * row_count, row_count)
    queries = head_major(query[0], row_count, head_count, DN + DR)
    grads = head_major(grad_out[0], row_count, head_count, DV)
    outputs = head_major(attn_out[0], row_count, head_count, DV)
    delta_rows = jnp.sum(grads.astype(jnp.float32) * outputs.astype(jnp.float32), axis=2)
    lse_rows = lse[0]
    nope_keys = head_major(
        jnp.dot(latent_rows, w_uk, preferred_element_type=jnp.float32).astype(jnp.bfloat16),
        row_count,
        head_count,
        DN,
    )
    value_rows = head_major(
        jnp.dot(latent_rows, w_uv, preferred_element_type=jnp.float32).astype(jnp.bfloat16),
        row_count,
        head_count,
        DV,
    )
    rope_keys = jnp.broadcast_to(rope[0][None, :, :], (head_count, row_count, DR))
    key_rows = jnp.concatenate([nope_keys, rope_keys], axis=2)
    groups = ((0, head_count, 1),)
    blocks = [(queries, grads) for first_head, last_head, direction in groups]
    stat_rows = [
        (jnp.zeros((last_head - first_head, row_count, DN + DR), jnp.float32), lse_rows, delta_rows)
        for first_head, last_head, direction in groups
    ]
    key_parts = [
        jnp.zeros((last_head - first_head, row_count, DN + DR), jnp.float32)
        for first_head, last_head, direction in groups
    ]
    value_parts = [
        jnp.zeros((last_head - first_head, row_count, DV), jnp.float32)
        for first_head, last_head, direction in groups
    ]
    for cycle_step in range(cycle_size):
        first_head, last_head, direction = groups[0]
        source = (my_index - direction * cycle_step) % cycle_size
        query_pos = lax.dynamic_slice_in_dim(seq_order, source * row_count, row_count)
        block_query, block_output_grads = blocks[0]
        query_acc, block_lse, block_delta = stat_rows[0]
        query_grad, key_grad, value_grad = guarded_grads(
            block_query,
            block_output_grads,
            block_lse,
            block_delta,
            query_pos,
            key_rows,
            value_rows,
            key_pos,
            score_scale,
        )
        key_parts[0] = key_parts[0] + key_grad
        value_parts[0] = value_parts[0] + value_grad
        blocks[0], stat_rows[0] = rotate(
            blocks[0],
            (query_acc + query_grad, block_lse, block_delta),
            direction,
            cycle_step + 1 == cycle_size,
        )
    query_total = jnp.concatenate([entry[0] for entry in stat_rows], axis=0)
    key_total = key_parts[0]
    value_total = value_parts[0]
    key_nope = row_major(key_total[:, :, :DN])
    value_flat = row_major(value_total)
    rope_part = jnp.sum(key_total[:, :, DN:], axis=0)
    latent_part = jnp.dot(key_nope, w_uk.astype(jnp.float32).T, precision=highest) + jnp.dot(
        value_flat, w_uv.astype(jnp.float32).T, precision=highest
    )
    latent_f = latent_rows.astype(jnp.float32).T
    weight_uk = jnp.dot(latent_f, key_nope, precision=highest)
    weight_uv = jnp.dot(latent_f, value_flat, precision=highest)
    latent_grad, rope_grad = (
        lax.psum(latent_part.astype(jnp.bfloat16), "head").astype(jnp.float32),
        lax.psum(rope_part.astype(jnp.bfloat16), "head").astype(jnp.float32),
    )
    weight_uk, weight_uv = (
        lax.psum_scatter(weight_uk, ("dp", "ctx"), scatter_dimension=0, tiled=True),
        lax.psum_scatter(weight_uv, ("dp", "ctx"), scatter_dimension=0, tiled=True),
    )
    query_out = row_major(query_total).astype(jnp.bfloat16)
    return (
        query_out[None],
        latent_grad[None],
        rope_grad[None],
        weight_uk.astype(jnp.bfloat16),
        weight_uv.astype(jnp.bfloat16),
    )


def solution(mesh):
    return jax.shard_map(
        on_device,
        mesh=mesh,
        in_specs=(
            P("dp", "ctx", None),
            P("dp", "ctx", None),
            P("dp", "ctx", "head"),
            P("dp", "ctx", "head"),
            P("dp", "ctx", "head"),
            P("dp", "head", "ctx"),
            P("dp", None),
            P(None, "head"),
            P(None, "head"),
        ),
        out_specs=(
            P("dp", "ctx", "head"),
            P("dp", "ctx", None),
            P("dp", "ctx", None),
            P(("dp", "ctx"), "head"),
            P(("dp", "ctx"), "head"),
        ),
        check_vma=False,
    )
```

profile of v0, /device:TPU:0, one launch (start us, length us, event | category | flops | bytes accessed | tf_op | source)
XLA Modules:
  0.0 201.4 jit_solution(4418443518932257076)
XLA Ops:
  8.1 3.1 %collective-permute-start.2 = (f32[16,128]{1,0:T(8,128)}, f32[16,128]{1,0:T(8,128)}, u32[]{:S(2)}, u32[]{:S(2)}) collective-permute-start(f32[16,128]{1,0:T(8,128)} %bitcast.100), channel_id=1, source_target_pairs={{0,4},{4,0},{1,5},{5,1},{2,6},{6,2},{3,7},{7,3},{8,12},{12,8},{9,1... | collective-permute-start | bytes 24584 | tf_op jit(solution)/shard_map/ppermute | solution.py:23
  11.1 2.0 %copy.40 = bf16[1,128,2048]{1,2,0:T(8,128)(2,1)} copy(bf16[1,128,2048]{2,1,0:T(8,128)(2,1)} %param.16) | data formatting | bytes 1048576 | tf_op args[3]
  14.5 1.9 collective-permute-start.1
  16.6 1.8 fusion.20
  19.5 2.8 %fusion.16 = bf16[16,16,8,128]{3,2,1,0:T(8,128)(2,1)} fusion(bf16[512,2048]{1,0:T(8,128)(2,1)} %param.21, bf16[1,128,512]{2,1,0:T(8,128)(2,1)S(1)} %copy-done.11), kind=kOutput, calls=%fused_computation.26 | convolution fusion | flops 268697600 | bytes 2752512 | tf_op jit(solution)/shard_map/dot_general | solution.py:123
  27.3 7.5 %conditional.2 = (f32[16,128,192]{1,2,0:T(8,128)S(1)}, f32[16,128,192]{1,2,0:T(8,128)S(1)}, f32[16,128,128]{1,2,0:T(8,128)S(1)}) conditional(s32[]{:T(128)} %convert_element_type.69, (s32[128]{0:T(128)S(1)}, s32[1,128]{1,0:T(1,128)}, bf16[16,128,192]{1,2,0:T(8,128)(2,1)}, bf16[16,128,192]{1,2,0:T(8,128)(2,1)S(1)}, f32[1,16,128]{2,1,0:T(8,128)}, ...), branch_computations={%region_3.4_spmd, %region_4.5_spmd} | conditional | flops 438321152 | bytes 13681688 | solution.py:79
  28.1 1.8 fusion.4
  29.9 1.6 fusion.5
  31.5 1.3 fusion.6
  32.9 1.5 fusion.30
  34.9 9.0 %collective-permute-done.4 = f32[16,128]{1,0:T(8,128)S(1)} collective-permute-done((f32[16,128]{1,0:T(8,128)}, f32[16,128]{1,0:T(8,128)S(1)}, u32[]{:S(2)}, u32[]{:S(2)}) %collective-permute-start.4) | collective-permute-done | bytes 8224 | tf_op jit(solution)/shard_map/ppermute | solution.py:23
  43.9 8.0 %conditional.3 = (f32[16,128,192]{1,2,0:T(8,128)S(1)}, f32[16,128,192]{1,2,0:T(8,128)}, f32[16,128,128]{1,2,0:T(8,128)S(1)}) conditional(s32[]{:T(128)} %convert_element_type.76, (s32[128]{0:T(128)S(1)}, s32[1,128]{1,0:T(1,128)S(1)}, bf16[16,128,192]{1,2,0:T(8,128)(2,1)}, bf16[16,128,192]{1,2,0:T(8,128)(2,1)S(1)}, f32[16,128]{1,0:T(8,128)}, ...), branch_computations={%region_6.7_spmd, %region_7.8_spmd} | conditional | flops 438321152 | bytes 13681688 | solution.py:79
  44.0 1.8 fusion.12
  45.8 1.6 fusion.13
  47.4 1.3 fusion.14
  48.8 2.7 %fusion.32 = f32[16,128,192]{1,2,0:T(8,128)} fusion(bf16[16,128,192]{1,2,0:T(8,128)(2,1)} %get-tuple-element.44, bf16[16,128,128]{2,1,0:T(8,128)(2,1)S(1)} %fusion.13), kind=kOutput, calls=%fused_computation.51 | convolution fusion | flops 100663296 | bytes 2883584 | tf_op jit(solution)/shard_map/cond/branch_0_fun/grs,grd->gsd/dot_general | solution.py:50
  53.4 2.1 %add.43 = f32[16,128,192]{1,2,0:T(8,128)S(1)} add(f32[16,128,192]{1,2,0:T(8,128)} %copy-done.5, f32[16,128,192]{1,2,0:T(8,128)} %get-tuple-element.64) | non-fusion elementwise | flops 393216 | bytes 4718592 | tf_op jit(solution)/shard_map/add | solution.py:161
  55.5 2.3 %fusion.33 = f32[128,512]{1,0:T(8,128)S(1)} fusion(f32[128,2048]{0,1:T(8,128)S(1)} %bitcast.89, bf16[512,2048]{1,0:T(8,128)(2,1)S(1)} %copy-done), kind=kOutput, calls=%fused_computation.52 | convolution fusion | flops 1610612736 | bytes 3407872 | tf_op jit(solution)/shard_map/dot_general | solution.py:175
  58.1 1.4 copy-done.3
  59.5 2.9 %fusion.18 = bf16[1,128,512]{2,1,0:T(8,128)(2,1)} fusion(f32[128,512]{1,0:T(8,128)S(1)} %fusion.33, f32[128,2048]{0,1:T(8,128)S(1)} %bitcast.87, bf16[512,2048]{1,0:T(8,128)(2,1)S(1)} %copy-done.3), kind=kOutput, calls=%fused_computation.29 | convolution fusion | flops 1610743808 | bytes 3538944 | tf_op jit(solution)/shard_map/dot_general | solution.py:175
  62.7 3.8 %convolution_bitcast_fusion = f32[512,2048]{0,1:T(8,128)} fusion(f32[128,2048]{0,1:T(8,128)S(1)} %bitcast.88, bf16[1,128,512]{2,1,0:T(8,128)(2,1)S(1)} %copy-done.11), kind=kOutput, calls=%fused_computation.22 | convolution fusion | flops 1610612736 | bytes 5373952 | tf_op jit(solution)/shard_map/dot_general | solution.py:180
  66.5 5.4 %copy.57 = f32[512,2048]{1,0:T(8,128)} copy(f32[512,2048]{0,1:T(8,128)} %convolution_bitcast_fusion) | data formatting | bytes 8388608
  73.1 3.8 %convolution_bitcast_fusion.1 = f32[512,2048]{0,1:T(8,128)} fusion(f32[128,2048]{0,1:T(8,128)S(1)} %bitcast.90, bf16[1,128,512]{2,1,0:T(8,128)(2,1)S(1)} %copy-done.11), kind=kOutput, calls=%fused_computation.23 | convolution fusion | flops 1610612736 | bytes 5373952 | tf_op jit(solution)/shard_map/dot_general | solution.py:179
  76.8 5.9 %copy.55 = f32[512,2048]{1,0:T(8,128)} copy(f32[512,2048]{0,1:T(8,128)} %convolution_bitcast_fusion.1) | data formatting | bytes 8388608
  82.8 47.8 %collective-permute-done = f32[16,128,192]{1,2,0:T(8,128)S(1)} collective-permute-done((f32[16,128,192]{1,2,0:T(8,128)}, f32[16,128,192]{1,2,0:T(8,128)S(1)}, u32[]{:S(2)}, u32[]{:S(2)}) %collective-permute-start) | collective-permute-done | bytes 1572896 | tf_op jit(solution)/shard_map/ppermute | solution.py:23
  130.6 2.5 %add.42 = bf16[16,128,192]{1,2,0:T(8,128)(2,1)} add(f32[16,128,192]{1,2,0:T(8,128)S(1)} %collective-permute-done, f32[16,128,192]{1,2,0:T(8,128)} %copy-done.6) | non-fusion elementwise | flops 393216 | bytes 3932160 | tf_op jit(solution)/shard_map/add | solution.py:165
  133.1 1.6 collective-permute-start.5
  135.8 19.4 %psum.15 = bf16[1,128,64]{1,2,0:T(8,128)(2,1)S(1)} all-reduce(bf16[1,128,64]{1,2,0:T(8,128)(2,1)S(1)} %bitcast.96), channel_id=1, replica_groups=mesh['dp'=4,'ctx'=2,'head'=4] {'head'}, use_global_device_ids=true, to_apply=%region_10.11 | all-reduce | flops 8192 | bytes 32768 | tf_op jit(solution)/shard_map/psum | solution.py:183
  155.9 1.6 broadcast_in_dim.50
  158.7 1.3 copy.58
  160.9 30.8 %reduce-scatter.7.cloned.1.call-done = f32[64,2048]{1,0:T(8,128)} async-done(((f32[512,2048]{1,0:T(8,128)}), f32[64,2048]{1,0:T(8,128)}) %reduce-scatter.7.cloned.1.call-update) | async-done | bytes 524304
  191.7 1.3 copy.56
  (67 shorter events, 14.7 us)
Async XLA Ops:
  8.0 10.6 %copy-start = (bf16[512,2048]{1,0:T(8,128)(2,1)S(1)}, bf16[512,2048]{1,0:T(8,128)(2,1)}, u32[]{:S(2)}) copy-start(bf16[512,2048]{1,0:T(8,128)(2,1)} %param.20) | copy-start | bytes 6291460
  8.0 5.3 %copy-start.13 = (bf16[1,128,3072]{2,1,0:T(8,128)(2,1)S(1)}, bf16[1,128,3072]{2,1,0:T(8,128)(2,1)}, u32[]{:S(2)}) copy-start(bf16[1,128,3072]{2,1,0:T(8,128)(2,1)} %param.15) | copy-start | bytes 2359300
  8.0 8.3 %copy-start.14 = (bf16[1,128,2048]{2,1,0:T(8,128)(2,1)S(1)}, bf16[1,128,2048]{2,1,0:T(8,128)(2,1)}, u32[]{:S(2)}) copy-start(bf16[1,128,2048]{2,1,0:T(8,128)(2,1)} %param.17) | copy-start | bytes 1572868
  8.0 147.8 %all-reduce.2.cloned.1.call-start = ((), (), s32[]{:S(2)}) async-start(), calls=%async_computation.2 | async-start | bytes 262144 | tf_op jit(solution)/shard_map/psum | solution.py:182
  8.1 26.8 %collective-permute-start.2 = (f32[16,128]{1,0:T(8,128)}, f32[16,128]{1,0:T(8,128)}, u32[]{:S(2)}, u32[]{:S(2)}) collective-permute-start(f32[16,128]{1,0:T(8,128)} %bitcast.100), channel_id=1, source_target_pairs={{0,4},{4,0},{1,5},{5,1},{2,6},{6,2},{3,7},{7,3},{8,12},{12,8},{9,1... | collective-permute-start | bytes 24584 | tf_op jit(solution)/shard_map/ppermute | solution.py:23
  13.2 5.4 %copy-start.11 = (bf16[1,128,512]{2,1,0:T(8,128)(2,1)S(1)}, bf16[1,128,512]{2,1,0:T(8,128)(2,1)}, u32[]{:S(2)}) copy-start(bf16[1,128,512]{2,1,0:T(8,128)(2,1)} %param.13) | copy-start | bytes 393220
  13.2 30.6 %collective-permute-start.3 = (bf16[16,128,128]{1,2,0:T(8,128)(2,1)}, bf16[16,128,128]{1,2,0:T(8,128)(2,1)}, u32[]{:S(2)}, u32[]{:S(2)}) collective-permute-start(bf16[16,128,128]{1,2,0:T(8,128)(2,1)} %bitcast.11), channel_id=1, source_target_pairs={{0,4},{4,0},{1,5},{5,1},{2,6},{6,2},{3,7},{7,3},{8,12},{12,8},{9,1... | collective-permute-start | bytes 1572872 | tf_op jit(solution)/shard_map/ppermute | solution.py:23
  14.5 29.3 %collective-permute-start.1 = (bf16[16,128,192]{1,2,0:T(8,128)(2,1)}, bf16[16,128,192]{1,2,0:T(8,128)(2,1)}, u32[]{:S(2)}, u32[]{:S(2)}) collective-permute-start(bf16[16,128,192]{1,2,0:T(8,128)(2,1)} %bitcast.5), channel_id=1, source_target_pairs={{0,4},{4,0},{1,5},{5,1},{2,6},{6,2},{3,7},{7,3},{8,12},{12,8},{9,1... | collective-permute-start | bytes 2359304 | tf_op jit(solution)/shard_map/ppermute | solution.py:23
  18.4 1.0 copy-start.15
  18.4 25.4 %collective-permute-start.4 = (f32[16,128]{1,0:T(8,128)}, f32[16,128]{1,0:T(8,128)S(1)}, u32[]{:S(2)}, u32[]{:S(2)}) collective-permute-start(f32[16,128]{1,0:T(8,128)} %fusion.20), channel_id=1, source_target_pairs={{0,4},{4,0},{1,5},{5,1},{2,6},{6,2},{3,7},{7,3},{8,12},{12,8},{9,1... | collective-permute-start | bytes 24584 | tf_op jit(solution)/shard_map/ppermute | solution.py:23
  19.5 2.9 %copy-start.16 = (s32[1,256]{1,0:T(1,128)S(1)}, s32[1,256]{1,0:T(1,128)}, u32[]{:S(2)}) copy-start(s32[1,256]{1,0:T(1,128)} %param.19) | copy-start | bytes 3076
  34.8 9.0 %copy-start.5 = (f32[16,128,192]{1,2,0:T(8,128)}, f32[16,128,192]{1,2,0:T(8,128)S(1)}, u32[]{:S(2)}) copy-start(f32[16,128,192]{1,2,0:T(8,128)S(1)} %get-tuple-element.63) | copy-start | bytes 4718596
  34.8 9.0 %copy-start.12 = (f32[16,128,192]{1,2,0:T(8,128)}, f32[16,128,192]{1,2,0:T(8,128)S(1)}, u32[]{:S(2)}) copy-start(f32[16,128,192]{1,2,0:T(8,128)S(1)} %get-tuple-element.61) | copy-start | bytes 4718596
  34.8 9.0 %copy-start.7 = (f32[16,128,128]{1,2,0:T(8,128)}, f32[16,128,128]{1,2,0:T(8,128)S(1)}, u32[]{:S(2)}) copy-start(f32[16,128,128]{1,2,0:T(8,128)S(1)} %get-tuple-element.114) | copy-start | bytes 3145732
  51.9 1.1 copy-start.6
  51.9 1.5 copy-start.9
  55.4 2.5 %copy-start.4 = (f32[16,128,192]{1,2,0:T(8,128)}, f32[16,128,192]{1,2,0:T(8,128)S(1)}, u32[]{:S(2)}) copy-start(f32[16,128,192]{1,2,0:T(8,128)S(1)} %add.43) | copy-start | bytes 4718596
  55.5 2.4 %copy-start.1 = (f32[16,128,128]{1,2,0:T(8,128)}, f32[16,128,128]{1,2,0:T(8,128)S(1)}, u32[]{:S(2)}) copy-start(f32[16,128,128]{1,2,0:T(8,128)S(1)} %slice.8) | copy-start | bytes 3145732
  55.5 2.4 %copy-start.8 = (f32[16,128,128]{1,2,0:T(8,128)S(1)}, f32[16,128,128]{1,2,0:T(8,128)}, u32[]{:S(2)}) copy-start(f32[16,128,128]{1,2,0:T(8,128)} %copy-done.7) | copy-start | bytes 3145732
  55.5 2.4 %copy-start.10 = (f32[16,128,128]{1,2,0:T(8,128)S(1)}, f32[16,128,128]{1,2,0:T(8,128)}, u32[]{:S(2)}) copy-start(f32[16,128,128]{1,2,0:T(8,128)} %copy-done.9) | copy-start | bytes 3145732
  57.9 1.6 copy-start.3
  62.5 96.2 %reduce-scatter.9.cloned.1.call-start = ((), (), s32[]{:S(2)}) async-start(), calls=%async_computation.4 | async-start | bytes 4718592
  71.9 1.2 copy-start.2
  71.9 119.8 %reduce-scatter.7.cloned.1.call-start = ((), (), s32[]{:S(2)}) async-start(), calls=%async_computation.3 | async-start | bytes 4718592
  82.7 47.8 %collective-permute-start = (f32[16,128,192]{1,2,0:T(8,128)}, f32[16,128,192]{1,2,0:T(8,128)S(1)}, u32[]{:S(2)}, u32[]{:S(2)}) collective-permute-start(f32[16,128,192]{1,2,0:T(8,128)} %copy-done.12), channel_id=1, source_target_pairs={{0,4},{4,0},{1,5},{5,1},{2,6},{6,2},{3,7},{7,3},{8,12},{12,8},{9,1... | collective-permute-start | bytes 4718600 | tf_op jit(solution)/shard_map/ppermute | solution.py:23
  133.1 24.4 %collective-permute-start.5 = (bf16[16,128,192]{1,2,0:T(8,128)(2,1)}, bf16[16,128,192]{1,2,0:T(8,128)(2,1)S(1)}, u32[]{:S(2)}, u32[]{:S(2)}) collective-permute-start(bf16[16,128,192]{1,2,0:T(8,128)(2,1)} %add.42), channel_id=1, source_target_pairs={{0,4},{4,0},{1,5},{5,1},{2,6},{6,2},{3,7},{7,3},{8,12},{12,8},{9,1... | collective-permute-start | bytes 2359304 | tf_op jit(solution)/shard_map/ppermute | solution.py:23
Sparse Core Ops, SparseCore 0:
  62.6 35.0 all-reduce.1
Sparse Core Ops, SparseCore 1:
  72.0 65.1 reduce-scatter.8
  140.3 51.3 reduce-scatter.6
where the time goes:
time: 202 us; the launch traced here: 201 us
  waiting for transfers between devices  87.6 us (43%)
  matrix products  30.7 us (15%)
  local copies, waits for them, and re-layouts  26 us (13%)
  blocking collectives  19.4 us (10%)
  between operations  18.4 us (9%)
  other arithmetic  11.9 us (6%)
  starting transfers between devices  7.23 us (4%)
    ppermute x6, waiting for transfers between devices, shifted(): return lax.ppermute(value, axis, pairs)  56.7 us
    unnamed x5, waiting for transfers between devices  30.9 us
    unnamed x44, local copies, waits for them, and re-layouts  24.5 us
    psum x1, blocking collectives, on_device(): lax.psum(rope_part.astype(jnp.bfloat16), 'head').astype(jnp.float32)  19.4 us
    ppermute x6, starting transfers between devices, shifted(): return lax.ppermute(value, axis, pairs)  6.92 us
    dot_general x2, matrix products, head_grads(): jnp.einsum('grs,grd->gsd', score_grad, queries, preferred_element_type=jn...  4.15 us
  transfers between devices with their start and end apart: 9, of which 3 were waited for; matrix products, arithmetic and copies ran while one was open for 23% of the time, Pallas kernels for 0%

commit v1 on v0

v1 whole, which is shorter than its diff:
```python
import functools
import math

import jax
import jax.numpy as jnp
import numpy as np
from jax import lax
from jax.experimental import pallas as pl
from jax.experimental.pallas import tpu as pltpu
from jax.sharding import PartitionSpec as P

DR = 64
DN = 128
DV = 128
DQ = DN + DR

MASKED = -1e30
NT = (((1,), (1,)), ((), ()))


def bits_of(count):
    return [1 << b for b in range(count.bit_length() - 1)]


def stage_orders(dp_size, ctx_size):
    outer = [("dp", bit) for bit in bits_of(dp_size)[1:]]
    inner = [("ctx", bit) for bit in bits_of(ctx_size)]
    return outer + inner, inner + outer


def row_table(dp_size, ctx_size, rows):
    orders = stage_orders(dp_size, ctx_size)
    blocks = dp_size * ctx_size
    width = rows // blocks
    table = np.zeros((blocks, rows), np.int32)
    for dp in range(dp_size):
        for ctx in range(ctx_size):
            for place in range(blocks):
                digits = [(place >> b) & 1 for b in reversed(range(blocks.bit_length() - 1))]
                target = {"dp": dp, "ctx": ctx}
                if digits[0] == 0:
                    target["dp"] ^= 1
                for digit, (axis, bit) in zip(digits[1:], orders[target["dp"] & 1]):
                    if digit == 0:
                        target[axis] ^= bit
                block = target["dp"] * ctx_size + target["ctx"]
                table[dp * ctx_size + ctx, place * width:(place + 1) * width] = (
                    block * width + np.arange(width)
                )
    return table


def stage_pairs(stage, dp_size, ctx_size):
    pairs = []
    orders = stage_orders(dp_size, ctx_size)
    for dp in range(dp_size):
        for ctx in range(ctx_size):
            place = {"dp": dp, "ctx": ctx}
            axis, bit = ("dp", 1) if stage == 0 else orders[dp & 1][stage - 1]
            place[axis] ^= bit
            pairs.append((dp * ctx_size + ctx, place["dp"] * ctx_size + place["ctx"]))
    return pairs


def dot(a, b):
    return jnp.dot(a, b, preferred_element_type=jnp.float32)


def dot_nt(a, b):
    return lax.dot_general(a, b, NT, preferred_element_type=jnp.float32)


def grads_body(place_ref, pos_ref, order_ref, latent_ref, rope_ref, query_ref, grad_ref, out_ref,
               lse_ref, wuk_ref, wuv_ref, *rest, heads, chunk_start, has_prior, final):
    if has_prior:
        prior_ref, _, *rest = rest
    dq_ref, send_ref, keep_ref, total_ref, flat_ref, bias_ref, acc_ref, rope_acc_ref = rest
    step = pl.program_id(0)
    steps = pl.num_programs(0)
    tokens = latent_ref.shape[0]
    rows = query_ref.shape[0]
    scale = 1.0 / math.sqrt(DQ)
    latent = latent_ref[...]
    rope = rope_ref[...]

    @pl.when(step == 0)
    def _():
        width = latent_ref.shape[1]
        spot = lax.broadcasted_iota(jnp.int32, (width, width), 0)
        pick = jnp.where(spot == order_ref[0], 1.0, 0.0).astype(jnp.bfloat16)
        flat_ref[...] = dot(latent, pick).T.astype(jnp.bfloat16)
        mine = place_ref[1]
        count = tokens // rows
        own_pos = pos_ref[mine]
        for chunk in range(count):
            key_pos = pos_ref[lax.rem(mine + chunk, count)]
            key_col = jnp.broadcast_to(key_pos, (rows, rows)).T
            bias_ref[chunk * rows:(chunk + 1) * rows, :] = jnp.where(
                key_col <= jnp.broadcast_to(own_pos, (rows, rows)), 0.0, MASKED
            )
        if has_prior:
            acc_ref[...] = prior_ref[:, :width]
            rope_acc_ref[...] = prior_ref[:, width:]
        else:
            acc_ref[...] = jnp.zeros_like(acc_ref)
            rope_acc_ref[...] = jnp.zeros_like(rope_acc_ref)

    bias = bias_ref[...]
    key_grads = []
    value_grads = []
    rope_total = rope_acc_ref[...]
    for head in range(heads):
        cols = slice(head * DN, (head + 1) * DN)
        wide = slice(head * DQ, (head + 1) * DQ)
        keys = jnp.concatenate([dot(latent, wuk_ref[:, cols]).astype(jnp.bfloat16), rope], axis=1)
        values = dot(latent, wuv_ref[:, cols]).astype(jnp.bfloat16)
        query = query_ref[:, wide]
        grad = grad_ref[:, cols]
        product = grad.astype(jnp.float32) * out_ref[:, cols].astype(jnp.float32)
        delta = jnp.sum(product.T, axis=0, keepdims=True)
        lse = lse_ref[pl.ds((chunk_start + step) * heads + head, 1), :]
        weights = jnp.exp(dot_nt(keys, query) * scale - lse + bias)
        score_grad = (weights * (dot_nt(values, grad) - delta) * scale).astype(jnp.bfloat16)
        dq_ref[:, wide] = dot(score_grad.T, keys).astype(jnp.bfloat16)
        key_grad = dot(score_grad, query)
        value_grads.append(dot(weights.astype(jnp.bfloat16), grad).astype(jnp.bfloat16))
        key_grads.append(key_grad[:, :DN].astype(jnp.bfloat16))
        rope_total = rope_total + key_grad[:, DN:]
    rope_acc_ref[...] = rope_total
    key_flat = jnp.concatenate(key_grads, axis=1)
    value_flat = jnp.concatenate(value_grads, axis=1)
    half = flat_ref.shape[0] // 2
    flat = flat_ref[...]
    weight_uk = dot(flat, key_flat).astype(jnp.bfloat16)
    weight_uv = dot(flat, value_flat).astype(jnp.bfloat16)
    send_ref[0] = weight_uk[:half]
    send_ref[1] = weight_uv[:half]
    keep_ref[0] = weight_uk[half:]
    keep_ref[1] = weight_uv[half:]
    acc_ref[...] += dot_nt(key_flat, wuk_ref[...]) + dot_nt(value_flat, wuv_ref[...])

    @pl.when(step == steps - 1)
    def _():
        width = latent_ref.shape[1]
        total_ref[:, :width] = acc_ref[...].astype(total_ref.dtype)
        total_ref[:, width:] = rope_acc_ref[...].astype(total_ref.dtype)


def chunk_grads(place, positions, order, latent, rope, query, grad_out, attn_out, lse, w_uk, w_uv,
                prior, *, chunk, chunks, heads):
    tokens, width = latent.shape
    rows = query.shape[0]
    head_count = lse.shape[0]
    steps = head_count // heads // chunks
    start = chunk * steps
    final = chunk + 1 == chunks
    whole = lambda shape: pl.BlockSpec(shape, lambda j, p: (0,) * len(shape))
    columns = lambda height, size: pl.BlockSpec((height, size), lambda j, p: (0, start + j))
    in_specs = [
        whole(positions.shape),
        pl.BlockSpec((1, 1, width), lambda j, p: (p[0], 0, 0)),
        whole(latent.shape),
        whole(rope.shape),
        columns(rows, heads * DQ),
        columns(rows, heads * DV),
        columns(rows, heads * DV),
        whole(lse.shape),
        columns(width, heads * DN),
        columns(width, heads * DV),
    ]
    operands = [positions, order, latent, rope, query, grad_out, attn_out, lse, w_uk, w_uv]
    aliases = {}
    if prior is not None:
        in_specs += [whole(prior[1].shape), pl.BlockSpec(memory_space=pl.ANY)]
        operands += [prior[1], prior[0]]
        aliases = {len(operands): 0}
    half = jax.ShapeDtypeStruct((2, width // 2, steps * heads * DN), jnp.bfloat16)
    half_spec = pl.BlockSpec((2, width // 2, heads * DN), lambda j, p: (0, 0, j))
    total = jax.ShapeDtypeStruct((tokens, width + DR), jnp.bfloat16 if final else jnp.float32)
    return pl.pallas_call(
        functools.partial(grads_body, heads=heads, chunk_start=start,
                          has_prior=prior is not None, final=final),
        grid_spec=pltpu.PrefetchScalarGridSpec(
            num_scalar_prefetch=1,
            grid=(steps,),
            in_specs=in_specs,
            out_specs=[columns(rows, heads * DQ), half_spec, half_spec, whole(total.shape)],
            scratch_shapes=[
                pltpu.VMEM((width, tokens), jnp.bfloat16),
                pltpu.VMEM((tokens, rows), jnp.float32),
                pltpu.VMEM((tokens, width), jnp.float32),
                pltpu.VMEM((tokens, DR), jnp.float32),
            ],
        ),
        out_shape=[jax.ShapeDtypeStruct(query.shape, jnp.bfloat16), half, half, total],
        input_output_aliases=aliases,
        name="grads",
    )(place, *operands)


def shifted(value, axis, steps):
    count = lax.axis_size(axis)
    return lax.ppermute(value, axis, [(s, (s + steps) % count) for s in range(count)])


def on_device(latent, rope, query, grad_out, attn_out, lse, positions, w_uk, w_uv):
    dp_size, ctx_size, head_size = (lax.axis_size(a) for a in ("dp", "ctx", "head"))
    rows, width = latent.shape[1:]
    my_ctx = lax.axis_index("ctx")
    my_place = lax.axis_index("dp") * ctx_size + my_ctx
    place = jnp.stack([my_place, my_ctx]).astype(jnp.int32)
    order = jnp.asarray(row_table(dp_size, ctx_size, width))[:, None, :]
    own = jnp.concatenate([latent[0], rope[0]], axis=1)
    features = jnp.concatenate([own] + [shifted(own, "ctx", -s) for s in range(1, ctx_size)], axis=0)
    head_count = lse.shape[1]
    heads = math.gcd(head_count, 4)
    chunks = math.gcd(head_count // heads, 2)
    prior = None
    sends = []
    keeps = []
    for chunk in range(chunks):
        grad_query, send, keep, total = chunk_grads(
            place, positions.reshape(ctx_size, 1, rows), order, features[:, :width],
            features[:, width:], query[0], grad_out[0], attn_out[0], lse[0], w_uk, w_uv, prior,
            chunk=chunk, chunks=chunks, heads=heads,
        )
        prior = (grad_query, total)
        sends.append(send)
        keeps.append(keep)
    parts = total.reshape(ctx_size, rows, width + DR)
    summed = parts[0].astype(jnp.float32)
    for s in range(1, ctx_size):
        summed = summed + shifted(parts[s], "ctx", s).astype(jnp.float32)
    for bit in bits_of(head_size):
        mine = summed.astype(jnp.bfloat16)
        other = lax.ppermute(mine, "head", [(s, s ^ bit) for s in range(head_size)])
        summed = mine.astype(jnp.float32) + other.astype(jnp.float32)
    stages = (dp_size * ctx_size).bit_length() - 1
    finals = []
    for send, keep in zip(sends, keeps):
        for stage in range(stages):
            got = lax.ppermute(send, ("dp", "ctx"), stage_pairs(stage, dp_size, ctx_size))
            left = keep.astype(jnp.float32) + got.astype(jnp.float32)
            left = left.astype(jnp.bfloat16)
            half = left.shape[1] // 2
            send, keep = left[:, :half], left[:, half:]
        finals.append(left)
    weight_uk = jnp.concatenate([part[0] for part in finals], axis=1)
    weight_uv = jnp.concatenate([part[1] for part in finals], axis=1)
    return (
        grad_query[None],
        summed[None, :, :width],
        summed[None, :, width:],
        weight_uk,
        weight_uv,
    )


def solution(mesh):
    return jax.shard_map(
        on_device,
        mesh=mesh,
        in_specs=(
            P("dp", "ctx", None),
            P("dp", "ctx", None),
            P("dp", "ctx", "head"),
            P("dp", "ctx", "head"),
            P("dp", "ctx", "head"),
            P("dp", "head", "ctx"),
            P("dp", None),
            P(None, "head"),
            P(None, "head"),
        ),
        out_specs=(
            P("dp", "ctx", "head"),
            P("dp", "ctx", None),
            P("dp", "ctx", None),
            P(("dp", "ctx"), "head"),
            P(("dp", "ctx"), "head"),
        ),
        check_vma=False,
    )
```

time: 202 us -> 83.1 us (0.41)
  waiting for transfers between devices: 87.6 us -> 33.8 us
  matrix products: 30.7 us -> 0 us
  local copies, waits for them, and re-layouts: 26 us -> 5.75 us
  Pallas kernels: 0 us -> 19.8 us
  blocking collectives: 19.4 us -> 0 us
  between operations: 18.4 us -> 0.8 us
  starting transfers between devices: 7.23 us -> 16.4 us
  other arithmetic: 11.9 us -> 6.28 us
    unnamed x5 -> x0, waiting for transfers between devices: 30.9 us -> none
    dot_general x14 -> x0, matrix products: 28 us -> none  [the longest x2 4.15 us: head_grads(): jnp.einsum('grs,grd->gsd', score_grad, queries, preferred_element_type=jn...]
    ppermute x6 -> x10, waiting for transfers between devices: 56.7 us -> 33.8 us  [the longest x6 17.9 us: on_device(): lax.ppermute(send, ('dp', 'ctx'), stage_pairs(stage, dp_size, ctx_size))]
    unnamed x44 -> x8, local copies, waits for them, and re-layouts: 24.5 us -> 1.53 us
    pallas_call x0 -> x2, Pallas kernels: none -> 19.8 us  [chunk_grads(): pl.pallas_call(functools.partial(grads_body, heads=heads, chunk_start=sta...]
    psum x1 -> x0, blocking collectives: 19.4 us -> none  [on_device(): lax.psum(rope_part.astype(jnp.bfloat16), 'head').astype(jnp.float32)]
    ppermute x6 -> x10, starting transfers between devices: 6.92 us -> 16.4 us  [the longest x6 6.12 us: on_device(): lax.ppermute(send, ('dp', 'ctx'), stage_pairs(stage, dp_size, ctx_size))]
    add x3 -> x1, other arithmetic: 4.72 us -> 0.03 us  [on_device(): summed = mine.astype(jnp.float32) + other.astype(jnp.float32)]
  transfers between devices with their start and end apart: 9 -> 10, of which waited for: 3 -> 7; matrix products, arithmetic and copies ran while one was open for 23% -> 7% of each run, Pallas kernels for 0% -> 0%
where the time goes in v1:
time: 83.1 us; the launch traced here: 82.8 us
  waiting for transfers between devices  33.8 us (41%)
  Pallas kernels  19.8 us (24%)
  starting transfers between devices  16.4 us (20%)
  other arithmetic  6.28 us (8%)
  local copies, waits for them, and re-layouts  5.75 us (7%)
    pallas_call x2, Pallas kernels, chunk_grads(): pl.pallas_call(functools.partial(grads_body, heads=heads, chunk_start=sta...  19.8 us
    ppermute x6, waiting for transfers between devices, on_device(): lax.ppermute(send, ('dp', 'ctx'), stage_pairs(stage, dp_size, ctx_size))  17.9 us
    ppermute x2, waiting for transfers between devices, on_device(): other = lax.ppermute(mine, 'head', [(s, s ^ bit) for s in range(head_size)])  8.61 us
    ppermute x2, waiting for transfers between devices, shifted(): lax.ppermute(value, axis, [(s, (s + steps) % count) for s in range(count)])  7.23 us
    ppermute x6, starting transfers between devices, on_device(): lax.ppermute(send, ('dp', 'ctx'), stage_pairs(stage, dp_size, ctx_size))  6.12 us
    ppermute x2, starting transfers between devices, on_device(): other = lax.ppermute(mine, 'head', [(s, s ^ bit) for s in range(head_size)])  5.38 us
    ppermute x2, starting transfers between devices, shifted(): lax.ppermute(value, axis, [(s, (s + steps) % count) for s in range(count)])  4.86 us
    slice x4, local copies, waits for them, and re-layouts, on_device(): send, keep = (left[:, :half], left[:, half:])  1.7 us
  transfers between devices with their start and end apart: 10, of which 7 were waited for; matrix products, arithmetic and copies ran while one was open for 7% of the time, Pallas kernels for 0%

profile of v1, /device:TPU:0, one launch (start us, length us, event | category | flops | bytes accessed | tf_op | source)
XLA Modules:
  0.0 82.8 jit_solution(10381697189773225971)
XLA Ops:
  0.6 0.8 copy.16
  1.5 0.9 %pad_maximum_fusion.3 = bf16[128,576]{1,0:T(8,128)(2,1)S(1)} fusion(bf16[128,64]{1,0:T(8,128)(2,1)S(1)} %bitcast.32, bf16[128,512]{1,0:T(8,128)(2,1)} %bitcast.28), kind=kLoop, calls=%fused_computation.13 | loop fusion | flops 294912 | bytes 294912 | tf_op jit(solution)/shard_map/concatenate | solution.py:213
  2.4 3.1 %collective-permute-start = (bf16[128,576]{1,0:T(8,128)(2,1)S(1)}, bf16[128,576]{1,0:T(8,128)(2,1)S(1)}, u32[]{:S(2)}, u32[]{:S(2)}) collective-permute-start(bf16[128,576]{1,0:T(8,128)(2,1)S(1)} %pad_maximum_fusion.3), channel_id=1, source_target_pairs={{0,4},{4,0},{1,5},{5,1},{2,6},{6,2},{3,7},{7,3},{8,12},{12,8},{9,1... | collective-permute-start | bytes 442376 | tf_op jit(solution)/shard_map/ppermute | solution.py:203
  5.5 0.6 pad_add_fusion.place_ref
  6.0 3.6 %collective-permute-done = bf16[128,576]{1,0:T(8,128)(2,1)S(1)} collective-permute-done((bf16[128,576]{1,0:T(8,128)(2,1)S(1)}, bf16[128,576]{1,0:T(8,128)(2,1)S(1)}, u32[]{:S(2)}, u32[]{:S(2)}) %collective-permute-start) | collective-permute-done | bytes 147488 | tf_op jit(solution)/shard_map/ppermute | solution.py:203
  9.7 0.9 %pad_maximum_fusion = bf16[256,576]{1,0:T(8,128)(2,1)S(1)} fusion(bf16[128,576]{1,0:T(8,128)(2,1)S(1)} %collective-permute-done, bf16[128,64]{1,0:T(8,128)(2,1)S(1)} %bitcast.33, bf16[128,512]{1,0:T(8,128)(2,1)} %bitcast.29), kind=kLoop, calls=%fused_computation.6 | loop fusion | flops 884736 | bytes 589824 | tf_op jit(solution)/shard_map/concatenate | solution.py:214
  10.6 0.7 slice.76.latent_ref
  11.3 0.6 pad_maximum_fusion.4.rope_ref
  12.0 9.8 %grads.2 = (bf16[128,3072]{1,0:T(8,128)(2,1)}, bf16[2,256,1024]{2,1,0:T(8,128)(2,1)}, bf16[2,256,1024]{2,1,0:T(8,128)(2,1)}, f32[256,576]{1,0:T(8,128)}) custom-call(s32[2]{0:T(128)} %pad_add_fusion.place_ref, s32[2,1,128]{2,1,0:T(1,128)} %bitcast.37, s32[8,1,512]{2,1,0:T(1,128)} %constant.22.order_ref, bf16[256,512]{1,0:T(8,128)(2,1)} %slice.76.latent_ref, ...), custom_call_target="tpu_custom_call" | custom-call | tf_op jit(solution)/shard_map/grads/pallas_call | solution.py:180
  21.7 10.0 %grads.3 = (bf16[128,3072]{1,0:T(8,128)(2,1)}, bf16[2,256,1024]{2,1,0:T(8,128)(2,1)}, bf16[2,256,1024]{2,1,0:T(8,128)(2,1)}, bf16[256,576]{1,0:T(8,128)(2,1)}) custom-call(s32[2]{0:T(128)} %pad_add_fusion.place_ref, s32[2,1,128]{2,1,0:T(1,128)} %bitcast.38, s32[8,1,512]{2,1,0:T(1,128)} %constant.22.order_ref, ...), custom_call_target="tpu_custom_call", output_to_operand_aliasing={{0}: (12, {})} | custom-call | tf_op jit(solution)/shard_map/grads/pallas_call | solution.py:180
  31.8 1.0 %slice.61 = bf16[128,576]{1,0:T(8,128)(2,1)S(1)} slice(bf16[256,576]{1,0:T(8,128)(2,1)} %get-tuple-element.16), slice={[128:256], [0:576]} | slice | bytes 294912 | tf_op jit(solution)/shard_map/slice | solution.py:233
  32.8 1.8 %collective-permute-start.1 = (bf16[128,576]{1,0:T(8,128)(2,1)S(1)}, bf16[128,576]{1,0:T(8,128)(2,1)S(1)}, u32[]{:S(2)}, u32[]{:S(2)}) collective-permute-start(bf16[128,576]{1,0:T(8,128)(2,1)S(1)} %slice.61), channel_id=1, source_target_pairs={{0,4},{4,0},{1,5},{5,1},{2,6},{6,2},{3,7},{7,3},{8,12},{12,8},{9,1... | collective-permute-start | bytes 442376 | tf_op jit(solution)/shard_map/ppermute | solution.py:203
  34.6 3.6 %collective-permute-done.1 = bf16[128,576]{1,0:T(8,128)(2,1)S(1)} collective-permute-done((bf16[128,576]{1,0:T(8,128)(2,1)S(1)}, bf16[128,576]{1,0:T(8,128)(2,1)S(1)}, u32[]{:S(2)}, u32[]{:S(2)}) %collective-permute-start.1) | collective-permute-done | bytes 147488 | tf_op jit(solution)/shard_map/ppermute | solution.py:203
  38.2 1.0 %add_convert_fusion.7 = bf16[128,576]{1,0:T(8,128)(2,1)S(1)} fusion(bf16[128,576]{1,0:T(8,128)(2,1)S(1)} %collective-permute-done.1, bf16[256,576]{1,0:T(8,128)(2,1)} %get-tuple-element.16), kind=kLoop, calls=%fused_computation.9 | loop fusion | flops 294912 | bytes 442368 | tf_op jit(solution)/shard_map/convert_element_type | solution.py:235
  39.2 1.8 %collective-permute-start.2 = (bf16[128,576]{1,0:T(8,128)(2,1)S(1)}, bf16[128,576]{1,0:T(8,128)(2,1)S(1)}, u32[]{:S(2)}, u32[]{:S(2)}) collective-permute-start(bf16[128,576]{1,0:T(8,128)(2,1)S(1)} %add_convert_fusion.7), channel_id=1, source_target_pairs={{0,1},{1,0},{2,3},{3,2},{4,5},{5,4},{6,7},{7,6},{8,9},{9,8},{10,11... | collective-permute-start | bytes 442376 | tf_op jit(solution)/shard_map/ppermute | solution.py:236
  41.0 3.6 %collective-permute-done.2 = bf16[128,576]{1,0:T(8,128)(2,1)S(1)} collective-permute-done((bf16[128,576]{1,0:T(8,128)(2,1)S(1)}, bf16[128,576]{1,0:T(8,128)(2,1)S(1)}, u32[]{:S(2)}, u32[]{:S(2)}) %collective-permute-start.2) | collective-permute-done | bytes 147488 | tf_op jit(solution)/shard_map/ppermute | solution.py:236
  44.6 3.6 %collective-permute-start.3 = (bf16[128,576]{1,0:T(8,128)(2,1)S(1)}, bf16[128,576]{1,0:T(8,128)(2,1)S(1)}, u32[]{:S(2)}, u32[]{:S(2)}) collective-permute-start(bf16[128,576]{1,0:T(8,128)(2,1)S(1)} %add_convert_fusion.6), channel_id=1, source_target_pairs={{0,2},{1,3},{2,0},{3,1},{4,6},{5,7},{6,4},{7,5},{8,10},{9,11},{10,... | collective-permute-start | bytes 442376 | tf_op jit(solution)/shard_map/ppermute | solution.py:236
  48.2 5.1 %collective-permute-done.3 = bf16[128,576]{1,0:T(8,128)(2,1)S(1)} collective-permute-done((bf16[128,576]{1,0:T(8,128)(2,1)S(1)}, bf16[128,576]{1,0:T(8,128)(2,1)S(1)}, u32[]{:S(2)}, u32[]{:S(2)}) %collective-permute-start.3) | collective-permute-done | bytes 147488 | tf_op jit(solution)/shard_map/ppermute | solution.py:236
  53.3 0.4 add_convert_fusion.1
  53.7 0.8 slice.80
  54.5 1.5 %collective-permute-start.5 = (bf16[2,128,1024]{2,1,0:T(8,128)(2,1)}, bf16[2,128,1024]{2,1,0:T(8,128)(2,1)S(1)}, u32[]{:S(2)}, u32[]{:S(2)}) collective-permute-start(bf16[2,128,1024]{2,1,0:T(8,128)(2,1)} %slice.80), channel_id=1, source_target_pairs={{0,16},{4,20},{8,12},{12,8},{16,0},{20,4},{24,28},{28,24},{1,17},{... | collective-permute-start | bytes 1572872 | tf_op jit(solution)/shard_map/ppermute | solution.py:242
  56.0 0.4 add_convert_fusion
  56.5 0.8 %slice.85 = bf16[2,128,1024]{2,1,0:T(8,128)(2,1)} slice(bf16[2,256,1024]{2,1,0:T(8,128)(2,1)S(1)} %add_convert_fusion), slice={[0:2], [0:128], [0:1024]} | slice | bytes 1048576 | tf_op jit(solution)/shard_map/slice | solution.py:246
  57.3 0.5 collective-permute-start.8
  57.8 0.7 copy.17
  58.5 0.7 slice_bitcast_fusion
  59.3 7.4 %collective-permute-done.5 = bf16[2,128,1024]{2,1,0:T(8,128)(2,1)S(1)} collective-permute-done((bf16[2,128,1024]{2,1,0:T(8,128)(2,1)}, bf16[2,128,1024]{2,1,0:T(8,128)(2,1)S(1)}, u32[]{:S(2)}, u32[]{:S(2)}) %collective-permute-start.5) | collective-permute-done | bytes 524320 | tf_op jit(solution)/shard_map/ppermute | solution.py:242
  66.9 2.5 %collective-permute-start.6 = (bf16[2,64,1024]{2,1,0:T(8,128)(2,1)S(1)}, bf16[2,64,1024]{2,1,0:T(8,128)(2,1)S(1)}, u32[]{:S(2)}, u32[]{:S(2)}) collective-permute-start(bf16[2,64,1024]{2,1,0:T(8,128)(2,1)S(1)} %slice.82), channel_id=1, source_target_pairs={{0,4},{4,0},{8,24},{12,28},{16,20},{20,16},{24,8},{28,12},{1,5},{5... | collective-permute-start | bytes 786440 | tf_op jit(solution)/shard_map/ppermute | solution.py:242
  69.4 5.7 %collective-permute-done.8 = bf16[2,128,1024]{2,1,0:T(8,128)(2,1)S(1)} collective-permute-done((bf16[2,128,1024]{2,1,0:T(8,128)(2,1)}, bf16[2,128,1024]{2,1,0:T(8,128)(2,1)S(1)}, u32[]{:S(2)}, u32[]{:S(2)}) %collective-permute-start.8) | collective-permute-done | bytes 524320 | tf_op jit(solution)/shard_map/ppermute | solution.py:242
  75.4 1.6 %collective-permute-start.9 = (bf16[2,64,1024]{2,1,0:T(8,128)(2,1)S(1)}, bf16[2,64,1024]{2,1,0:T(8,128)(2,1)S(1)}, u32[]{:S(2)}, u32[]{:S(2)}) collective-permute-start(bf16[2,64,1024]{2,1,0:T(8,128)(2,1)S(1)} %slice.87), channel_id=1, source_target_pairs={{0,4},{4,0},{8,24},{12,28},{16,20},{20,16},{24,8},{28,12},{1,5},{5... | collective-permute-start | bytes 786440 | tf_op jit(solution)/shard_map/ppermute | solution.py:242
  77.1 4.7 %collective-permute-done.9 = bf16[2,64,1024]{2,1,0:T(8,128)(2,1)S(1)} collective-permute-done((bf16[2,64,1024]{2,1,0:T(8,128)(2,1)S(1)}, bf16[2,64,1024]{2,1,0:T(8,128)(2,1)S(1)}, u32[]{:S(2)}, u32[]{:S(2)}) %collective-permute-start.9) | collective-permute-done | bytes 262176 | tf_op jit(solution)/shard_map/ppermute | solution.py:242
  81.9 0.8 pad_maximum_fusion.1
  (22 shorter events, 0.7 us)
Async XLA Ops:
  2.4 7.3 %collective-permute-start = (bf16[128,576]{1,0:T(8,128)(2,1)S(1)}, bf16[128,576]{1,0:T(8,128)(2,1)S(1)}, u32[]{:S(2)}, u32[]{:S(2)}) collective-permute-start(bf16[128,576]{1,0:T(8,128)(2,1)S(1)} %pad_maximum_fusion.3), channel_id=1, source_target_pairs={{0,4},{4,0},{1,5},{5,1},{2,6},{6,2},{3,7},{7,3},{8,12},{12,8},{9,1... | collective-permute-start | bytes 442376 | tf_op jit(solution)/shard_map/ppermute | solution.py:203
  21.7 12.9 %copy-start.2 = (bf16[2,256,1024]{2,1,0:T(8,128)(2,1)S(1)}, bf16[2,256,1024]{2,1,0:T(8,128)(2,1)}, u32[]{:S(2)}) copy-start(bf16[2,256,1024]{2,1,0:T(8,128)(2,1)} %get-tuple-element.18) | copy-start | bytes 3145732
  31.8 21.5 %copy-start.1 = (bf16[2,256,1024]{2,1,0:T(8,128)(2,1)S(1)}, bf16[2,256,1024]{2,1,0:T(8,128)(2,1)}, u32[]{:S(2)}) copy-start(bf16[2,256,1024]{2,1,0:T(8,128)(2,1)} %get-tuple-element.17) | copy-start | bytes 3145732
  32.8 5.4 %collective-permute-start.1 = (bf16[128,576]{1,0:T(8,128)(2,1)S(1)}, bf16[128,576]{1,0:T(8,128)(2,1)S(1)}, u32[]{:S(2)}, u32[]{:S(2)}) collective-permute-start(bf16[128,576]{1,0:T(8,128)(2,1)S(1)} %slice.61), channel_id=1, source_target_pairs={{0,4},{4,0},{1,5},{5,1},{2,6},{6,2},{3,7},{7,3},{8,12},{12,8},{9,1... | collective-permute-start | bytes 442376 | tf_op jit(solution)/shard_map/ppermute | solution.py:203
  34.6 18.7 %collective-permute-start.4 = (bf16[2,256,1024]{2,1,0:T(8,128)(2,1)S(1)}, bf16[2,256,1024]{2,1,0:T(8,128)(2,1)S(1)}, u32[]{:S(2)}, u32[]{:S(2)}) collective-permute-start(bf16[2,256,1024]{2,1,0:T(8,128)(2,1)S(1)} %copy-done.2), channel_id=1, source_target_pairs={{0,8},{4,12},{8,0},{12,4},{16,24},{20,28},{24,16},{28,20},{1,9},{5... | collective-permute-start | bytes 3145736 | tf_op jit(solution)/shard_map/ppermute | solution.py:242
  39.2 5.4 %collective-permute-start.2 = (bf16[128,576]{1,0:T(8,128)(2,1)S(1)}, bf16[128,576]{1,0:T(8,128)(2,1)S(1)}, u32[]{:S(2)}, u32[]{:S(2)}) collective-permute-start(bf16[128,576]{1,0:T(8,128)(2,1)S(1)} %add_convert_fusion.7), channel_id=1, source_target_pairs={{0,1},{1,0},{2,3},{3,2},{4,5},{5,4},{6,7},{7,6},{8,9},{9,8},{10,11... | collective-permute-start | bytes 442376 | tf_op jit(solution)/shard_map/ppermute | solution.py:236
  41.0 15.0 %collective-permute-start.7 = (bf16[2,256,1024]{2,1,0:T(8,128)(2,1)}, bf16[2,256,1024]{2,1,0:T(8,128)(2,1)S(1)}, u32[]{:S(2)}, u32[]{:S(2)}) collective-permute-start(bf16[2,256,1024]{2,1,0:T(8,128)(2,1)} %get-tuple-element.20), channel_id=1, source_target_pairs={{0,8},{4,12},{8,0},{12,4},{16,24},{20,28},{24,16},{28,20},{1,9},{5... | collective-permute-start | bytes 3145736 | tf_op jit(solution)/shard_map/ppermute | solution.py:242
  44.6 8.6 %collective-permute-start.3 = (bf16[128,576]{1,0:T(8,128)(2,1)S(1)}, bf16[128,576]{1,0:T(8,128)(2,1)S(1)}, u32[]{:S(2)}, u32[]{:S(2)}) collective-permute-start(bf16[128,576]{1,0:T(8,128)(2,1)S(1)} %add_convert_fusion.6), channel_id=1, source_target_pairs={{0,2},{1,3},{2,0},{3,1},{4,6},{5,7},{6,4},{7,5},{8,10},{9,11},{10,... | collective-permute-start | bytes 442376 | tf_op jit(solution)/shard_map/ppermute | solution.py:236
  53.3 2.7 %copy-start = (bf16[2,256,1024]{2,1,0:T(8,128)(2,1)S(1)}, bf16[2,256,1024]{2,1,0:T(8,128)(2,1)}, u32[]{:S(2)}) copy-start(bf16[2,256,1024]{2,1,0:T(8,128)(2,1)} %get-tuple-element.19) | copy-start | bytes 3145732
  54.5 12.2 %collective-permute-start.5 = (bf16[2,128,1024]{2,1,0:T(8,128)(2,1)}, bf16[2,128,1024]{2,1,0:T(8,128)(2,1)S(1)}, u32[]{:S(2)}, u32[]{:S(2)}) collective-permute-start(bf16[2,128,1024]{2,1,0:T(8,128)(2,1)} %slice.80), channel_id=1, source_target_pairs={{0,16},{4,20},{8,12},{12,8},{16,0},{20,4},{24,28},{28,24},{1,17},{... | collective-permute-start | bytes 1572872 | tf_op jit(solution)/shard_map/ppermute | solution.py:242
  57.3 17.9 %collective-permute-start.8 = (bf16[2,128,1024]{2,1,0:T(8,128)(2,1)}, bf16[2,128,1024]{2,1,0:T(8,128)(2,1)S(1)}, u32[]{:S(2)}, u32[]{:S(2)}) collective-permute-start(bf16[2,128,1024]{2,1,0:T(8,128)(2,1)} %slice.85), channel_id=1, source_target_pairs={{0,16},{4,20},{8,12},{12,8},{16,0},{20,4},{24,28},{28,24},{1,17},{... | collective-permute-start | bytes 1572872 | tf_op jit(solution)/shard_map/ppermute | solution.py:242
  66.9 10.1 %collective-permute-start.6 = (bf16[2,64,1024]{2,1,0:T(8,128)(2,1)S(1)}, bf16[2,64,1024]{2,1,0:T(8,128)(2,1)S(1)}, u32[]{:S(2)}, u32[]{:S(2)}) collective-permute-start(bf16[2,64,1024]{2,1,0:T(8,128)(2,1)S(1)} %slice.82), channel_id=1, source_target_pairs={{0,4},{4,0},{8,24},{12,28},{16,20},{20,16},{24,8},{28,12},{1,5},{5... | collective-permute-start | bytes 786440 | tf_op jit(solution)/shard_map/ppermute | solution.py:242
  75.4 6.4 %collective-permute-start.9 = (bf16[2,64,1024]{2,1,0:T(8,128)(2,1)S(1)}, bf16[2,64,1024]{2,1,0:T(8,128)(2,1)S(1)}, u32[]{:S(2)}, u32[]{:S(2)}) collective-permute-start(bf16[2,64,1024]{2,1,0:T(8,128)(2,1)S(1)} %slice.87), channel_id=1, source_target_pairs={{0,4},{4,0},{8,24},{12,28},{16,20},{20,16},{24,8},{28,12},{1,5},{5... | collective-permute-start | bytes 786440 | tf_op jit(solution)/shard_map/ppermute | solution.py:242

commit v2 on v1

v2 whole, which is shorter than its diff:
```python
import functools
import math

import jax
import jax.numpy as jnp
import numpy as np
from jax import lax
from jax.experimental import pallas as pl
from jax.experimental.pallas import tpu as pltpu
from jax.sharding import PartitionSpec as P

DR = 64
DN = 128
DV = 128
DQ = DN + DR

MASKED = -1e30
GROUP = 4
VMEM_LIMIT = 16 << 20
LOAD_LIMIT = 16 << 20
CHUNKS = 2
NT = (((1,), (1,)), ((), ()))


def bits_of(count):
    return [1 << b for b in range(count.bit_length() - 1)]


def stage_orders(dp_size, ctx_size):
    outer = [("dp", bit) for bit in bits_of(dp_size)[1:]]
    inner = [("ctx", bit) for bit in bits_of(ctx_size)]
    return outer + inner, inner + outer


def row_table(dp_size, ctx_size, rows):
    orders = stage_orders(dp_size, ctx_size)
    blocks = dp_size * ctx_size
    width = rows // blocks
    table = np.zeros((blocks, rows), np.int32)
    for dp in range(dp_size):
        for ctx in range(ctx_size):
            for place in range(blocks):
                digits = [(place >> b) & 1 for b in reversed(range(blocks.bit_length() - 1))]
                target = {"dp": dp, "ctx": ctx}
                if digits[0] == 0:
                    target["dp"] ^= 1
                for digit, (axis, bit) in zip(digits[1:], orders[target["dp"] & 1]):
                    if digit == 0:
                        target[axis] ^= bit
                block = target["dp"] * ctx_size + target["ctx"]
                table[dp * ctx_size + ctx, place * width:(place + 1) * width] = (
                    block * width + np.arange(width)
                )
    return table


def stage_pairs(stage, dp_size, ctx_size):
    pairs = []
    orders = stage_orders(dp_size, ctx_size)
    for dp in range(dp_size):
        for ctx in range(ctx_size):
            place = {"dp": dp, "ctx": ctx}
            axis, bit = ("dp", 1) if stage == 0 else orders[dp & 1][stage - 1]
            place[axis] ^= bit
            pairs.append((dp * ctx_size + ctx, place["dp"] * ctx_size + place["ctx"]))
    return pairs


def dot(a, b):
    return jnp.dot(a, b, preferred_element_type=jnp.float32)


def dot_nt(a, b):
    return lax.dot_general(a, b, NT, preferred_element_type=jnp.float32)


def load_body(place_ref, pos_ref, order_ref, latent_ref, rope_ref, query_ref, grad_ref, out_ref,
              lse_ref, wuk_ref, wuv_ref, latent_out, rope_out, query_out, grad_out, lse_out,
              delta_out, wuk_out, wuv_out, keys_out, values_out, flat_out, bias_out,
              pos, order, attn, sems, *, ctx_size):
    pairs = [(latent_ref, latent_out), (order_ref, order), (pos_ref, pos), (rope_ref, rope_out),
             (wuk_ref, wuk_out), (wuv_ref, wuv_out), (grad_ref, grad_out), (out_ref, attn),
             (lse_ref, lse_out), (query_ref, query_out)]
    copies = [pltpu.make_async_copy(a, b, sems.at[k]) for k, (a, b) in enumerate(pairs)]
    for copy in copies:
        copy.start()
    rows, width = latent_out.shape
    for copy in copies[:3]:
        copy.wait()
    mine = place_ref[1]
    own_pos = jnp.broadcast_to(pos[mine], (rows, rows))
    for chunk in range(ctx_size):
        key_pos = pos[lax.rem(mine + chunk, ctx_size)]
        key_col = jnp.broadcast_to(key_pos, (rows, rows)).T
        bias_out[chunk * rows:(chunk + 1) * rows, :] = jnp.where(key_col <= own_pos, 0.0, MASKED)
    latent = latent_out[...]
    flat_out[...] = rows_first(latent, order[place_ref[0]])
    copies[4].wait()
    keys_out[...] = dot(latent, wuk_out[...]).astype(jnp.bfloat16)
    copies[5].wait()
    values_out[...] = dot(latent, wuv_out[...]).astype(jnp.bfloat16)
    copies[6].wait()
    copies[7].wait()
    for head in range(delta_out.shape[0]):
        cols = slice(head * DV, (head + 1) * DV)
        product = grad_out[:, cols].astype(jnp.float32) * attn[:, cols].astype(jnp.float32)
        delta_out[head:head + 1, :] = jnp.sum(product.T, axis=0, keepdims=True)
    for k in (3, 8, 9):
        copies[k].wait()


def rows_first(latent, order):
    width = latent.shape[1]
    spot = lax.broadcasted_iota(jnp.int32, (width, width), 0)
    pick = jnp.where(spot == order, 1.0, 0.0).astype(jnp.bfloat16)
    return dot(latent, pick).astype(jnp.bfloat16).T


def grads_body(place_ref, order_ref, *rest, ctx_size, start, count, group, has_prior, final, pieces):
    far_latents = rest[:ctx_size - 1]
    far_ropes = rest[ctx_size - 1:2 * ctx_size - 2]
    (latent_ref, rope_ref, query_ref, grad_ref, lse_ref, delta_ref, wuk_ref, wuv_ref, keys_ref,
     values_ref, flat_ref, bias_ref, *rest) = rest[2 * ctx_size - 2:]
    if has_prior:
        prior_ref, *rest = rest
    dq_ref, *rest = rest
    piece_refs, total_refs = rest[:pieces], rest[pieces:]
    rows, width = latent_ref.shape
    scale = 1.0 / math.sqrt(DQ)
    rope = jnp.concatenate([ref[...] for ref in (rope_ref, *far_ropes)], axis=1).T
    far = jnp.concatenate([ref[...] for ref in far_latents], axis=0)
    bias = bias_ref[...]
    flat = jnp.concatenate([flat_ref[...], rows_first(far, order_ref[place_ref[0]])], axis=1)
    rope_total = prior_ref[:, width:] if has_prior else 0.0
    latent_total = prior_ref[:, :width] if has_prior else 0.0
    for first in range(0, count, group):
        span = slice((start + first) * DN, (start + first + group) * DN)
        out_span = slice(first * DN, (first + group) * DN)
        wuk = wuk_ref[:, span]
        wuv = wuv_ref[:, span]
        keys_all = jnp.concatenate([keys_ref[:, span], dot(far, wuk).astype(jnp.bfloat16)], axis=0)
        values_all = jnp.concatenate(
            [values_ref[:, span], dot(far, wuv).astype(jnp.bfloat16)], axis=0
        )
        key_grads = []
        value_grads = []
        for inner in range(group):
            head = start + first + inner
            cols = slice(head * DN, (head + 1) * DN)
            wide = slice(head * DQ, (head + 1) * DQ)
            out_wide = slice((first + inner) * DQ, (first + inner + 1) * DQ)
            part = slice(inner * DN, (inner + 1) * DN)
            keys = jnp.concatenate([keys_all[:, part], rope], axis=1)
            query = query_ref[:, wide]
            grad = grad_ref[:, cols]
            delta = delta_ref[head:head + 1, :]
            lse = lse_ref[head:head + 1, :]
            weights = jnp.exp(dot_nt(keys, query) * scale - lse + bias)
            dots = dot_nt(values_all[:, part], grad)
            score_grad = (weights * (dots - delta) * scale).astype(jnp.bfloat16)
            dq_ref[:, out_wide] = dot(score_grad.T, keys).astype(jnp.bfloat16)
            key_grad = dot(score_grad, query)
            value_grads.append(dot(weights.astype(jnp.bfloat16), grad).astype(jnp.bfloat16))
            key_grads.append(key_grad[:, :DN].astype(jnp.bfloat16))
            rope_total = rope_total + key_grad[:, DN:]
        key_flat = jnp.concatenate(key_grads, axis=1)
        value_flat = jnp.concatenate(value_grads, axis=1)
        row = 0
        for piece_ref in piece_refs:
            size = piece_ref.shape[1]
            piece_ref[0, :, out_span] = dot(flat[row:row + size], key_flat).astype(jnp.bfloat16)
            piece_ref[1, :, out_span] = dot(flat[row:row + size], value_flat).astype(jnp.bfloat16)
            row += size
        latent_total = latent_total + dot_nt(key_flat, wuk) + dot_nt(value_flat, wuv)
    for chunk, total_ref in enumerate(total_refs):
        part = slice(chunk * rows, chunk * rows + total_ref.shape[0])
        total_ref[:, :width] = latent_total[part].astype(total_ref.dtype)
        total_ref[:, width:] = rope_total[part].astype(total_ref.dtype)


def in_vmem(array):
    return pltpu.with_memory_space_constraint(array, pltpu.VMEM)


def load(place, positions, order, latent, rope, query, grad_out, attn_out, lse, w_uk, w_uv):
    ctx_size = positions.shape[0]
    rows, width = latent.shape
    flat_size = w_uk.shape[1]
    like = lambda a: pltpu.VMEM(a.shape, a.dtype)
    vmem = pl.BlockSpec(memory_space=pltpu.VMEM)
    operands = [positions, order, latent, rope, query, grad_out, attn_out, lse, w_uk, w_uv]
    operands = [pltpu.with_memory_space_constraint(a, pltpu.HBM) for a in operands]
    outs = [like(a) for a in (latent, rope, query, grad_out, lse, lse, w_uk, w_uv)]
    outs += [pltpu.VMEM((rows, flat_size), jnp.bfloat16)] * 2
    outs += [pltpu.VMEM((width, rows), jnp.bfloat16), pltpu.VMEM((ctx_size * rows, rows), jnp.float32)]
    return pl.pallas_call(
        functools.partial(load_body, ctx_size=ctx_size),
        in_specs=[pl.BlockSpec(memory_space=pltpu.SMEM)]
        + [pl.BlockSpec(memory_space=pltpu.HBM)] * len(operands),
        out_specs=[vmem] * len(outs),
        out_shape=outs,
        scratch_shapes=[like(positions), like(order), like(attn_out), pltpu.SemaphoreType.DMA((10,))],
        compiler_params=pltpu.CompilerParams(vmem_limit_bytes=LOAD_LIMIT),
        name="load",
    )(place, *operands)


def chunk_grads(place, order, latents, ropes, loaded, prior, *, start, count, final):
    ctx_size = len(latents) + 1
    rows, width = loaded[0].shape
    blocks = order.shape[0]
    smem = pl.BlockSpec(memory_space=pltpu.SMEM)
    vmem = pl.BlockSpec(memory_space=pltpu.VMEM)
    operands = [*latents, *ropes, *loaded] + ([] if prior is None else [prior])
    operands = [in_vmem(a) for a in operands]
    sizes = [width >> (s + 1) for s in range(blocks.bit_length() - 1)]
    sizes.append(sizes[-1])
    if final:
        totals = [pltpu.VMEM((rows, width + DR), jnp.bfloat16)] * ctx_size
    else:
        totals = [pltpu.VMEM((ctx_size * rows, width + DR), jnp.float32)]
    outs = pl.pallas_call(
        functools.partial(grads_body, ctx_size=ctx_size, start=start, count=count,
                          group=math.gcd(count, GROUP), has_prior=prior is not None, final=final,
                          pieces=len(sizes)),
        in_specs=[smem] + [vmem] * (1 + len(operands)),
        out_specs=[vmem] * (1 + len(sizes) + len(totals)),
        out_shape=[pltpu.VMEM((rows, count * DQ), jnp.bfloat16)]
        + [pltpu.VMEM((2, size, count * DN), jnp.bfloat16) for size in sizes] + totals,
        compiler_params=pltpu.CompilerParams(vmem_limit_bytes=VMEM_LIMIT),
        name="grads",
    )(place, order, *operands)
    return outs[0], outs[1:1 + len(sizes)], outs[1 + len(sizes):]


def shifted(value, axis, steps):
    count = lax.axis_size(axis)
    return lax.ppermute(value, axis, [(s, (s + steps) % count) for s in range(count)])


def on_device(latent, rope, query, grad_out, attn_out, lse, positions, w_uk, w_uv):
    dp_size, ctx_size, head_size = (lax.axis_size(a) for a in ("dp", "ctx", "head"))
    rows, width = latent.shape[1:]
    my_ctx = lax.axis_index("ctx")
    my_place = lax.axis_index("dp") * ctx_size + my_ctx
    place = jnp.stack([my_place, my_ctx]).astype(jnp.int32)
    order = jnp.asarray(row_table(dp_size, ctx_size, width))[:, None, :]
    rope_cols = rope[0].T
    latents = [shifted(latent[0], "ctx", -s) for s in range(1, ctx_size)]
    ropes = [shifted(rope_cols, "ctx", -s) for s in range(1, ctx_size)]
    loaded = load(place, positions.reshape(ctx_size, 1, rows), order, latent[0], rope_cols, query[0],
                  grad_out[0], attn_out[0], lse[0], w_uk, w_uv)
    head_count = lse.shape[1]
    chunks = math.gcd(head_count // math.gcd(head_count, GROUP), CHUNKS)
    count = head_count // chunks
    prior = None
    chunk_pieces = []
    query_grads = []
    for chunk in range(chunks):
        query_grad, pieces, totals = chunk_grads(
            place, order, latents, ropes, loaded, prior,
            start=chunk * count, count=count, final=chunk + 1 == chunks,
        )
        prior = totals[0]
        chunk_pieces.append(pieces)
        query_grads.append(query_grad)
    summed = totals[0].astype(jnp.float32)
    for s in range(1, ctx_size):
        summed = summed + shifted(totals[s], "ctx", s).astype(jnp.float32)
    for bit in bits_of(head_size):
        mine = summed.astype(jnp.bfloat16)
        other = lax.ppermute(mine, "head", [(s, s ^ bit) for s in range(head_size)])
        summed = mine.astype(jnp.float32) + other.astype(jnp.float32)
    finals = []
    for pieces in chunk_pieces:
        arrivals = []
        for stage, piece in enumerate(pieces):
            size = piece.shape[1]
            done = sum(p.shape[1] for p in pieces[:stage])
            value = piece.astype(jnp.float32)
            for past, arrival in enumerate(arrivals):
                first = done - sum(p.shape[1] for p in pieces[:past + 1])
                value = value + arrival[:, first:first + size].astype(jnp.float32)
            value = value.astype(jnp.bfloat16)
            if stage + 1 < len(pieces):
                pairs = stage_pairs(stage, dp_size, ctx_size)
                arrivals.append(lax.ppermute(value, ("dp", "ctx"), pairs))
        finals.append(value)
    weight_uk = jnp.concatenate([part[0] for part in finals], axis=1)
    weight_uv = jnp.concatenate([part[1] for part in finals], axis=1)
    return (
        jnp.concatenate(query_grads, axis=1)[None],
        summed[None, :, :width],
        summed[None, :, width:],
        weight_uk,
        weight_uv,
    )


def solution(mesh):
    return jax.shard_map(
        on_device,
        mesh=mesh,
        in_specs=(
            P("dp", "ctx", None),
            P("dp", "ctx", None),
            P("dp", "ctx", "head"),
            P("dp", "ctx", "head"),
            P("dp", "ctx", "head"),
            P("dp", "head", "ctx"),
            P("dp", None),
            P(None, "head"),
            P(None, "head"),
        ),
        out_specs=(
            P("dp", "ctx", "head"),
            P("dp", "ctx", None),
            P("dp", "ctx", None),
            P(("dp", "ctx"), "head"),
            P(("dp", "ctx"), "head"),
        ),
        check_vma=False,
    )
```

time: 83.1 us -> 62.7 us (0.75)
  waiting for transfers between devices: 33.8 us -> 23.8 us
  Pallas kernels: 19.8 us -> 13.7 us
  local copies, waits for them, and re-layouts: 5.75 us -> 1.48 us
    ppermute x6, waiting for transfers between devices: 17.9 us -> 11 us  [on_device(): arrivals.append(lax.ppermute(value, ('dp', 'ctx'), pairs))]
    pallas_call x2 -> x3, Pallas kernels: 19.8 us -> 13.7 us  [the longest x2 9.9 us: chunk_grads(): pl.pallas_call(functools.partial(grads_body, ctx_size=ctx_size, start=sta...]
    slice x6 -> x0, local copies, waits for them, and re-layouts: 3.44 us -> none  [the longest x4 1.7 us: on_device(): send, keep = (left[:, :half], left[:, half:])]
    convert_element_type x6, other arithmetic: 1.33 us -> 4.64 us  [on_device(): value = value.astype(jnp.bfloat16)]
    ppermute x2 -> x3, waiting for transfers between devices: 7.23 us -> 4.76 us  [shifted(): lax.ppermute(value, axis, [(s, (s + steps) % count) for s in range(count)])]
    concatenate x2 -> x0, other arithmetic: 1.86 us -> none  [the longest x1 0.93 us: on_device(): jnp.concatenate([own] + [shifted(own, 'ctx', -s) for s in range(1, ctx_si...]
    broadcast_in_dim x0 -> x1, other arithmetic: none -> 0.96 us  [on_device(): jnp.concatenate(query_grads, axis=1)[None]]
    convert_element_type x2, other arithmetic: 1 us -> 0.08 us  [on_device(): mine = summed.astype(jnp.bfloat16)]
  transfers between devices with their start and end apart: 10 -> 11, of which waited for: 7 -> 7; matrix products, arithmetic and copies ran while one was open for 7% -> 10% of each run, Pallas kernels for 0% -> 14%
where the time goes in v2:
time: 62.7 us; the launch traced here: 62.5 us
  waiting for transfers between devices  23.8 us (38%)
  starting transfers between devices  16.2 us (26%)
  Pallas kernels  13.7 us (22%)
  other arithmetic  6.62 us (11%)
  local copies, waits for them, and re-layouts  1.48 us (2%)
  between operations  0.74 us (1%)
    ppermute x6, waiting for transfers between devices, on_device(): arrivals.append(lax.ppermute(value, ('dp', 'ctx'), pairs))  11 us
    pallas_call x2, Pallas kernels, chunk_grads(): pl.pallas_call(functools.partial(grads_body, ctx_size=ctx_size, start=sta...  9.9 us
    ppermute x2, waiting for transfers between devices, on_device(): other = lax.ppermute(mine, 'head', [(s, s ^ bit) for s in range(head_size)])  8.05 us
    ppermute x6, starting transfers between devices, on_device(): arrivals.append(lax.ppermute(value, ('dp', 'ctx'), pairs))  6.55 us
    ppermute x3, starting transfers between devices, shifted(): lax.ppermute(value, axis, [(s, (s + steps) % count) for s in range(count)])  5.07 us
    ppermute x3, waiting for transfers between devices, shifted(): lax.ppermute(value, axis, [(s, (s + steps) % count) for s in range(count)])  4.76 us
    convert_element_type x6, other arithmetic, on_device(): value = value.astype(jnp.bfloat16)  4.64 us
    ppermute x2, starting transfers between devices, on_device(): other = lax.ppermute(mine, 'head', [(s, s ^ bit) for s in range(head_size)])  4.62 us
  transfers between devices with their start and end apart: 11, of which 7 were waited for; matrix products, arithmetic and copies ran while one was open for 10% of the time, Pallas kernels for 14%

profile of v2, /device:TPU:0, one launch (start us, length us, event | category | flops | bytes accessed | tf_op | source)
XLA Modules:
  0.0 62.5 jit_solution(291382973872217997)
XLA Ops:
  0.6 3.1 %collective-permute-start = (bf16[128,512]{1,0:T(8,128)(2,1)}, bf16[128,512]{1,0:T(8,128)(2,1)S(1)}, u32[]{:S(2)}, u32[]{:S(2)}) collective-permute-start(bf16[128,512]{1,0:T(8,128)(2,1)} %bitcast.28), channel_id=1, source_target_pairs={{0,4},{4,0},{1,5},{5,1},{2,6},{6,2},{3,7},{7,3},{8,12},{12,8},{9,1... | collective-permute-start | bytes 393224 | tf_op jit(solution)/shard_map/ppermute | solution.py:238
  3.7 0.1 collective-permute-start.1
  3.8 0.1 pad_add_fusion.place_ref
  3.8 3.8 %load.1 = (bf16[128,512]{1,0:T(8,128)(2,1)S(1)}, bf16[64,128]{1,0:T(8,128)(2,1)S(1)}, bf16[128,3072]{1,0:T(8,128)(2,1)S(1)}, bf16[128,2048]{1,0:T(8,128)(2,1)S(1...) custom-call(s32[2]{0:T(128)S(1)} %pad_add_fusion.place_ref, ...), custom_call_target="tpu_custom_call" | custom-call | tf_op jit(solution)/shard_map/load/pallas_call | solution.py:196
  7.6 0.1 collective-permute-done.1.rest_1_
  7.8 4.9 %grads.2 = (bf16[128,1536]{1,0:T(8,128)(2,1)S(1)}, bf16[2,256,1024]{2,1,0:T(8,128)(2,1)S(1)}, bf16[2,128,1024]{2,1,0:T(8,128)(2,1)S(1)}, bf16[2,64,1024]{2,1,0:T...) custom-call(s32[2]{0:T(128)S(1)} %pad_add_fusion.place_ref, s32[8,1,512]{2,1,0:T(1,128)S(1)} %copy-done, ...), custom_call_target="tpu_custom_call" | custom-call | tf_op jit(solution)/shard_map/grads/pallas_call | solution.py:222
  12.7 0.1 collective-permute-start.5
  12.8 5.0 %grads.3 = (bf16[128,1536]{1,0:T(8,128)(2,1)S(1)}, bf16[2,256,1024]{2,1,0:T(8,128)(2,1)S(1)}, bf16[2,128,1024]{2,1,0:T(8,128)(2,1)S(1)}, bf16[2,64,1024]{2,1,0:T...) custom-call(s32[2]{0:T(128)S(1)} %pad_add_fusion.place_ref, ...), custom_call_target="tpu_custom_call" | custom-call | tf_op jit(solution)/shard_map/grads/pallas_call | solution.py:222
  17.7 1.9 %collective-permute-start.2 = (bf16[128,576]{1,0:T(8,128)(2,1)S(1)}, bf16[128,576]{1,0:T(8,128)(2,1)S(1)}, u32[]{:S(2)}, u32[]{:S(2)}) collective-permute-start(bf16[128,576]{1,0:T(8,128)(2,1)S(1)} %get-tuple-element.46), channel_id=1, source_target_pairs={{0,4},{4,0},{1,5},{5,1},{2,6},{6,2},{3,7},{7,3},{8,12},{12,8},{9,1... | collective-permute-start | bytes 442376 | tf_op jit(solution)/shard_map/ppermute | solution.py:238
  19.7 0.2 collective-permute-start.8
  19.9 4.6 %collective-permute-done.2 = bf16[128,576]{1,0:T(8,128)(2,1)S(1)} collective-permute-done((bf16[128,576]{1,0:T(8,128)(2,1)S(1)}, bf16[128,576]{1,0:T(8,128)(2,1)S(1)}, u32[]{:S(2)}, u32[]{:S(2)}) %collective-permute-start.2) | collective-permute-done | bytes 147488 | tf_op jit(solution)/shard_map/ppermute | solution.py:238
  24.6 1.9 %collective-permute-start.3 = (bf16[128,576]{1,0:T(8,128)(2,1)S(1)}, bf16[128,576]{1,0:T(8,128)(2,1)S(1)}, u32[]{:S(2)}, u32[]{:S(2)}) collective-permute-start(bf16[128,576]{1,0:T(8,128)(2,1)S(1)} %add_convert_fusion.7), channel_id=1, source_target_pairs={{0,1},{1,0},{2,3},{3,2},{4,5},{5,4},{6,7},{7,6},{8,9},{9,8},{10,11... | collective-permute-start | bytes 442376 | tf_op jit(solution)/shard_map/ppermute | solution.py:272
  26.4 1.0 %maximum_bitcast_fusion = bf16[1,128,3072]{2,1,0:T(8,128)(2,1)} fusion(bf16[128,1536]{1,0:T(8,128)(2,1)S(1)} %get-tuple-element.44, bf16[128,1536]{1,0:T(8,128)(2,1)S(1)} %get-tuple-element.42), kind=kLoop, calls=%fused_computation.2 | loop fusion | flops 1572864 | bytes 1572864 | tf_op jit(solution)/shard_map/broadcast_in_dim | solution.py:292
  27.4 3.1 %collective-permute-done.3 = bf16[128,576]{1,0:T(8,128)(2,1)S(1)} collective-permute-done((bf16[128,576]{1,0:T(8,128)(2,1)S(1)}, bf16[128,576]{1,0:T(8,128)(2,1)S(1)}, u32[]{:S(2)}, u32[]{:S(2)}) %collective-permute-start.3) | collective-permute-done | bytes 147488 | tf_op jit(solution)/shard_map/ppermute | solution.py:272
  30.5 2.8 %collective-permute-start.4 = (bf16[128,576]{1,0:T(8,128)(2,1)S(1)}, bf16[128,576]{1,0:T(8,128)(2,1)S(1)}, u32[]{:S(2)}, u32[]{:S(2)}) collective-permute-start(bf16[128,576]{1,0:T(8,128)(2,1)S(1)} %add_convert_fusion.6), channel_id=1, source_target_pairs={{0,2},{1,3},{2,0},{3,1},{4,6},{5,7},{6,4},{7,5},{8,10},{9,11},{10,... | collective-permute-start | bytes 442376 | tf_op jit(solution)/shard_map/ppermute | solution.py:272
  33.3 0.2 add_convert_fusion.1
  33.5 1.6 %collective-permute-start.6 = (bf16[2,128,1024]{2,1,0:T(8,128)(2,1)S(1)}, bf16[2,128,1024]{2,1,0:T(8,128)(2,1)S(1)}, u32[]{:S(2)}, u32[]{:S(2)}) collective-permute-start(bf16[2,128,1024]{2,1,0:T(8,128)(2,1)S(1)} %add_convert_fusion.1), channel_id=1, source_target_pairs={{0,16},{4,20},{8,12},{12,8},{16,0},{20,4},{24,28},{28,24},{1,17},{... | collective-permute-start | bytes 1572872 | tf_op jit(solution)/shard_map/ppermute | solution.py:287
  35.1 5.0 %collective-permute-done.4 = bf16[128,576]{1,0:T(8,128)(2,1)S(1)} collective-permute-done((bf16[128,576]{1,0:T(8,128)(2,1)S(1)}, bf16[128,576]{1,0:T(8,128)(2,1)S(1)}, u32[]{:S(2)}, u32[]{:S(2)}) %collective-permute-start.4) | collective-permute-done | bytes 147488 | tf_op jit(solution)/shard_map/ppermute | solution.py:272
  40.1 0.2 add_convert_fusion
  40.3 1.5 %collective-permute-start.9 = (bf16[2,128,1024]{2,1,0:T(8,128)(2,1)S(1)}, bf16[2,128,1024]{2,1,0:T(8,128)(2,1)}, u32[]{:S(2)}, u32[]{:S(2)}) collective-permute-start(bf16[2,128,1024]{2,1,0:T(8,128)(2,1)S(1)} %add_convert_fusion), channel_id=1, source_target_pairs={{0,16},{4,20},{8,12},{12,8},{16,0},{20,4},{24,28},{28,24},{1,17},{... | collective-permute-start | bytes 1572872 | tf_op jit(solution)/shard_map/ppermute | solution.py:287
  41.8 0.7 %slice_bitcast_fusion = f32[1,128,512]{2,1,0:T(8,128)} fusion(f32[128,576]{1,0:T(8,128)S(1)} %convert_add_fusion), kind=kLoop, calls=%fused_computation.10 | loop fusion | bytes 524288 | tf_op jit(solution)/shard_map/broadcast_in_dim | solution.py:293
  42.5 0.2 collective-permute-done.6
  42.7 0.9 %add_convert_fusion.5 = bf16[2,64,1024]{2,1,0:T(8,128)(2,1)} fusion(bf16[2,64,1024]{2,1,0:T(8,128)(2,1)S(1)} %get-tuple-element.50, bf16[2,128,1024]{2,1,0:T(8,128)(2,1)S(1)} %collective-permute-done.6, bf16[2,256,1024]{2,1,0:T(8,128)(2,1)S(1)} %collective-permute-done.5), kind=kLoop, calls=%fused_computation.6 | loop fusion | flops 786432 | bytes 1048576 | tf_op jit(solution)/shard_map/convert_element_type | solution.py:284
  43.6 1.5 %collective-permute-start.7 = (bf16[2,64,1024]{2,1,0:T(8,128)(2,1)}, bf16[2,64,1024]{2,1,0:T(8,128)(2,1)}, u32[]{:S(2)}, u32[]{:S(2)}) collective-permute-start(bf16[2,64,1024]{2,1,0:T(8,128)(2,1)} %add_convert_fusion.5), channel_id=1, source_target_pairs={{0,4},{4,0},{8,24},{12,28},{16,20},{20,16},{24,8},{28,12},{1,5},{5... | collective-permute-start | bytes 786440 | tf_op jit(solution)/shard_map/ppermute | solution.py:287
  45.1 0.7 %copy.15 = f32[1,128,64]{1,2,0:T(8,128)} copy(f32[1,128,64]{2,1,0:T(8,128)S(1)} %slice_bitcast_fusion.5) | data formatting | bytes 65536
  45.8 7.2 %collective-permute-done.9 = bf16[2,128,1024]{2,1,0:T(8,128)(2,1)} collective-permute-done((bf16[2,128,1024]{2,1,0:T(8,128)(2,1)S(1)}, bf16[2,128,1024]{2,1,0:T(8,128)(2,1)}, u32[]{:S(2)}, u32[]{:S(2)}) %collective-permute-start.9) | collective-permute-done | bytes 524320 | tf_op jit(solution)/shard_map/ppermute | solution.py:287
  53.0 1.1 %add_convert_fusion.3 = bf16[2,64,1024]{2,1,0:T(8,128)(2,1)S(1)} fusion(bf16[2,64,1024]{2,1,0:T(8,128)(2,1)S(1)} %get-tuple-element.54, bf16[2,128,1024]{2,1,0:T(8,128)(2,1)} %collective-permute-done.9, bf16[2,256,1024]{2,1,0:T(8,128)(2,1)S(1)} %collective-permute-done.8), kind=kLoop, calls=%fused_computation.4 | loop fusion | flops 786432 | bytes 1048576 | tf_op jit(solution)/shard_map/convert_element_type | solution.py:284
  54.1 1.7 %collective-permute-start.10 = (bf16[2,64,1024]{2,1,0:T(8,128)(2,1)S(1)}, bf16[2,64,1024]{2,1,0:T(8,128)(2,1)S(1)}, u32[]{:S(2)}, u32[]{:S(2)}) collective-permute-start(bf16[2,64,1024]{2,1,0:T(8,128)(2,1)S(1)} %add_convert_fusion.3), channel_id=1, source_target_pairs={{0,4},{4,0},{8,24},{12,28},{16,20},{20,16},{24,8},{28,12},{1,5},{5... | collective-permute-start | bytes 786440 | tf_op jit(solution)/shard_map/ppermute | solution.py:287
  55.8 1.2 %add_convert_fusion.4 = bf16[2,64,1024]{2,1,0:T(8,128)(2,1)S(1)} fusion(bf16[2,64,1024]{2,1,0:T(8,128)(2,1)} %collective-permute-done.7, bf16[2,64,1024]{2,1,0:T(8,128)(2,1)S(1)} %get-tuple-element.47, bf16[2,128,1024]{2,1,0:T(8,128)(2,1)} %copy-done.1, bf16[2,256,1024]{2,1,0:T(8,128)(2,1)S(1)} %collective-permute-done.5), kind=kLoop, calls=%fused_computation.5 | loop fusion | flops 1048576 | bytes 1310720 | tf_op jit(solution)/shard_map/convert_element_type | solution.py:284
  57.0 3.5 %collective-permute-done.10 = bf16[2,64,1024]{2,1,0:T(8,128)(2,1)S(1)} collective-permute-done((bf16[2,64,1024]{2,1,0:T(8,128)(2,1)S(1)}, bf16[2,64,1024]{2,1,0:T(8,128)(2,1)S(1)}, u32[]{:S(2)}, u32[]{:S(2)}) %collective-permute-start.10) | collective-permute-done | bytes 262176 | tf_op jit(solution)/shard_map/ppermute | solution.py:287
  60.6 1.1 %add_convert_fusion.2 = bf16[2,64,1024]{2,1,0:T(8,128)(2,1)S(1)} fusion(bf16[2,64,1024]{2,1,0:T(8,128)(2,1)S(1)} %collective-permute-done.10, bf16[2,64,1024]{2,1,0:T(8,128)(2,1)S(1)} %get-tuple-element.51, bf16[2,128,1024]{2,1,0:T(8,128)(2,1)} %collective-permute-done.9, bf16[2,256,1024]{2,1,0:T(8,128)(2,1)S(1)} %collective-permute-done.8), kind=kLoop, calls=%fused_computation.3 | loop fusion | flops 1048576 | bytes 1310720 | tf_op jit(solution)/shard_map/convert_element_type | solution.py:284
  61.7 0.8 %pad_maximum_fusion = (bf16[64,2048]{1,0:T(8,128)(2,1)}, bf16[64,2048]{1,0:T(8,128)(2,1)}) fusion(bf16[64,1024]{1,0:T(8,128)(2,1)S(1)} %get-tuple-element.63, bf16[64,1024]{1,0:T(8,128)(2,1)S(1)} %get-tuple-element.61, bf16[64,1024]{1,0:T(8,128)(2,1)S(1)} %get-tuple-element.62, bf16[64,1024]{1,0:T(8,128)(2,1)S(1)} %get-tuple-element.60), kind=kLoop, calls=%fused_computation.11 | loop fusion | flops 1048576 | bytes 1048576 | tf_op jit(solution)/shard_map/concatenate | solution.py:289
  (14 shorter events, 0.2 us)
Async XLA Ops:
  0.6 7.1 %collective-permute-start = (bf16[128,512]{1,0:T(8,128)(2,1)}, bf16[128,512]{1,0:T(8,128)(2,1)S(1)}, u32[]{:S(2)}, u32[]{:S(2)}) collective-permute-start(bf16[128,512]{1,0:T(8,128)(2,1)} %bitcast.28), channel_id=1, source_target_pairs={{0,4},{4,0},{1,5},{5,1},{2,6},{6,2},{3,7},{7,3},{8,12},{12,8},{9,1... | collective-permute-start | bytes 393224 | tf_op jit(solution)/shard_map/ppermute | solution.py:238
  3.7 4.1 %collective-permute-start.1 = (bf16[64,128]{1,0:T(8,128)(2,1)}, bf16[64,128]{1,0:T(8,128)(2,1)S(1)}, u32[]{:S(2)}, u32[]{:S(2)}) collective-permute-start(bf16[64,128]{1,0:T(8,128)(2,1)} %bitcast.30), channel_id=1, source_target_pairs={{0,4},{4,0},{1,5},{5,1},{2,6},{6,2},{3,7},{7,3},{8,12},{12,8},{9,1... | collective-permute-start | bytes 49160 | tf_op jit(solution)/shard_map/ppermute | solution.py:238
  3.8 3.9 %copy-start = (s32[8,1,512]{2,1,0:T(1,128)S(1)}, s32[8,1,512]{2,1,0:T(1,128)}, u32[]{:S(2)}) copy-start(s32[8,1,512]{2,1,0:T(1,128)} %constant.22.order_ref) | copy-start | bytes 49156
  12.7 20.6 %collective-permute-start.5 = (bf16[2,256,1024]{2,1,0:T(8,128)(2,1)S(1)}, bf16[2,256,1024]{2,1,0:T(8,128)(2,1)S(1)}, u32[]{:S(2)}, u32[]{:S(2)}) collective-permute-start(bf16[2,256,1024]{2,1,0:T(8,128)(2,1)S(1)} %get-tuple-element.48), channel_id=1, source_target_pairs={{0,8},{4,12},{8,0},{12,4},{16,24},{20,28},{24,16},{28,20},{1,9},{5... | collective-permute-start | bytes 3145736 | tf_op jit(solution)/shard_map/ppermute | solution.py:287
  17.7 6.8 %collective-permute-start.2 = (bf16[128,576]{1,0:T(8,128)(2,1)S(1)}, bf16[128,576]{1,0:T(8,128)(2,1)S(1)}, u32[]{:S(2)}, u32[]{:S(2)}) collective-permute-start(bf16[128,576]{1,0:T(8,128)(2,1)S(1)} %get-tuple-element.46), channel_id=1, source_target_pairs={{0,4},{4,0},{1,5},{5,1},{2,6},{6,2},{3,7},{7,3},{8,12},{12,8},{9,1... | collective-permute-start | bytes 442376 | tf_op jit(solution)/shard_map/ppermute | solution.py:238
  19.7 20.4 %collective-permute-start.8 = (bf16[2,256,1024]{2,1,0:T(8,128)(2,1)S(1)}, bf16[2,256,1024]{2,1,0:T(8,128)(2,1)S(1)}, u32[]{:S(2)}, u32[]{:S(2)}) collective-permute-start(bf16[2,256,1024]{2,1,0:T(8,128)(2,1)S(1)} %get-tuple-element.52), channel_id=1, source_target_pairs={{0,8},{4,12},{8,0},{12,4},{16,24},{20,28},{24,16},{28,20},{1,9},{5... | collective-permute-start | bytes 3145736 | tf_op jit(solution)/shard_map/ppermute | solution.py:287
  24.6 5.9 %collective-permute-start.3 = (bf16[128,576]{1,0:T(8,128)(2,1)S(1)}, bf16[128,576]{1,0:T(8,128)(2,1)S(1)}, u32[]{:S(2)}, u32[]{:S(2)}) collective-permute-start(bf16[128,576]{1,0:T(8,128)(2,1)S(1)} %add_convert_fusion.7), channel_id=1, source_target_pairs={{0,1},{1,0},{2,3},{3,2},{4,5},{5,4},{6,7},{7,6},{8,9},{9,8},{10,11... | collective-permute-start | bytes 442376 | tf_op jit(solution)/shard_map/ppermute | solution.py:272
  30.5 9.5 %collective-permute-start.4 = (bf16[128,576]{1,0:T(8,128)(2,1)S(1)}, bf16[128,576]{1,0:T(8,128)(2,1)S(1)}, u32[]{:S(2)}, u32[]{:S(2)}) collective-permute-start(bf16[128,576]{1,0:T(8,128)(2,1)S(1)} %add_convert_fusion.6), channel_id=1, source_target_pairs={{0,2},{1,3},{2,0},{3,1},{4,6},{5,7},{6,4},{7,5},{8,10},{9,11},{10,... | collective-permute-start | bytes 442376 | tf_op jit(solution)/shard_map/ppermute | solution.py:272
  33.5 9.2 %collective-permute-start.6 = (bf16[2,128,1024]{2,1,0:T(8,128)(2,1)S(1)}, bf16[2,128,1024]{2,1,0:T(8,128)(2,1)S(1)}, u32[]{:S(2)}, u32[]{:S(2)}) collective-permute-start(bf16[2,128,1024]{2,1,0:T(8,128)(2,1)S(1)} %add_convert_fusion.1), channel_id=1, source_target_pairs={{0,16},{4,20},{8,12},{12,8},{16,0},{20,4},{24,28},{28,24},{1,17},{... | collective-permute-start | bytes 1572872 | tf_op jit(solution)/shard_map/ppermute | solution.py:287
  40.3 12.8 %collective-permute-start.9 = (bf16[2,128,1024]{2,1,0:T(8,128)(2,1)S(1)}, bf16[2,128,1024]{2,1,0:T(8,128)(2,1)}, u32[]{:S(2)}, u32[]{:S(2)}) collective-permute-start(bf16[2,128,1024]{2,1,0:T(8,128)(2,1)S(1)} %add_convert_fusion), channel_id=1, source_target_pairs={{0,16},{4,20},{8,12},{12,8},{16,0},{20,4},{24,28},{28,24},{1,17},{... | collective-permute-start | bytes 1572872 | tf_op jit(solution)/shard_map/ppermute | solution.py:287
  42.7 0.9 %copy-start.1 = (bf16[2,128,1024]{2,1,0:T(8,128)(2,1)}, bf16[2,128,1024]{2,1,0:T(8,128)(2,1)S(1)}, u32[]{:S(2)}) copy-start(bf16[2,128,1024]{2,1,0:T(8,128)(2,1)S(1)} %collective-permute-done.6) | copy-start | bytes 1572868
  43.6 12.2 %collective-permute-start.7 = (bf16[2,64,1024]{2,1,0:T(8,128)(2,1)}, bf16[2,64,1024]{2,1,0:T(8,128)(2,1)}, u32[]{:S(2)}, u32[]{:S(2)}) collective-permute-start(bf16[2,64,1024]{2,1,0:T(8,128)(2,1)} %add_convert_fusion.5), channel_id=1, source_target_pairs={{0,4},{4,0},{8,24},{12,28},{16,20},{20,16},{24,8},{28,12},{1,5},{5... | collective-permute-start | bytes 786440 | tf_op jit(solution)/shard_map/ppermute | solution.py:287
  54.1 6.4 %collective-permute-start.10 = (bf16[2,64,1024]{2,1,0:T(8,128)(2,1)S(1)}, bf16[2,64,1024]{2,1,0:T(8,128)(2,1)S(1)}, u32[]{:S(2)}, u32[]{:S(2)}) collective-permute-start(bf16[2,64,1024]{2,1,0:T(8,128)(2,1)S(1)} %add_convert_fusion.3), channel_id=1, source_target_pairs={{0,4},{4,0},{8,24},{12,28},{16,20},{20,16},{24,8},{28,12},{1,5},{5... | collective-permute-start | bytes 786440 | tf_op jit(solution)/shard_map/ppermute | solution.py:287

commit v3 on v2

--- a/solution.py
+++ b/solution.py
@@ -9,6 +9,7 @@
 from jax.experimental.pallas import tpu as pltpu
 from jax.sharding import PartitionSpec as P
 
+
 DR = 64
 DN = 128
 DV = 128
@@ -16,9 +17,9 @@
 
 MASKED = -1e30
 GROUP = 4
-VMEM_LIMIT = 16 << 20
-LOAD_LIMIT = 16 << 20
-CHUNKS = 2
+VMEM_LIMIT = 6 << 20
+LOAD_LIMIT = 4 << 20
+ADD_LIMIT = 2 << 20
 NT = (((1,), (1,)), ((), ()))
 
 
@@ -84,7 +85,7 @@
     copies = [pltpu.make_async_copy(a, b, sems.at[k]) for k, (a, b) in enumerate(pairs)]
     for copy in copies:
         copy.start()
-    rows, width = latent_out.shape
+    rows, _ = latent_out.shape
     for copy in copies[:3]:
         copy.wait()
     mine = place_ref[1]
@@ -116,14 +117,15 @@
     return dot(latent, pick).astype(jnp.bfloat16).T
 
 
-def grads_body(place_ref, order_ref, *rest, ctx_size, start, count, group, has_prior, final, pieces):
+def grads_body(place_ref, order_ref, *rest, ctx_size, start, count, first_col, group, has_prior,
+               aliased, final, pieces):
     far_latents = rest[:ctx_size - 1]
     far_ropes = rest[ctx_size - 1:2 * ctx_size - 2]
     (latent_ref, rope_ref, query_ref, grad_ref, lse_ref, delta_ref, wuk_ref, wuv_ref, keys_ref,
      values_ref, flat_ref, bias_ref, *rest) = rest[2 * ctx_size - 2:]
     if has_prior:
         prior_ref, *rest = rest
-    dq_ref, *rest = rest
+    dq_ref, *rest = rest[aliased:]
     piece_refs, total_refs = rest[:pieces], rest[pieces:]
     rows, width = latent_ref.shape
     scale = 1.0 / math.sqrt(DQ)
@@ -135,7 +137,7 @@
     latent_total = prior_ref[:, :width] if has_prior else 0.0
     for first in range(0, count, group):
         span = slice((start + first) * DN, (start + first + group) * DN)
-        out_span = slice(first * DN, (first + group) * DN)
+        out_span = slice(first_col + first * DN, first_col + (first + group) * DN)
         wuk = wuk_ref[:, span]
         wuv = wuv_ref[:, span]
         keys_all = jnp.concatenate([keys_ref[:, span], dot(far, wuk).astype(jnp.bfloat16)], axis=0)
@@ -148,7 +150,6 @@
             head = start + first + inner
             cols = slice(head * DN, (head + 1) * DN)
             wide = slice(head * DQ, (head + 1) * DQ)
-            out_wide = slice((first + inner) * DQ, (first + inner + 1) * DQ)
             part = slice(inner * DN, (inner + 1) * DN)
             keys = jnp.concatenate([keys_all[:, part], rope], axis=1)
             query = query_ref[:, wide]
@@ -158,7 +159,7 @@
             weights = jnp.exp(dot_nt(keys, query) * scale - lse + bias)
             dots = dot_nt(values_all[:, part], grad)
             score_grad = (weights * (dots - delta) * scale).astype(jnp.bfloat16)
-            dq_ref[:, out_wide] = dot(score_grad.T, keys).astype(jnp.bfloat16)
+            dq_ref[:, wide] = dot(score_grad.T, keys).astype(jnp.bfloat16)
             key_grad = dot(score_grad, query)
             value_grads.append(dot(weights.astype(jnp.bfloat16), grad).astype(jnp.bfloat16))
             key_grads.append(key_grad[:, :DN].astype(jnp.bfloat16))
@@ -205,13 +206,15 @@
     )(place, *operands)
 
 
-def chunk_grads(place, order, latents, ropes, loaded, prior, *, start, count, final):
+def chunk_grads(place, order, latents, ropes, loaded, prior, query_grad, pieces, *, start, count,
+                chunk_heads, first_head, final):
     ctx_size = len(latents) + 1
     rows, width = loaded[0].shape
     blocks = order.shape[0]
     smem = pl.BlockSpec(memory_space=pltpu.SMEM)
     vmem = pl.BlockSpec(memory_space=pltpu.VMEM)
-    operands = [*latents, *ropes, *loaded] + ([] if prior is None else [prior])
+    buffers = ([] if query_grad is None else [query_grad]) + list(pieces)
+    operands = [*latents, *ropes, *loaded] + ([] if prior is None else [prior]) + buffers
     operands = [in_vmem(a) for a in operands]
     sizes = [width >> (s + 1) for s in range(blocks.bit_length() - 1)]
     sizes.append(sizes[-1])
@@ -219,18 +222,83 @@
         totals = [pltpu.VMEM((rows, width + DR), jnp.bfloat16)] * ctx_size
     else:
         totals = [pltpu.VMEM((ctx_size * rows, width + DR), jnp.float32)]
+    first_buffer = 2 + len(operands) - len(buffers)
     outs = pl.pallas_call(
         functools.partial(grads_body, ctx_size=ctx_size, start=start, count=count,
-                          group=math.gcd(count, GROUP), has_prior=prior is not None, final=final,
+                          first_col=(start - first_head) * DN, group=math.gcd(count, GROUP),
+                          has_prior=prior is not None, aliased=len(buffers), final=final,
                           pieces=len(sizes)),
         in_specs=[smem] + [vmem] * (1 + len(operands)),
         out_specs=[vmem] * (1 + len(sizes) + len(totals)),
-        out_shape=[pltpu.VMEM((rows, count * DQ), jnp.bfloat16)]
-        + [pltpu.VMEM((2, size, count * DN), jnp.bfloat16) for size in sizes] + totals,
+        out_shape=[pltpu.VMEM(loaded[2].shape, jnp.bfloat16)]
+        + [pltpu.VMEM((2, size, chunk_heads * DN), jnp.bfloat16) for size in sizes] + totals,
+        input_output_aliases={first_buffer + k: k for k in range(len(buffers))},
         compiler_params=pltpu.CompilerParams(vmem_limit_bytes=VMEM_LIMIT),
         name="grads",
     )(place, order, *operands)
     return outs[0], outs[1:1 + len(sizes)], outs[1 + len(sizes):]
+
+
+def piece_sum(refs, offsets, size):
+    total = refs[0][...].astype(jnp.float32)
+    for ref, first in zip(refs[1:], offsets):
+        total = total + ref[:, first:first + size, :].astype(jnp.float32)
+    return total.astype(jnp.bfloat16)
+
+
+def add_body(*refs, offsets):
+    refs[-1][...] = piece_sum(refs[:-1], offsets, refs[0].shape[1])
+
+
+def last_body(*refs):
+    *refs, uk_ref, uv_ref = refs
+    width = refs[0].shape[2]
+    for chunk in range(len(refs) // 2):
+        keep_ref, arrival_ref = refs[2 * chunk:2 * chunk + 2]
+        total = piece_sum((keep_ref, arrival_ref), (0,), keep_ref.shape[1])
+        uk_ref[:, chunk * width:(chunk + 1) * width] = total[0]
+        uv_ref[:, chunk * width:(chunk + 1) * width] = total[1]
+
+
+def piece_offsets(pieces, stage):
+    sizes = [p.shape[1] for p in pieces]
+    return tuple(sum(sizes[past + 1:stage]) for past in range(stage))
+
+
+def add_arrivals(pieces, stage, arrivals):
+    operands = [in_vmem(a) for a in (pieces[stage], *arrivals)]
+    vmem = pl.BlockSpec(memory_space=pltpu.VMEM)
+    return pl.pallas_call(
+        functools.partial(add_body, offsets=piece_offsets(pieces, stage)),
+        in_specs=[vmem] * len(operands),
+        out_specs=vmem,
+        out_shape=pltpu.VMEM(pieces[stage].shape, jnp.bfloat16),
+        compiler_params=pltpu.CompilerParams(vmem_limit_bytes=ADD_LIMIT),
+        name="add",
+    )(*operands)
+
+
+def last_sums(keeps, arrivals):
+    operands = [in_vmem(a) for pair in zip(keeps, arrivals) for a in pair]
+    _, size, width = keeps[0].shape
+    vmem = pl.BlockSpec(memory_space=pltpu.VMEM)
+    out = jax.ShapeDtypeStruct((size, width * len(keeps)), jnp.bfloat16)
+    return pl.pallas_call(
+        last_body,
+        in_specs=[vmem] * len(operands),
+        out_specs=[vmem] * 2,
+        out_shape=[out, out],
+        compiler_params=pltpu.CompilerParams(vmem_limit_bytes=ADD_LIMIT),
+        name="last",
+    )(*operands)
+
+
+def kernel_plan(head_count):
+    groups = head_count // math.gcd(head_count, GROUP)
+    if groups % 4:
+        return [(0, head_count, 0)]
+    half = head_count // 2
+    return [(0, half, 0), (half, half // 2, 1), (half + half // 2, half // 2, 1)]
 
 
 def shifted(value, axis, steps):
@@ -250,20 +318,19 @@
     ropes = [shifted(rope_cols, "ctx", -s) for s in range(1, ctx_size)]
     loaded = load(place, positions.reshape(ctx_size, 1, rows), order, latent[0], rope_cols, query[0],
                   grad_out[0], attn_out[0], lse[0], w_uk, w_uv)
-    head_count = lse.shape[1]
-    chunks = math.gcd(head_count // math.gcd(head_count, GROUP), CHUNKS)
-    count = head_count // chunks
-    prior = None
-    chunk_pieces = []
-    query_grads = []
-    for chunk in range(chunks):
+    plan = kernel_plan(lse.shape[1])
+    chunks = plan[-1][2] + 1
+    chunk_heads = lse.shape[1] // chunks
+    prior = query_grad = None
+    chunk_pieces = [()] * chunks
+    for number, (start, count, chunk) in enumerate(plan):
         query_grad, pieces, totals = chunk_grads(
-            place, order, latents, ropes, loaded, prior,
-            start=chunk * count, count=count, final=chunk + 1 == chunks,
+            place, order, latents, ropes, loaded, prior, query_grad, chunk_pieces[chunk],
+            start=start, count=count, chunk_heads=chunk_heads, first_head=chunk * chunk_heads,
+            final=number + 1 == len(plan),
         )
         prior = totals[0]
-        chunk_pieces.append(pieces)
-        query_grads.append(query_grad)
+        chunk_pieces[chunk] = pieces
     summed = totals[0].astype(jnp.float32)
     for s in range(1, ctx_size):
         summed = summed + shifted(totals[s], "ctx", s).astype(jnp.float32)
@@ -271,25 +338,19 @@
         mine = summed.astype(jnp.bfloat16)
         other = lax.ppermute(mine, "head", [(s, s ^ bit) for s in range(head_size)])
         summed = mine.astype(jnp.float32) + other.astype(jnp.float32)
-    finals = []
+    keeps = []
+    lasts = []
     for pieces in chunk_pieces:
         arrivals = []
-        for stage, piece in enumerate(pieces):
-            size = piece.shape[1]
-            done = sum(p.shape[1] for p in pieces[:stage])
-            value = piece.astype(jnp.float32)
-            for past, arrival in enumerate(arrivals):
-                first = done - sum(p.shape[1] for p in pieces[:past + 1])
-                value = value + arrival[:, first:first + size].astype(jnp.float32)
-            value = value.astype(jnp.bfloat16)
-            if stage + 1 < len(pieces):
-                pairs = stage_pairs(stage, dp_size, ctx_size)
-                arrivals.append(lax.ppermute(value, ("dp", "ctx"), pairs))
-        finals.append(value)
-    weight_uk = jnp.concatenate([part[0] for part in finals], axis=1)
-    weight_uv = jnp.concatenate([part[1] for part in finals], axis=1)
+        for stage in range(len(pieces) - 1):
+            value = add_arrivals(pieces, stage, arrivals) if stage else pieces[0]
+            pairs = stage_pairs(stage, dp_size, ctx_size)
+            arrivals.append(lax.ppermute(value, ("dp", "ctx"), pairs))
+        keeps.append(add_arrivals(pieces, len(pieces) - 1, arrivals[:-1]))
+        lasts.append(arrivals[-1])
+    weight_uk, weight_uv = last_sums(keeps, lasts)
     return (
-        jnp.concatenate(query_grads, axis=1)[None],
+        query_grad[None],
         summed[None, :, :width],
         summed[None, :, width:],
         weight_uk,

time: 62.7 us -> 53.3 us (0.85); the launches traced: 62.5 us -> 52.5 us
  waiting for transfers between devices: 23.8 us -> 13.5 us
  other arithmetic: 6.62 us -> 0.19 us
  Pallas kernels: 13.7 us -> 18.5 us
  local copies, waits for them, and re-layouts: 1.48 us -> 4.22 us
  starting transfers between devices: 16.2 us -> 15.3 us
    ppermute x6, waiting for transfers between devices: 11 us -> 2.29 us  [on_device(): arrivals.append(lax.ppermute(value, ('dp', 'ctx'), pairs))]
    convert_element_type x6 -> x0, other arithmetic: 4.64 us -> none  [on_device(): value = value.astype(jnp.bfloat16)]
    pallas_call x0 -> x7, Pallas kernels: none -> 3.96 us  [the longest x6 2.05 us: add_arrivals(): pl.pallas_call(functools.partial(add_body, offsets=piece_offsets(pieces,...]
    unnamed x5 -> x10, local copies, waits for them, and re-layouts: 0.7 us -> 2.54 us
    ppermute x2, waiting for transfers between devices: 8.05 us -> 6.68 us  [on_device(): other = lax.ppermute(mine, 'head', [(s, s ^ bit) for s in range(head_size)])]
    broadcast_in_dim x1 -> x0, other arithmetic: 0.96 us -> none  [on_device(): jnp.concatenate(query_grads, axis=1)[None]]
    broadcast_in_dim x1, local copies, waits for them, and re-layouts: 0.73 us -> 1.67 us  [on_device(): summed[None, :, :width]]
    pallas_call x2 -> x3, Pallas kernels: 9.9 us -> 10.8 us  [chunk_grads(): pl.pallas_call(functools.partial(grads_body, ctx_size=ctx_size, start=sta...]
  transfers between devices with their start and end apart: 11 -> 11, of which waited for: 7 -> 5; matrix products, arithmetic and copies ran while one was open for 10% -> 7% of each run, Pallas kernels for 14% -> 22%
where the time goes in v3:
time: 53.3 us; the launch traced here: 52.5 us
  Pallas kernels  18.5 us (35%)
  starting transfers between devices  15.3 us (29%)
  waiting for transfers between devices  13.5 us (25%)
  local copies, waits for them, and re-layouts  4.22 us (8%)
  between operations  0.75 us (1%)
    pallas_call x3, Pallas kernels, chunk_grads(): pl.pallas_call(functools.partial(grads_body, ctx_size=ctx_size, start=sta...  10.8 us
    ppermute x2, waiting for transfers between devices, on_device(): other = lax.ppermute(mine, 'head', [(s, s ^ bit) for s in range(head_size)])  6.68 us
    ppermute x6, starting transfers between devices, on_device(): arrivals.append(lax.ppermute(value, ('dp', 'ctx'), pairs))  5.65 us
    ppermute x3, starting transfers between devices, shifted(): lax.ppermute(value, axis, [(s, (s + steps) % count) for s in range(count)])  5.01 us
    ppermute x2, starting transfers between devices, on_device(): other = lax.ppermute(mine, 'head', [(s, s ^ bit) for s in range(head_size)])  4.62 us
    ppermute x3, waiting for transfers between devices, shifted(): lax.ppermute(value, axis, [(s, (s + steps) % count) for s in range(count)])  4.56 us
    pallas_call x1, Pallas kernels, load(): pl.pallas_call(functools.partial(load_body, ctx_size=ctx_size), in_specs=...  3.78 us
    unnamed x10, local copies, waits for them, and re-layouts  2.54 us
  transfers between devices with their start and end apart: 11, of which 5 were waited for; matrix products, arithmetic and copies ran while one was open for 7% of the time, Pallas kernels for 22%

profile of v3, /device:TPU:0, one launch (start us, length us, event | category | flops | bytes accessed | tf_op | source)
XLA Modules:
  0.0 52.5 jit_solution(8288011205358771685)
XLA Ops:
  0.6 3.1 %collective-permute-start = (bf16[128,512]{1,0:T(8,128)(2,1)}, bf16[128,512]{1,0:T(8,128)(2,1)S(1)}, u32[]{:S(2)}, u32[]{:S(2)}) collective-permute-start(bf16[128,512]{1,0:T(8,128)(2,1)} %bitcast.20), channel_id=1, source_target_pairs={{0,4},{4,0},{1,5},{5,1},{2,6},{6,2},{3,7},{7,3},{8,12},{12,8},{9,1... | collective-permute-start | bytes 393224 | tf_op jit(solution)/shard_map/ppermute | solution.py:306
  3.7 0.1 collective-permute-start.1
  3.8 0.1 pad_add_fusion.place_ref
  3.8 3.8 %load.1 = (bf16[128,512]{1,0:T(8,128)(2,1)S(1)}, bf16[64,128]{1,0:T(8,128)(2,1)S(1)}, bf16[128,3072]{1,0:T(8,128)(2,1)S(1)}, bf16[128,2048]{1,0:T(8,128)(2,1)S(1...) custom-call(s32[2]{0:T(128)S(1)} %pad_add_fusion.place_ref, ...), custom_call_target="tpu_custom_call" | custom-call | tf_op jit(solution)/shard_map/load/pallas_call | solution.py:197
  7.6 0.1 collective-permute-done.1.rest_1_
  7.8 5.0 %grads.3 = (bf16[128,3072]{1,0:T(8,128)(2,1)S(1)}, bf16[2,256,1024]{2,1,0:T(8,128)(2,1)S(1)}, bf16[2,128,1024]{2,1,0:T(8,128)(2,1)S(1)}, bf16[2,64,1024]{2,1,0:T...) custom-call(s32[2]{0:T(128)S(1)} %pad_add_fusion.place_ref, s32[8,1,512]{2,1,0:T(1,128)S(1)} %copy-done, ...), custom_call_target="tpu_custom_call" | custom-call | tf_op jit(solution)/shard_map/grads/pallas_call | solution.py:226
  12.7 0.1 collective-permute-start.5
  12.8 2.9 %grads.4 = (bf16[128,3072]{1,0:T(8,128)(2,1)S(1)}, bf16[2,256,1024]{2,1,0:T(8,128)(2,1)S(1)}, bf16[2,128,1024]{2,1,0:T(8,128)(2,1)S(1)}, bf16[2,64,1024]{2,1,0:T...) custom-call(s32[2]{0:T(128)S(1)} %pad_add_fusion.place_ref, ...), custom_call_target="tpu_custom_call", output_to_operand_aliasing={{0}: (17, {})} | custom-call | tf_op jit(solution)/shard_map/grads/pallas_call | solution.py:226
  15.8 2.9 %grads.5 = (bf16[128,3072]{1,0:T(8,128)(2,1)S(1)}, bf16[2,256,1024]{2,1,0:T(8,128)(2,1)S(1)}, bf16[2,128,1024]{2,1,0:T(8,128)(2,1)S(1)}, bf16[2,64,1024]{2,1,0:T...) custom-call(s32[2]{0:T(128)S(1)} %pad_add_fusion.place_ref, ...), custom_call_target="tpu_custom_call", output_to_operand_aliasing={{0}: (17, {}), {1}: (18, {}), {2}: (19, {}), {3}: (20, {}),... | custom-call | tf_op jit(solution)/shard_map/grads/pallas_call | solution.py:226
  18.7 0.6 %collective-permute-start.8 = (bf16[2,256,1024]{2,1,0:T(8,128)(2,1)S(1)}, bf16[2,256,1024]{2,1,0:T(8,128)(2,1)S(1)}, u32[]{:S(2)}, u32[]{:S(2)}) collective-permute-start(bf16[2,256,1024]{2,1,0:T(8,128)(2,1)S(1)} %get-tuple-element.66), channel_id=1, source_target_pairs={{0,8},{4,12},{8,0},{12,4},{16,24},{20,28},{24,16},{28,20},{1,9},{5... | collective-permute-start | bytes 3145736 | tf_op jit(solution)/shard_map/ppermute | solution.py:348
  19.2 1.9 %collective-permute-start.2 = (bf16[128,576]{1,0:T(8,128)(2,1)S(1)}, bf16[128,576]{1,0:T(8,128)(2,1)S(1)}, u32[]{:S(2)}, u32[]{:S(2)}) collective-permute-start(bf16[128,576]{1,0:T(8,128)(2,1)S(1)} %get-tuple-element.60), channel_id=1, source_target_pairs={{0,4},{4,0},{1,5},{5,1},{2,6},{6,2},{3,7},{7,3},{8,12},{12,8},{9,1... | collective-permute-start | bytes 442376 | tf_op jit(solution)/shard_map/ppermute | solution.py:306
  21.1 4.4 %collective-permute-done.2 = bf16[128,576]{1,0:T(8,128)(2,1)S(1)} collective-permute-done((bf16[128,576]{1,0:T(8,128)(2,1)S(1)}, bf16[128,576]{1,0:T(8,128)(2,1)S(1)}, u32[]{:S(2)}, u32[]{:S(2)}) %collective-permute-start.2) | collective-permute-done | bytes 147488 | tf_op jit(solution)/shard_map/ppermute | solution.py:306
  25.6 1.9 %collective-permute-start.3 = (bf16[128,576]{1,0:T(8,128)(2,1)S(1)}, bf16[128,576]{1,0:T(8,128)(2,1)S(1)}, u32[]{:S(2)}, u32[]{:S(2)}) collective-permute-start(bf16[128,576]{1,0:T(8,128)(2,1)S(1)} %add_convert_fusion.1), channel_id=1, source_target_pairs={{0,1},{1,0},{2,3},{3,2},{4,5},{5,4},{6,7},{7,6},{8,9},{9,8},{10,11... | collective-permute-start | bytes 442376 | tf_op jit(solution)/shard_map/ppermute | solution.py:339
  27.5 0.1 add.27
  27.6 1.5 %collective-permute-start.6 = (bf16[2,128,1024]{2,1,0:T(8,128)(2,1)S(1)}, bf16[2,128,1024]{2,1,0:T(8,128)(2,1)S(1)}, u32[]{:S(2)}, u32[]{:S(2)}) collective-permute-start(bf16[2,128,1024]{2,1,0:T(8,128)(2,1)S(1)} %add.27), channel_id=1, source_target_pairs={{0,16},{4,20},{8,12},{12,8},{16,0},{20,4},{24,28},{28,24},{1,17},{... | collective-permute-start | bytes 1572872 | tf_op jit(solution)/shard_map/ppermute | solution.py:348
  29.1 0.1 add.30
  29.3 0.6 %collective-permute-start.9 = (bf16[2,128,1024]{2,1,0:T(8,128)(2,1)S(1)}, bf16[2,128,1024]{2,1,0:T(8,128)(2,1)S(1)}, u32[]{:S(2)}, u32[]{:S(2)}) collective-permute-start(bf16[2,128,1024]{2,1,0:T(8,128)(2,1)S(1)} %add.30), channel_id=1, source_target_pairs={{0,16},{4,20},{8,12},{12,8},{16,0},{20,4},{24,28},{28,24},{1,17},{... | collective-permute-start | bytes 1572872 | tf_op jit(solution)/shard_map/ppermute | solution.py:348
  29.9 1.2 %collective-permute-done.3 = bf16[128,576]{1,0:T(8,128)(2,1)S(1)} collective-permute-done((bf16[128,576]{1,0:T(8,128)(2,1)S(1)}, bf16[128,576]{1,0:T(8,128)(2,1)S(1)}, u32[]{:S(2)}, u32[]{:S(2)}) %collective-permute-start.3) | collective-permute-done | bytes 147488 | tf_op jit(solution)/shard_map/ppermute | solution.py:339
  31.1 2.7 %collective-permute-start.4 = (bf16[128,576]{1,0:T(8,128)(2,1)S(1)}, bf16[128,576]{1,0:T(8,128)(2,1)S(1)}, u32[]{:S(2)}, u32[]{:S(2)}) collective-permute-start(bf16[128,576]{1,0:T(8,128)(2,1)S(1)} %add_convert_fusion), channel_id=1, source_target_pairs={{0,2},{1,3},{2,0},{3,1},{4,6},{5,7},{6,4},{7,5},{8,10},{9,11},{10,... | collective-permute-start | bytes 442376 | tf_op jit(solution)/shard_map/ppermute | solution.py:339
  33.9 0.9 %copy.28 = bf16[1,128,3072]{2,1,0:T(8,128)(2,1)} copy(bf16[1,128,3072]{2,1,0:T(8,128)(2,1)S(1)} %bitcast.16) | data formatting | bytes 1572864
  34.8 5.4 %collective-permute-done.4 = bf16[128,576]{1,0:T(8,128)(2,1)S(1)} collective-permute-done((bf16[128,576]{1,0:T(8,128)(2,1)S(1)}, bf16[128,576]{1,0:T(8,128)(2,1)S(1)}, u32[]{:S(2)}, u32[]{:S(2)}) %collective-permute-start.4) | collective-permute-done | bytes 147488 | tf_op jit(solution)/shard_map/ppermute | solution.py:339
  40.3 0.8 %add.29 = bf16[2,64,1024]{2,1,0:T(8,128)(2,1)} custom-call(bf16[2,64,1024]{2,1,0:T(8,128)(2,1)S(1)} %get-tuple-element.64.refs_0_, bf16[2,256,1024]{2,1,0:T(8,128)(2,1)S(1)} %collective-permute-done.5.refs_1_, bf16[2,128,1024]{2,1,0:T(8,128)(2,1)S(1)} %collective-permute-done.6.refs_2_), custom_call_target="tpu_custom_call" | custom-call | tf_op jit(solution)/shard_map/add/pallas_call | solution.py:271
  41.1 1.5 %collective-permute-start.7 = (bf16[2,64,1024]{2,1,0:T(8,128)(2,1)}, bf16[2,64,1024]{2,1,0:T(8,128)(2,1)}, u32[]{:S(2)}, u32[]{:S(2)}) collective-permute-start(bf16[2,64,1024]{2,1,0:T(8,128)(2,1)} %add.29), channel_id=1, source_target_pairs={{0,4},{4,0},{8,24},{12,28},{16,20},{20,16},{24,8},{28,12},{1,5},{5... | collective-permute-start | bytes 786440 | tf_op jit(solution)/shard_map/ppermute | solution.py:348
  42.6 0.8 %add.32 = bf16[2,64,1024]{2,1,0:T(8,128)(2,1)} custom-call(bf16[2,64,1024]{2,1,0:T(8,128)(2,1)S(1)} %get-tuple-element.68.refs_0_, bf16[2,256,1024]{2,1,0:T(8,128)(2,1)S(1)} %collective-permute-done.8.refs_1_, bf16[2,128,1024]{2,1,0:T(8,128)(2,1)S(1)} %collective-permute-done.9.refs_2_), custom_call_target="tpu_custom_call" | custom-call | tf_op jit(solution)/shard_map/add/pallas_call | solution.py:271
  43.4 1.4 %collective-permute-start.10 = (bf16[2,64,1024]{2,1,0:T(8,128)(2,1)}, bf16[2,64,1024]{2,1,0:T(8,128)(2,1)}, u32[]{:S(2)}, u32[]{:S(2)}) collective-permute-start(bf16[2,64,1024]{2,1,0:T(8,128)(2,1)} %add.32), channel_id=1, source_target_pairs={{0,4},{4,0},{8,24},{12,28},{16,20},{20,16},{24,8},{28,12},{1,5},{5... | collective-permute-start | bytes 786440 | tf_op jit(solution)/shard_map/ppermute | solution.py:348
  44.8 0.7 %copy.21 = f32[1,128,64]{1,2,0:T(8,128)} copy(f32[1,128,64]{2,1,0:T(8,128)S(1)} %slice_bitcast_fusion.1) | data formatting | bytes 65536
  45.5 1.7 %slice_bitcast_fusion = f32[1,128,512]{2,1,0:T(8,128)} fusion(f32[128,576]{1,0:T(8,128)} %copy-done.3), kind=kLoop, calls=%fused_computation.3 | loop fusion | bytes 524288 | tf_op jit(solution)/shard_map/broadcast_in_dim | solution.py:354
  47.1 0.9 %copy-done.2 = bf16[2,64,1024]{2,1,0:T(8,128)(2,1)S(1)} copy-done((bf16[2,64,1024]{2,1,0:T(8,128)(2,1)S(1)}, bf16[2,64,1024]{2,1,0:T(8,128)(2,1)}, u32[]{:S(2)}) %copy-start.2) | copy-done | bytes 262168
  48.1 0.1 add.28.refs_0_
  48.2 0.1 add.31.refs_2_
  48.3 2.3 %collective-permute-done.10.refs_3_ = bf16[2,64,1024]{2,1,0:T(8,128)(2,1)} collective-permute-done((bf16[2,64,1024]{2,1,0:T(8,128)(2,1)}, bf16[2,64,1024]{2,1,0:T(8,128)(2,1)}, u32[]{:S(2)}, u32[]{:S(2)}) %collective-permute-start.10) | collective-permute-done | bytes 262176 | tf_op jit(solution)/shard_map/ppermute | solution.py:348
  50.6 1.9 %last.1 = (bf16[64,2048]{1,0:T(8,128)(2,1)}, bf16[64,2048]{1,0:T(8,128)(2,1)}) custom-call(bf16[2,64,1024]{2,1,0:T(8,128)(2,1)S(1)} %add.28.refs_0_, bf16[2,64,1024]{2,1,0:T(8,128)(2,1)} %collective-permute-done.7.refs_1_, bf16[2,64,1024]{2,1,0:T(8,128)(2,1)S(1)} %add.31.refs_2_, bf16[2,64,1024]{2,1,0:T(8,128)(2,1)} %collective-permute-done.10.refs_3_), custom_call_target="tpu_custom_call" | custom-call | tf_op jit(solution)/shard_map/last/pallas_call | solution.py:286
  (17 shorter events, 0.2 us)
Async XLA Ops:
  0.6 7.1 %collective-permute-start = (bf16[128,512]{1,0:T(8,128)(2,1)}, bf16[128,512]{1,0:T(8,128)(2,1)S(1)}, u32[]{:S(2)}, u32[]{:S(2)}) collective-permute-start(bf16[128,512]{1,0:T(8,128)(2,1)} %bitcast.20), channel_id=1, source_target_pairs={{0,4},{4,0},{1,5},{5,1},{2,6},{6,2},{3,7},{7,3},{8,12},{12,8},{9,1... | collective-permute-start | bytes 393224 | tf_op jit(solution)/shard_map/ppermute | solution.py:306
  3.7 4.1 %collective-permute-start.1 = (bf16[64,128]{1,0:T(8,128)(2,1)}, bf16[64,128]{1,0:T(8,128)(2,1)S(1)}, u32[]{:S(2)}, u32[]{:S(2)}) collective-permute-start(bf16[64,128]{1,0:T(8,128)(2,1)} %bitcast.22), channel_id=1, source_target_pairs={{0,4},{4,0},{1,5},{5,1},{2,6},{6,2},{3,7},{7,3},{8,12},{12,8},{9,1... | collective-permute-start | bytes 49160 | tf_op jit(solution)/shard_map/ppermute | solution.py:306
  3.8 3.9 %copy-start = (s32[8,1,512]{2,1,0:T(1,128)S(1)}, s32[8,1,512]{2,1,0:T(1,128)}, u32[]{:S(2)}) copy-start(s32[8,1,512]{2,1,0:T(1,128)} %constant.22.order_ref) | copy-start | bytes 49156
  12.7 3.0 %copy-start.1 = (bf16[2,64,1024]{2,1,0:T(8,128)(2,1)}, bf16[2,64,1024]{2,1,0:T(8,128)(2,1)S(1)}, u32[]{:S(2)}) copy-start(bf16[2,64,1024]{2,1,0:T(8,128)(2,1)S(1)} %get-tuple-element.61.refs_0_) | copy-start | bytes 786436
  12.7 14.7 %collective-permute-start.5 = (bf16[2,256,1024]{2,1,0:T(8,128)(2,1)S(1)}, bf16[2,256,1024]{2,1,0:T(8,128)(2,1)S(1)}, u32[]{:S(2)}, u32[]{:S(2)}) collective-permute-start(bf16[2,256,1024]{2,1,0:T(8,128)(2,1)S(1)} %get-tuple-element.62), channel_id=1, source_target_pairs={{0,8},{4,12},{8,0},{12,4},{16,24},{20,28},{24,16},{28,20},{1,9},{5... | collective-permute-start | bytes 3145736 | tf_op jit(solution)/shard_map/ppermute | solution.py:348
  18.7 10.5 %collective-permute-start.8 = (bf16[2,256,1024]{2,1,0:T(8,128)(2,1)S(1)}, bf16[2,256,1024]{2,1,0:T(8,128)(2,1)S(1)}, u32[]{:S(2)}, u32[]{:S(2)}) collective-permute-start(bf16[2,256,1024]{2,1,0:T(8,128)(2,1)S(1)} %get-tuple-element.66), channel_id=1, source_target_pairs={{0,8},{4,12},{8,0},{12,4},{16,24},{20,28},{24,16},{28,20},{1,9},{5... | collective-permute-start | bytes 3145736 | tf_op jit(solution)/shard_map/ppermute | solution.py:348
  19.2 6.3 %collective-permute-start.2 = (bf16[128,576]{1,0:T(8,128)(2,1)S(1)}, bf16[128,576]{1,0:T(8,128)(2,1)S(1)}, u32[]{:S(2)}, u32[]{:S(2)}) collective-permute-start(bf16[128,576]{1,0:T(8,128)(2,1)S(1)} %get-tuple-element.60), channel_id=1, source_target_pairs={{0,4},{4,0},{1,5},{5,1},{2,6},{6,2},{3,7},{7,3},{8,12},{12,8},{9,1... | collective-permute-start | bytes 442376 | tf_op jit(solution)/shard_map/ppermute | solution.py:306
  25.6 5.5 %collective-permute-start.3 = (bf16[128,576]{1,0:T(8,128)(2,1)S(1)}, bf16[128,576]{1,0:T(8,128)(2,1)S(1)}, u32[]{:S(2)}, u32[]{:S(2)}) collective-permute-start(bf16[128,576]{1,0:T(8,128)(2,1)S(1)} %add_convert_fusion.1), channel_id=1, source_target_pairs={{0,1},{1,0},{2,3},{3,2},{4,5},{5,4},{6,7},{7,6},{8,9},{9,8},{10,11... | collective-permute-start | bytes 442376 | tf_op jit(solution)/shard_map/ppermute | solution.py:339
  27.6 12.7 %collective-permute-start.6 = (bf16[2,128,1024]{2,1,0:T(8,128)(2,1)S(1)}, bf16[2,128,1024]{2,1,0:T(8,128)(2,1)S(1)}, u32[]{:S(2)}, u32[]{:S(2)}) collective-permute-start(bf16[2,128,1024]{2,1,0:T(8,128)(2,1)S(1)} %add.27), channel_id=1, source_target_pairs={{0,16},{4,20},{8,12},{12,8},{16,0},{20,4},{24,28},{28,24},{1,17},{... | collective-permute-start | bytes 1572872 | tf_op jit(solution)/shard_map/ppermute | solution.py:348
  29.3 13.3 %collective-permute-start.9 = (bf16[2,128,1024]{2,1,0:T(8,128)(2,1)S(1)}, bf16[2,128,1024]{2,1,0:T(8,128)(2,1)S(1)}, u32[]{:S(2)}, u32[]{:S(2)}) collective-permute-start(bf16[2,128,1024]{2,1,0:T(8,128)(2,1)S(1)} %add.30), channel_id=1, source_target_pairs={{0,16},{4,20},{8,12},{12,8},{16,0},{20,4},{24,28},{28,24},{1,17},{... | collective-permute-start | bytes 1572872 | tf_op jit(solution)/shard_map/ppermute | solution.py:348
  31.1 9.1 %collective-permute-start.4 = (bf16[128,576]{1,0:T(8,128)(2,1)S(1)}, bf16[128,576]{1,0:T(8,128)(2,1)S(1)}, u32[]{:S(2)}, u32[]{:S(2)}) collective-permute-start(bf16[128,576]{1,0:T(8,128)(2,1)S(1)} %add_convert_fusion), channel_id=1, source_target_pairs={{0,2},{1,3},{2,0},{3,1},{4,6},{5,7},{6,4},{7,5},{8,10},{9,11},{10,... | collective-permute-start | bytes 442376 | tf_op jit(solution)/shard_map/ppermute | solution.py:339
  40.3 4.5 %copy-start.3 = (f32[128,576]{1,0:T(8,128)}, f32[128,576]{1,0:T(8,128)S(1)}, u32[]{:S(2)}) copy-start(f32[128,576]{1,0:T(8,128)S(1)} %convert_add_fusion) | copy-start | bytes 884740
  41.1 7.2 %collective-permute-start.7 = (bf16[2,64,1024]{2,1,0:T(8,128)(2,1)}, bf16[2,64,1024]{2,1,0:T(8,128)(2,1)}, u32[]{:S(2)}, u32[]{:S(2)}) collective-permute-start(bf16[2,64,1024]{2,1,0:T(8,128)(2,1)} %add.29), channel_id=1, source_target_pairs={{0,4},{4,0},{8,24},{12,28},{16,20},{20,16},{24,8},{28,12},{1,5},{5... | collective-permute-start | bytes 786440 | tf_op jit(solution)/shard_map/ppermute | solution.py:348
  43.4 7.2 %collective-permute-start.10 = (bf16[2,64,1024]{2,1,0:T(8,128)(2,1)}, bf16[2,64,1024]{2,1,0:T(8,128)(2,1)}, u32[]{:S(2)}, u32[]{:S(2)}) collective-permute-start(bf16[2,64,1024]{2,1,0:T(8,128)(2,1)} %add.32), channel_id=1, source_target_pairs={{0,4},{4,0},{8,24},{12,28},{16,20},{20,16},{24,8},{28,12},{1,5},{5... | collective-permute-start | bytes 786440 | tf_op jit(solution)/shard_map/ppermute | solution.py:348
  47.1 0.9 %copy-start.2 = (bf16[2,64,1024]{2,1,0:T(8,128)(2,1)S(1)}, bf16[2,64,1024]{2,1,0:T(8,128)(2,1)}, u32[]{:S(2)}) copy-start(bf16[2,64,1024]{2,1,0:T(8,128)(2,1)} %copy-done.1) | copy-start | bytes 786436

commit v4 on v3

--- a/solution.py
+++ b/solution.py
@@ -117,27 +117,24 @@
     return dot(latent, pick).astype(jnp.bfloat16).T
 
 
-def grads_body(place_ref, order_ref, *rest, ctx_size, start, count, first_col, group, has_prior,
-               aliased, final, pieces):
+def grads_body(place_ref, order_ref, *rest, ctx_size, group):
     far_latents = rest[:ctx_size - 1]
     far_ropes = rest[ctx_size - 1:2 * ctx_size - 2]
     (latent_ref, rope_ref, query_ref, grad_ref, lse_ref, delta_ref, wuk_ref, wuv_ref, keys_ref,
      values_ref, flat_ref, bias_ref, *rest) = rest[2 * ctx_size - 2:]
-    if has_prior:
-        prior_ref, *rest = rest
-    dq_ref, *rest = rest[aliased:]
-    piece_refs, total_refs = rest[:pieces], rest[pieces:]
-    rows, width = latent_ref.shape
+    dq_ref, key_out, value_out, flat_out, *total_refs = rest
+    rows, _ = latent_ref.shape
     scale = 1.0 / math.sqrt(DQ)
     rope = jnp.concatenate([ref[...] for ref in (rope_ref, *far_ropes)], axis=1).T
     far = jnp.concatenate([ref[...] for ref in far_latents], axis=0)
     bias = bias_ref[...]
-    flat = jnp.concatenate([flat_ref[...], rows_first(far, order_ref[place_ref[0]])], axis=1)
-    rope_total = prior_ref[:, width:] if has_prior else 0.0
-    latent_total = prior_ref[:, :width] if has_prior else 0.0
-    for first in range(0, count, group):
-        span = slice((start + first) * DN, (start + first + group) * DN)
-        out_span = slice(first_col + first * DN, first_col + (first + group) * DN)
+    flat_out[...] = jnp.concatenate(
+        [flat_ref[...], rows_first(far, order_ref[place_ref[0]])], axis=1
+    )
+    rope_total = 0.0
+    latent_total = 0.0
+    for first in range(0, lse_ref.shape[0], group):
+        span = slice(first * DN, (first + group) * DN)
         wuk = wuk_ref[:, span]
         wuv = wuv_ref[:, span]
         keys_all = jnp.concatenate([keys_ref[:, span], dot(far, wuk).astype(jnp.bfloat16)], axis=0)
@@ -147,7 +144,7 @@
         key_grads = []
         value_grads = []
         for inner in range(group):
-            head = start + first + inner
+            head = first + inner
             cols = slice(head * DN, (head + 1) * DN)
             wide = slice(head * DQ, (head + 1) * DQ)
             part = slice(inner * DN, (inner + 1) * DN)
@@ -166,17 +163,75 @@
             rope_total = rope_total + key_grad[:, DN:]
         key_flat = jnp.concatenate(key_grads, axis=1)
         value_flat = jnp.concatenate(value_grads, axis=1)
-        row = 0
-        for piece_ref in piece_refs:
-            size = piece_ref.shape[1]
-            piece_ref[0, :, out_span] = dot(flat[row:row + size], key_flat).astype(jnp.bfloat16)
-            piece_ref[1, :, out_span] = dot(flat[row:row + size], value_flat).astype(jnp.bfloat16)
-            row += size
+        key_out[:, span] = key_flat
+        value_out[:, span] = value_flat
         latent_total = latent_total + dot_nt(key_flat, wuk) + dot_nt(value_flat, wuv)
     for chunk, total_ref in enumerate(total_refs):
-        part = slice(chunk * rows, chunk * rows + total_ref.shape[0])
-        total_ref[:, :width] = latent_total[part].astype(total_ref.dtype)
-        total_ref[:, width:] = rope_total[part].astype(total_ref.dtype)
+        part = slice(chunk * rows, (chunk + 1) * rows)
+        total_ref[:rows, :] = latent_total[part].astype(jnp.bfloat16)
+        rope_cols = rope_total[part].T.astype(jnp.bfloat16)
+        extra = total_ref.shape[0] - rows
+        for k in range(DR // extra):
+            total_ref[rows:, k * rows:(k + 1) * rows] = rope_cols[k * extra:(k + 1) * extra]
+
+
+def write_pieces(piece_refs, span, flat, key_flat, value_flat):
+    row = 0
+    for piece_ref in piece_refs:
+        size = piece_ref.shape[1]
+        piece_ref[0, :, span] = dot(flat[row:row + size], key_flat).astype(jnp.bfloat16)
+        piece_ref[1, :, span] = dot(flat[row:row + size], value_flat).astype(jnp.bfloat16)
+        row += size
+
+
+def weights_body(flat_ref, key_ref, value_ref, *piece_refs, start):
+    flat = flat_ref[...]
+    count = piece_refs[0].shape[2]
+    step = math.gcd(count, 256)
+    for first in range(0, count, step):
+        part = slice(start + first, start + first + step)
+        span = slice(first, first + step)
+        write_pieces(piece_refs, span, flat, key_ref[:, part], value_ref[:, part])
+
+
+def store_body(source_ref, out_ref, sem):
+    copy = pltpu.make_async_copy(source_ref, out_ref, sem)
+    copy.start()
+    copy.wait()
+
+
+def store(array):
+    return pl.pallas_call(
+        store_body,
+        in_specs=[pl.BlockSpec(memory_space=pltpu.VMEM)],
+        out_specs=pl.BlockSpec(memory_space=pltpu.HBM),
+        out_shape=pltpu.HBM(array.shape, array.dtype),
+        scratch_shapes=[pltpu.SemaphoreType.DMA(())],
+        compiler_params=pltpu.CompilerParams(vmem_limit_bytes=ADD_LIMIT),
+        name="store",
+    )(in_vmem(array))
+
+
+def piece_sizes(width, blocks):
+    sizes = [width >> (s + 1) for s in range(blocks.bit_length() - 1)]
+    return sizes + sizes[-1:]
+
+
+def piece_shapes(width, blocks, columns):
+    return [pltpu.VMEM((2, size, columns), jnp.bfloat16) for size in piece_sizes(width, blocks)]
+
+
+def chunk_weights(flat, key_flat, value_flat, blocks, start, count):
+    vmem = pl.BlockSpec(memory_space=pltpu.VMEM)
+    shapes = piece_shapes(flat.shape[0], blocks, count * DN)
+    return pl.pallas_call(
+        functools.partial(weights_body, start=start * DN),
+        in_specs=[vmem] * 3,
+        out_specs=[vmem] * len(shapes),
+        out_shape=shapes,
+        compiler_params=pltpu.CompilerParams(vmem_limit_bytes=VMEM_LIMIT),
+        name="weights",
+    )(*[in_vmem(a) for a in (flat, key_flat, value_flat)])
 
 
 def in_vmem(array):
@@ -206,37 +261,25 @@
     )(place, *operands)
 
 
-def chunk_grads(place, order, latents, ropes, loaded, prior, query_grad, pieces, *, start, count,
-                chunk_heads, first_head, final):
+def all_grads(place, order, latents, ropes, loaded):
     ctx_size = len(latents) + 1
     rows, width = loaded[0].shape
-    blocks = order.shape[0]
-    smem = pl.BlockSpec(memory_space=pltpu.SMEM)
-    vmem = pl.BlockSpec(memory_space=pltpu.VMEM)
-    buffers = ([] if query_grad is None else [query_grad]) + list(pieces)
-    operands = [*latents, *ropes, *loaded] + ([] if prior is None else [prior]) + buffers
-    operands = [in_vmem(a) for a in operands]
-    sizes = [width >> (s + 1) for s in range(blocks.bit_length() - 1)]
-    sizes.append(sizes[-1])
-    if final:
-        totals = [pltpu.VMEM((rows, width + DR), jnp.bfloat16)] * ctx_size
-    else:
-        totals = [pltpu.VMEM((ctx_size * rows, width + DR), jnp.float32)]
-    first_buffer = 2 + len(operands) - len(buffers)
+    head_count = loaded[4].shape[0]
+    spread = pltpu.VMEM((ctx_size * rows, head_count * DN), jnp.bfloat16)
+    total = pltpu.VMEM((rows + DR * rows // width, width), jnp.bfloat16)
+    flat = pltpu.VMEM((width, ctx_size * rows), jnp.bfloat16)
+    operands = [in_vmem(a) for a in (order, *latents, *ropes, *loaded)]
+    vmem = pl.BlockSpec(memory_space=pltpu.VMEM)
     outs = pl.pallas_call(
-        functools.partial(grads_body, ctx_size=ctx_size, start=start, count=count,
-                          first_col=(start - first_head) * DN, group=math.gcd(count, GROUP),
-                          has_prior=prior is not None, aliased=len(buffers), final=final,
-                          pieces=len(sizes)),
-        in_specs=[smem] + [vmem] * (1 + len(operands)),
-        out_specs=[vmem] * (1 + len(sizes) + len(totals)),
-        out_shape=[pltpu.VMEM(loaded[2].shape, jnp.bfloat16)]
-        + [pltpu.VMEM((2, size, chunk_heads * DN), jnp.bfloat16) for size in sizes] + totals,
-        input_output_aliases={first_buffer + k: k for k in range(len(buffers))},
+        functools.partial(grads_body, ctx_size=ctx_size, group=math.gcd(head_count, GROUP)),
+        in_specs=[pl.BlockSpec(memory_space=pltpu.SMEM)] + [vmem] * len(operands),
+        out_specs=[vmem] * (4 + ctx_size),
+        out_shape=[pltpu.VMEM(loaded[2].shape, jnp.bfloat16), spread, spread, flat]
+        + [total] * ctx_size,
         compiler_params=pltpu.CompilerParams(vmem_limit_bytes=VMEM_LIMIT),
         name="grads",
-    )(place, order, *operands)
-    return outs[0], outs[1:1 + len(sizes)], outs[1 + len(sizes):]
+    )(place, *operands)
+    return outs[0], outs[1], outs[2], outs[3], outs[4:]
 
 
 def piece_sum(refs, offsets, size):
@@ -250,14 +293,38 @@
     refs[-1][...] = piece_sum(refs[:-1], offsets, refs[0].shape[1])
 
 
+def finish_body(mine_ref, other_ref, latent_out, rope_out):
+    rows = latent_out.shape[0]
+    total = mine_ref[...].astype(jnp.float32) + other_ref[...].astype(jnp.float32)
+    latent_out[...] = total[:rows]
+    extra = total.shape[0] - rows
+    for k in range(rope_out.shape[0] // extra):
+        rope_out[k * extra:(k + 1) * extra, :] = total[rows:, k * rows:(k + 1) * rows]
+
+
+def finish(mine, other, rows):
+    width = mine.shape[1]
+    vmem = pl.BlockSpec(memory_space=pltpu.VMEM)
+    return pl.pallas_call(
+        finish_body,
+        in_specs=[vmem] * 2,
+        out_specs=[vmem] * 2,
+        out_shape=[jax.ShapeDtypeStruct((rows, width), jnp.float32),
+                   jax.ShapeDtypeStruct((DR, rows), jnp.float32)],
+        compiler_params=pltpu.CompilerParams(vmem_limit_bytes=ADD_LIMIT),
+        name="finish",
+    )(in_vmem(mine), in_vmem(other))
+
+
 def last_body(*refs):
     *refs, uk_ref, uv_ref = refs
-    width = refs[0].shape[2]
-    for chunk in range(len(refs) // 2):
-        keep_ref, arrival_ref = refs[2 * chunk:2 * chunk + 2]
+    first = 0
+    for keep_ref, arrival_ref in zip(refs[::2], refs[1::2]):
         total = piece_sum((keep_ref, arrival_ref), (0,), keep_ref.shape[1])
-        uk_ref[:, chunk * width:(chunk + 1) * width] = total[0]
-        uv_ref[:, chunk * width:(chunk + 1) * width] = total[1]
+        width = keep_ref.shape[2]
+        uk_ref[:, first:first + width] = total[0]
+        uv_ref[:, first:first + width] = total[1]
+        first += width
 
 
 def piece_offsets(pieces, stage):
@@ -280,9 +347,9 @@
 
 def last_sums(keeps, arrivals):
     operands = [in_vmem(a) for pair in zip(keeps, arrivals) for a in pair]
-    _, size, width = keeps[0].shape
-    vmem = pl.BlockSpec(memory_space=pltpu.VMEM)
-    out = jax.ShapeDtypeStruct((size, width * len(keeps)), jnp.bfloat16)
+    size = keeps[0].shape[1]
+    vmem = pl.BlockSpec(memory_space=pltpu.VMEM)
+    out = jax.ShapeDtypeStruct((size, sum(k.shape[2] for k in keeps)), jnp.bfloat16)
     return pl.pallas_call(
         last_body,
         in_specs=[vmem] * len(operands),
@@ -291,14 +358,6 @@
         compiler_params=pltpu.CompilerParams(vmem_limit_bytes=ADD_LIMIT),
         name="last",
     )(*operands)
-
-
-def kernel_plan(head_count):
-    groups = head_count // math.gcd(head_count, GROUP)
-    if groups % 4:
-        return [(0, head_count, 0)]
-    half = head_count // 2
-    return [(0, half, 0), (half, half // 2, 1), (half + half // 2, half // 2, 1)]
 
 
 def shifted(value, axis, steps):
@@ -318,26 +377,25 @@
     ropes = [shifted(rope_cols, "ctx", -s) for s in range(1, ctx_size)]
     loaded = load(place, positions.reshape(ctx_size, 1, rows), order, latent[0], rope_cols, query[0],
                   grad_out[0], attn_out[0], lse[0], w_uk, w_uv)
-    plan = kernel_plan(lse.shape[1])
-    chunks = plan[-1][2] + 1
-    chunk_heads = lse.shape[1] // chunks
-    prior = query_grad = None
-    chunk_pieces = [()] * chunks
-    for number, (start, count, chunk) in enumerate(plan):
-        query_grad, pieces, totals = chunk_grads(
-            place, order, latents, ropes, loaded, prior, query_grad, chunk_pieces[chunk],
-            start=start, count=count, chunk_heads=chunk_heads, first_head=chunk * chunk_heads,
-            final=number + 1 == len(plan),
-        )
-        prior = totals[0]
-        chunk_pieces[chunk] = pieces
+    query_grad, key_flat, value_flat, flat, totals = all_grads(place, order, latents, ropes, loaded)
+    head_count = lse.shape[1]
+    quarter = head_count // 4
+    last = quarter // 2
+    counts = [quarter, head_count - quarter - last, last] if quarter >= GROUP else [head_count]
+    chunk_pieces = []
+    for chunk, count in enumerate(counts):
+        chunk_pieces.append(chunk_weights(flat, key_flat, value_flat, dp_size * ctx_size,
+                                          sum(counts[:chunk]), count))
+    query_grad = store(query_grad)
     summed = totals[0].astype(jnp.float32)
     for s in range(1, ctx_size):
         summed = summed + shifted(totals[s], "ctx", s).astype(jnp.float32)
+    mine, other = summed.astype(jnp.bfloat16), jnp.zeros(summed.shape, jnp.bfloat16)
     for bit in bits_of(head_size):
         mine = summed.astype(jnp.bfloat16)
         other = lax.ppermute(mine, "head", [(s, s ^ bit) for s in range(head_size)])
         summed = mine.astype(jnp.float32) + other.astype(jnp.float32)
+    grad_latent, grad_rope = finish(mine, other, rows)
     keeps = []
     lasts = []
     for pieces in chunk_pieces:
@@ -351,8 +409,8 @@
     weight_uk, weight_uv = last_sums(keeps, lasts)
     return (
         query_grad[None],
-        summed[None, :, :width],
-        summed[None, :, width:],
+        grad_latent[None],
+        grad_rope.T[None],
         weight_uk,
         weight_uv,
     )

time: 53.3 us -> 49.6 us (0.931)
  the two profiles are of different devices: /device:TPU:0 before, /device:TPU:1 now
where the time goes in v4:
time: 49.6 us; the launch traced here: 49.5 us
  starting transfers between devices  16.7 us (34%)
  Pallas kernels  16.5 us (33%)
  waiting for transfers between devices  15.4 us (31%)
  between operations  0.77 us (2%)
    ppermute x9, starting transfers between devices, on_device(): arrivals.append(lax.ppermute(value, ('dp', 'ctx'), pairs))  9.23 us
    ppermute x3, waiting for transfers between devices, shifted(): lax.ppermute(value, axis, [(s, (s + steps) % count) for s in range(count)])  8.22 us
    pallas_call x1, Pallas kernels, all_grads(): pl.pallas_call(functools.partial(grads_body, ctx_size=ctx_size, group=mat...  7.51 us
    ppermute x9, waiting for transfers between devices, on_device(): arrivals.append(lax.ppermute(value, ('dp', 'ctx'), pairs))  7.17 us
    ppermute x2, starting transfers between devices, on_device(): other = lax.ppermute(mine, 'head', [(s, s ^ bit) for s in range(head_size)])  3.99 us
    pallas_call x1, Pallas kernels, load(): pl.pallas_call(functools.partial(load_body, ctx_size=ctx_size), in_specs=...  3.78 us
    ppermute x3, starting transfers between devices, shifted(): lax.ppermute(value, axis, [(s, (s + steps) % count) for s in range(count)])  3.43 us
    pallas_call x3, Pallas kernels, chunk_weights(): pl.pallas_call(functools.partial(weights_body, start=start * DN), in_spec...  2 us
  transfers between devices with their start and end apart: 14, of which 5 were waited for; matrix products, arithmetic and copies ran while one was open for 0% of the time, Pallas kernels for 14%

profile of v4, /device:TPU:1, one launch (start us, length us, event | category | flops | bytes accessed | tf_op | source)
XLA Modules:
  0.0 49.5 jit_solution(5612250907579211035)
XLA Ops:
  0.6 2.1 %collective-permute-start = (bf16[128,512]{1,0:T(8,128)(2,1)}, bf16[128,512]{1,0:T(8,128)(2,1)S(1)}, u32[]{:S(2)}, u32[]{:S(2)}) collective-permute-start(bf16[128,512]{1,0:T(8,128)(2,1)} %bitcast.20), channel_id=1, source_target_pairs={{0,4},{4,0},{1,5},{5,1},{2,6},{6,2},{3,7},{7,3},{8,12},{12,8},{9,1... | collective-permute-start | bytes 393224 | tf_op jit(solution)/shard_map/ppermute | solution.py:365
  2.8 0.1 collective-permute-start.1
  2.8 0.1 pad_add_fusion.place_ref
  2.9 3.8 %load.1 = (bf16[128,512]{1,0:T(8,128)(2,1)S(1)}, bf16[64,128]{1,0:T(8,128)(2,1)S(1)}, bf16[128,3072]{1,0:T(8,128)(2,1)S(1)}, bf16[128,2048]{1,0:T(8,128)(2,1)S(1...) custom-call(s32[2]{0:T(128)S(1)} %pad_add_fusion.place_ref, ...), custom_call_target="tpu_custom_call" | custom-call | tf_op jit(solution)/shard_map/load/pallas_call | solution.py:252
  6.7 7.5 %grads.1 = (bf16[128,3072]{1,0:T(8,128)(2,1)S(1)}, bf16[256,2048]{1,0:T(8,128)(2,1)S(1)}, bf16[256,2048]{1,0:T(8,128)(2,1)S(1)}, bf16[512,256]{1,0:T(8,128)(2,1)...) custom-call(s32[2]{0:T(128)S(1)} %pad_add_fusion.place_ref, s32[8,1,512]{2,1,0:T(1,128)S(1)} %copy-done, ...), custom_call_target="tpu_custom_call" | custom-call | tf_op jit(solution)/shard_map/grads/pallas_call | solution.py:273
  14.3 1.2 %weights.4 = (bf16[2,256,1280]{2,1,0:T(8,128)(2,1)S(1)}, bf16[2,128,1280]{2,1,0:T(8,128)(2,1)S(1)}, bf16[2,64,1280]{2,1,0:T(8,128)(2,1)S(1)}, bf16[2,64,1280]{2,1,0:T(8,128)(2,1)S(1)}) custom-call(bf16[512,256]{1,0:T(8,128)(2,1)S(1)} %get-tuple-element.56.flat_ref, bf16[256,2048]{1,0:T(8,128)(2,1)S(1)} %get-tuple-element.57.key_ref, ...), custom_call_target="tpu_custom_call" | custom-call | tf_op jit(solution)/shard_map/weights/pallas_call | solution.py:227
  15.4 1.1 %collective-permute-start.8 = (bf16[2,256,1280]{2,1,0:T(8,128)(2,1)S(1)}, bf16[2,256,1280]{2,1,0:T(8,128)(2,1)S(1)}, u32[]{:S(2)}, u32[]{:S(2)}) collective-permute-start(bf16[2,256,1280]{2,1,0:T(8,128)(2,1)S(1)} %get-tuple-element.64), channel_id=1, source_target_pairs={{0,8},{4,12},{8,0},{12,4},{16,24},{20,28},{24,16},{28,20},{1,9},{5... | collective-permute-start | bytes 3932168 | tf_op jit(solution)/shard_map/ppermute | solution.py:406
  16.5 2.7 %collective-permute-done.8.refs_1_ = bf16[2,256,1280]{2,1,0:T(8,128)(2,1)S(1)} collective-permute-done((bf16[2,256,1280]{2,1,0:T(8,128)(2,1)S(1)}, bf16[2,256,1280]{2,1,0:T(8,128)(2,1)S(1)}, u32[]{:S(2)}, u32[]{:S(2)}) %collective-permute-start.8) | collective-permute-done | bytes 1310752 | tf_op jit(solution)/shard_map/ppermute | solution.py:406
  19.2 0.2 add.28
  19.3 1.6 %collective-permute-start.9 = (bf16[2,128,1280]{2,1,0:T(8,128)(2,1)S(1)}, bf16[2,128,1280]{2,1,0:T(8,128)(2,1)S(1)}, u32[]{:S(2)}, u32[]{:S(2)}) collective-permute-start(bf16[2,128,1280]{2,1,0:T(8,128)(2,1)S(1)} %add.28), channel_id=1, source_target_pairs={{0,16},{4,20},{8,12},{12,8},{16,0},{20,4},{24,28},{28,24},{1,17},{... | collective-permute-start | bytes 1966088 | tf_op jit(solution)/shard_map/ppermute | solution.py:406
  21.0 0.5 %weights.3 = (bf16[2,256,512]{2,1,0:T(8,128)(2,1)S(1)}, bf16[2,128,512]{2,1,0:T(8,128)(2,1)S(1)}, bf16[2,64,512]{2,1,0:T(8,128)(2,1)S(1)}, bf16[2,64,512]{2,1,0:T(8,128)(2,1)S(1)}) custom-call(bf16[512,256]{1,0:T(8,128)(2,1)S(1)} %get-tuple-element.56.flat_ref, bf16[256,2048]{1,0:T(8,128)(2,1)S(1)} %get-tuple-element.57.key_ref, ...), custom_call_target="tpu_custom_call" | custom-call | tf_op jit(solution)/shard_map/weights/pallas_call | solution.py:227
  21.5 0.7 %collective-permute-start.5 = (bf16[2,256,512]{2,1,0:T(8,128)(2,1)S(1)}, bf16[2,256,512]{2,1,0:T(8,128)(2,1)S(1)}, u32[]{:S(2)}, u32[]{:S(2)}) collective-permute-start(bf16[2,256,512]{2,1,0:T(8,128)(2,1)S(1)} %get-tuple-element.60), channel_id=1, source_target_pairs={{0,8},{4,12},{8,0},{12,4},{16,24},{20,28},{24,16},{28,20},{1,9},{5... | collective-permute-start | bytes 1572872 | tf_op jit(solution)/shard_map/ppermute | solution.py:406
  22.2 1.2 %collective-permute-start.2 = (bf16[144,512]{1,0:T(8,128)(2,1)S(1)}, bf16[144,512]{1,0:T(8,128)(2,1)S(1)}, u32[]{:S(2)}, u32[]{:S(2)}) collective-permute-start(bf16[144,512]{1,0:T(8,128)(2,1)S(1)} %get-tuple-element.53), channel_id=1, source_target_pairs={{0,4},{4,0},{1,5},{5,1},{2,6},{6,2},{3,7},{7,3},{8,12},{12,8},{9,1... | collective-permute-start | bytes 442376 | tf_op jit(solution)/shard_map/ppermute | solution.py:365
  23.5 0.3 weights.5
  23.8 0.4 collective-permute-start.11
  24.2 8.2 %collective-permute-done.2 = bf16[144,512]{1,0:T(8,128)(2,1)S(1)} collective-permute-done((bf16[144,512]{1,0:T(8,128)(2,1)S(1)}, bf16[144,512]{1,0:T(8,128)(2,1)S(1)}, u32[]{:S(2)}, u32[]{:S(2)}) %collective-permute-start.2) | collective-permute-done | bytes 147488 | tf_op jit(solution)/shard_map/ppermute | solution.py:365
  32.5 1.6 %collective-permute-start.3 = (bf16[144,512]{1,0:T(8,128)(2,1)S(1)}, bf16[144,512]{1,0:T(8,128)(2,1)S(1)}, u32[]{:S(2)}, u32[]{:S(2)}) collective-permute-start(bf16[144,512]{1,0:T(8,128)(2,1)S(1)} %add_convert_fusion.1), channel_id=1, source_target_pairs={{0,1},{1,0},{2,3},{3,2},{4,5},{5,4},{6,7},{7,6},{8,9},{9,8},{10,11... | collective-permute-start | bytes 442376 | tf_op jit(solution)/shard_map/ppermute | solution.py:396
  34.1 0.1 add.25
  34.1 1.3 %collective-permute-start.6 = (bf16[2,128,512]{2,1,0:T(8,128)(2,1)S(1)}, bf16[2,128,512]{2,1,0:T(8,128)(2,1)S(1)}, u32[]{:S(2)}, u32[]{:S(2)}) collective-permute-start(bf16[2,128,512]{2,1,0:T(8,128)(2,1)S(1)} %add.25), channel_id=1, source_target_pairs={{0,16},{4,20},{8,12},{12,8},{16,0},{20,4},{24,28},{28,24},{1,17},{... | collective-permute-start | bytes 786440 | tf_op jit(solution)/shard_map/ppermute | solution.py:406
  35.5 0.3 collective-permute-start.12
  35.8 0.1 add.30
  35.9 1.3 %collective-permute-start.10 = (bf16[2,64,1280]{2,1,0:T(8,128)(2,1)S(1)}, bf16[2,64,1280]{2,1,0:T(8,128)(2,1)S(1)}, u32[]{:S(2)}, u32[]{:S(2)}) collective-permute-start(bf16[2,64,1280]{2,1,0:T(8,128)(2,1)S(1)} %add.30), channel_id=1, source_target_pairs={{0,4},{4,0},{8,24},{12,28},{16,20},{20,16},{24,8},{28,12},{1,5},{5... | collective-permute-start | bytes 983048 | tf_op jit(solution)/shard_map/ppermute | solution.py:406
  37.2 2.4 %collective-permute-start.4 = (bf16[144,512]{1,0:T(8,128)(2,1)S(1)}, bf16[144,512]{1,0:T(8,128)(2,1)S(1)}, u32[]{:S(2)}, u32[]{:S(2)}) collective-permute-start(bf16[144,512]{1,0:T(8,128)(2,1)S(1)} %add_convert_fusion.mine_ref), channel_id=1, source_target_pairs={{0,2},{1,3},{2,0},{3,1},{4,6},{5,7},{6,4},{7,5},{8,10},{9,11},{10,... | collective-permute-start | bytes 442376 | tf_op jit(solution)/shard_map/ppermute | solution.py:396
  39.6 2.9 %collective-permute-done.6.refs_2_ = bf16[2,128,512]{2,1,0:T(8,128)(2,1)S(1)} collective-permute-done((bf16[2,128,512]{2,1,0:T(8,128)(2,1)S(1)}, bf16[2,128,512]{2,1,0:T(8,128)(2,1)S(1)}, u32[]{:S(2)}, u32[]{:S(2)}) %collective-permute-start.6) | collective-permute-done | bytes 262176 | tf_op jit(solution)/shard_map/ppermute | solution.py:406
  42.6 1.3 %collective-permute-start.7 = (bf16[2,64,512]{2,1,0:T(8,128)(2,1)S(1)}, bf16[2,64,512]{2,1,0:T(8,128)(2,1)S(1)}, u32[]{:S(2)}, u32[]{:S(2)}) collective-permute-start(bf16[2,64,512]{2,1,0:T(8,128)(2,1)S(1)} %add.27), channel_id=1, source_target_pairs={{0,4},{4,0},{8,24},{12,28},{16,20},{20,16},{24,8},{28,12},{1,5},{5... | collective-permute-start | bytes 393224 | tf_op jit(solution)/shard_map/ppermute | solution.py:406
  43.8 1.5 %collective-permute-done.12.refs_2_ = bf16[2,128,256]{2,1,0:T(8,128)(2,1)S(1)} collective-permute-done((bf16[2,128,256]{2,1,0:T(8,128)(2,1)S(1)}, bf16[2,128,256]{2,1,0:T(8,128)(2,1)S(1)}, u32[]{:S(2)}, u32[]{:S(2)}) %collective-permute-start.12) | collective-permute-done | bytes 131104 | tf_op jit(solution)/shard_map/ppermute | solution.py:406
  45.4 1.3 %collective-permute-start.13 = (bf16[2,64,256]{2,1,0:T(8,128)(2,1)S(1)}, bf16[2,64,256]{2,1,0:T(8,128)(2,1)S(1)}, u32[]{:S(2)}, u32[]{:S(2)}) collective-permute-start(bf16[2,64,256]{2,1,0:T(8,128)(2,1)S(1)} %add.33), channel_id=1, source_target_pairs={{0,4},{4,0},{8,24},{12,28},{16,20},{20,16},{24,8},{28,12},{1,5},{5... | collective-permute-start | bytes 196616 | tf_op jit(solution)/shard_map/ppermute | solution.py:406
  46.6 0.9 %store.1 = bf16[128,3072]{1,0:T(8,128)(2,1)} custom-call(bf16[128,3072]{1,0:T(8,128)(2,1)S(1)} %get-tuple-element.51.source_ref), custom_call_target="tpu_custom_call" | custom-call | tf_op jit(solution)/shard_map/store/pallas_call | solution.py:204
  47.6 0.7 %finish.1 = (f32[128,512]{1,0:T(8,128)}, f32[64,128]{1,0:T(8,128)}) custom-call(bf16[144,512]{1,0:T(8,128)(2,1)S(1)} %add_convert_fusion.mine_ref, bf16[144,512]{1,0:T(8,128)(2,1)S(1)} %collective-permute-done.4.other_ref), custom_call_target="tpu_custom_call" | custom-call | tf_op jit(solution)/shard_map/finish/pallas_call | solution.py:308
  48.3 0.1 add.29.refs_2_
  48.5 0.1 collective-permute-done.13.refs_5_
  48.5 0.9 %last.1 = (bf16[64,2048]{1,0:T(8,128)(2,1)}, bf16[64,2048]{1,0:T(8,128)(2,1)}) custom-call(bf16[2,64,512]{2,1,0:T(8,128)(2,1)S(1)} %add.26.refs_0_, bf16[2,64,512]{2,1,0:T(8,128)(2,1)S(1)} %collective-permute-done.7.refs_1_, bf16[2,64,1280]{2,1,0:T(8,128)(2,1)S(1)} %add.29.refs_2_, bf16[2,64,1280]{2,1,0:T(8,128)(2,1)S(1)} %collective-permute-done.10.refs_3_, ...), custom_call_target="tpu_custom_call" | custom-call | tf_op jit(solution)/shard_map/last/pallas_call | solution.py:353
  (18 shorter events, 0.3 us)
Async XLA Ops:
  0.6 6.1 %collective-permute-start = (bf16[128,512]{1,0:T(8,128)(2,1)}, bf16[128,512]{1,0:T(8,128)(2,1)S(1)}, u32[]{:S(2)}, u32[]{:S(2)}) collective-permute-start(bf16[128,512]{1,0:T(8,128)(2,1)} %bitcast.20), channel_id=1, source_target_pairs={{0,4},{4,0},{1,5},{5,1},{2,6},{6,2},{3,7},{7,3},{8,12},{12,8},{9,1... | collective-permute-start | bytes 393224 | tf_op jit(solution)/shard_map/ppermute | solution.py:365
  2.8 4.0 %collective-permute-start.1 = (bf16[64,128]{1,0:T(8,128)(2,1)}, bf16[64,128]{1,0:T(8,128)(2,1)S(1)}, u32[]{:S(2)}, u32[]{:S(2)}) collective-permute-start(bf16[64,128]{1,0:T(8,128)(2,1)} %bitcast.22), channel_id=1, source_target_pairs={{0,4},{4,0},{1,5},{5,1},{2,6},{6,2},{3,7},{7,3},{8,12},{12,8},{9,1... | collective-permute-start | bytes 49160 | tf_op jit(solution)/shard_map/ppermute | solution.py:365
  2.9 3.8 %copy-start = (s32[8,1,512]{2,1,0:T(1,128)S(1)}, s32[8,1,512]{2,1,0:T(1,128)}, u32[]{:S(2)}) copy-start(s32[8,1,512]{2,1,0:T(1,128)} %constant.22.order_ref) | copy-start | bytes 49156
  15.4 3.7 %collective-permute-start.8 = (bf16[2,256,1280]{2,1,0:T(8,128)(2,1)S(1)}, bf16[2,256,1280]{2,1,0:T(8,128)(2,1)S(1)}, u32[]{:S(2)}, u32[]{:S(2)}) collective-permute-start(bf16[2,256,1280]{2,1,0:T(8,128)(2,1)S(1)} %get-tuple-element.64), channel_id=1, source_target_pairs={{0,8},{4,12},{8,0},{12,4},{16,24},{20,28},{24,16},{28,20},{1,9},{5... | collective-permute-start | bytes 3932168 | tf_op jit(solution)/shard_map/ppermute | solution.py:406
  19.3 16.4 %collective-permute-start.9 = (bf16[2,128,1280]{2,1,0:T(8,128)(2,1)S(1)}, bf16[2,128,1280]{2,1,0:T(8,128)(2,1)S(1)}, u32[]{:S(2)}, u32[]{:S(2)}) collective-permute-start(bf16[2,128,1280]{2,1,0:T(8,128)(2,1)S(1)} %add.28), channel_id=1, source_target_pairs={{0,16},{4,20},{8,12},{12,8},{16,0},{20,4},{24,28},{28,24},{1,17},{... | collective-permute-start | bytes 1966088 | tf_op jit(solution)/shard_map/ppermute | solution.py:406
  21.5 12.5 %collective-permute-start.5 = (bf16[2,256,512]{2,1,0:T(8,128)(2,1)S(1)}, bf16[2,256,512]{2,1,0:T(8,128)(2,1)S(1)}, u32[]{:S(2)}, u32[]{:S(2)}) collective-permute-start(bf16[2,256,512]{2,1,0:T(8,128)(2,1)S(1)} %get-tuple-element.60), channel_id=1, source_target_pairs={{0,8},{4,12},{8,0},{12,4},{16,24},{20,28},{24,16},{28,20},{1,9},{5... | collective-permute-start | bytes 1572872 | tf_op jit(solution)/shard_map/ppermute | solution.py:406
  22.2 10.2 %collective-permute-start.2 = (bf16[144,512]{1,0:T(8,128)(2,1)S(1)}, bf16[144,512]{1,0:T(8,128)(2,1)S(1)}, u32[]{:S(2)}, u32[]{:S(2)}) collective-permute-start(bf16[144,512]{1,0:T(8,128)(2,1)S(1)} %get-tuple-element.53), channel_id=1, source_target_pairs={{0,4},{4,0},{1,5},{5,1},{2,6},{6,2},{3,7},{7,3},{8,12},{12,8},{9,1... | collective-permute-start | bytes 442376 | tf_op jit(solution)/shard_map/ppermute | solution.py:365
  23.8 11.7 %collective-permute-start.11 = (bf16[2,256,256]{2,1,0:T(8,128)(2,1)S(1)}, bf16[2,256,256]{2,1,0:T(8,128)(2,1)S(1)}, u32[]{:S(2)}, u32[]{:S(2)}) collective-permute-start(bf16[2,256,256]{2,1,0:T(8,128)(2,1)S(1)} %get-tuple-element.68), channel_id=1, source_target_pairs={{0,8},{4,12},{8,0},{12,4},{16,24},{20,28},{24,16},{28,20},{1,9},{5... | collective-permute-start | bytes 786440 | tf_op jit(solution)/shard_map/ppermute | solution.py:406
  32.5 4.7 %collective-permute-start.3 = (bf16[144,512]{1,0:T(8,128)(2,1)S(1)}, bf16[144,512]{1,0:T(8,128)(2,1)S(1)}, u32[]{:S(2)}, u32[]{:S(2)}) collective-permute-start(bf16[144,512]{1,0:T(8,128)(2,1)S(1)} %add_convert_fusion.1), channel_id=1, source_target_pairs={{0,1},{1,0},{2,3},{3,2},{4,5},{5,4},{6,7},{7,6},{8,9},{9,8},{10,11... | collective-permute-start | bytes 442376 | tf_op jit(solution)/shard_map/ppermute | solution.py:396
  34.1 8.4 %collective-permute-start.6 = (bf16[2,128,512]{2,1,0:T(8,128)(2,1)S(1)}, bf16[2,128,512]{2,1,0:T(8,128)(2,1)S(1)}, u32[]{:S(2)}, u32[]{:S(2)}) collective-permute-start(bf16[2,128,512]{2,1,0:T(8,128)(2,1)S(1)} %add.25), channel_id=1, source_target_pairs={{0,16},{4,20},{8,12},{12,8},{16,0},{20,4},{24,28},{28,24},{1,17},{... | collective-permute-start | bytes 786440 | tf_op jit(solution)/shard_map/ppermute | solution.py:406
  35.5 9.9 %collective-permute-start.12 = (bf16[2,128,256]{2,1,0:T(8,128)(2,1)S(1)}, bf16[2,128,256]{2,1,0:T(8,128)(2,1)S(1)}, u32[]{:S(2)}, u32[]{:S(2)}) collective-permute-start(bf16[2,128,256]{2,1,0:T(8,128)(2,1)S(1)} %add.31), channel_id=1, source_target_pairs={{0,16},{4,20},{8,12},{12,8},{16,0},{20,4},{24,28},{28,24},{1,17},{... | collective-permute-start | bytes 393224 | tf_op jit(solution)/shard_map/ppermute | solution.py:406
  35.9 12.7 %collective-permute-start.10 = (bf16[2,64,1280]{2,1,0:T(8,128)(2,1)S(1)}, bf16[2,64,1280]{2,1,0:T(8,128)(2,1)S(1)}, u32[]{:S(2)}, u32[]{:S(2)}) collective-permute-start(bf16[2,64,1280]{2,1,0:T(8,128)(2,1)S(1)} %add.30), channel_id=1, source_target_pairs={{0,4},{4,0},{8,24},{12,28},{16,20},{20,16},{24,8},{28,12},{1,5},{5... | collective-permute-start | bytes 983048 | tf_op jit(solution)/shard_map/ppermute | solution.py:406
  37.2 10.4 %collective-permute-start.4 = (bf16[144,512]{1,0:T(8,128)(2,1)S(1)}, bf16[144,512]{1,0:T(8,128)(2,1)S(1)}, u32[]{:S(2)}, u32[]{:S(2)}) collective-permute-start(bf16[144,512]{1,0:T(8,128)(2,1)S(1)} %add_convert_fusion.mine_ref), channel_id=1, source_target_pairs={{0,2},{1,3},{2,0},{3,1},{4,6},{5,7},{6,4},{7,5},{8,10},{9,11},{10,... | collective-permute-start | bytes 442376 | tf_op jit(solution)/shard_map/ppermute | solution.py:396
  42.6 6.0 %collective-permute-start.7 = (bf16[2,64,512]{2,1,0:T(8,128)(2,1)S(1)}, bf16[2,64,512]{2,1,0:T(8,128)(2,1)S(1)}, u32[]{:S(2)}, u32[]{:S(2)}) collective-permute-start(bf16[2,64,512]{2,1,0:T(8,128)(2,1)S(1)} %add.27), channel_id=1, source_target_pairs={{0,4},{4,0},{8,24},{12,28},{16,20},{20,16},{24,8},{28,12},{1,5},{5... | collective-permute-start | bytes 393224 | tf_op jit(solution)/shard_map/ppermute | solution.py:406
  45.4 3.2 %collective-permute-start.13 = (bf16[2,64,256]{2,1,0:T(8,128)(2,1)S(1)}, bf16[2,64,256]{2,1,0:T(8,128)(2,1)S(1)}, u32[]{:S(2)}, u32[]{:S(2)}) collective-permute-start(bf16[2,64,256]{2,1,0:T(8,128)(2,1)S(1)} %add.33), channel_id=1, source_target_pairs={{0,4},{4,0},{8,24},{12,28},{16,20},{20,16},{24,8},{28,12},{1,5},{5... | collective-permute-start | bytes 196616 | tf_op jit(solution)/shard_map/ppermute | solution.py:406

commit v5 on v4

--- a/solution.py
+++ b/solution.py
@@ -16,8 +16,9 @@
 DQ = DN + DR
 
 MASKED = -1e30
-GROUP = 4
+GROUP = 8
 VMEM_LIMIT = 6 << 20
+LIMIT_A_TOKEN = 24 << 10
 LOAD_LIMIT = 4 << 20
 ADD_LIMIT = 2 << 20
 NT = (((1,), (1,)), ((), ()))
@@ -143,24 +144,31 @@
         )
         key_grads = []
         value_grads = []
-        for inner in range(group):
-            head = first + inner
-            cols = slice(head * DN, (head + 1) * DN)
-            wide = slice(head * DQ, (head + 1) * DQ)
-            part = slice(inner * DN, (inner + 1) * DN)
-            keys = jnp.concatenate([keys_all[:, part], rope], axis=1)
-            query = query_ref[:, wide]
-            grad = grad_ref[:, cols]
-            delta = delta_ref[head:head + 1, :]
-            lse = lse_ref[head:head + 1, :]
-            weights = jnp.exp(dot_nt(keys, query) * scale - lse + bias)
-            dots = dot_nt(values_all[:, part], grad)
-            score_grad = (weights * (dots - delta) * scale).astype(jnp.bfloat16)
-            dq_ref[:, wide] = dot(score_grad.T, keys).astype(jnp.bfloat16)
-            key_grad = dot(score_grad, query)
-            value_grads.append(dot(weights.astype(jnp.bfloat16), grad).astype(jnp.bfloat16))
-            key_grads.append(key_grad[:, :DN].astype(jnp.bfloat16))
-            rope_total = rope_total + key_grad[:, DN:]
+        stages = []
+        for inner in range(group + 2):
+            if inner < group:
+                head = first + inner
+                cols = slice(head * DN, (head + 1) * DN)
+                wide = slice(head * DQ, (head + 1) * DQ)
+                part = slice(inner * DN, (inner + 1) * DN)
+                keys = jnp.concatenate([keys_all[:, part], rope], axis=1)
+                query = query_ref[:, wide]
+                grad = grad_ref[:, cols]
+                stages.append([head, wide, keys, query, grad, dot_nt(keys, query),
+                               dot_nt(values_all[:, part], grad)])
+            if 0 <= inner - 2:
+                wide, keys, query, grad, score_grad, weights_b = stages[inner - 2]
+                dq_ref[:, wide] = dot(score_grad.T, keys).astype(jnp.bfloat16)
+                key_grad = dot(score_grad, query)
+                value_grads.append(dot(weights_b, grad).astype(jnp.bfloat16))
+                key_grads.append(key_grad[:, :DN].astype(jnp.bfloat16))
+                rope_total = rope_total + key_grad[:, DN:]
+            if 0 <= inner - 1 < group:
+                head, wide, keys, query, grad, scores, dots = stages[inner - 1]
+                weights = jnp.exp(scores * scale - lse_ref[head:head + 1, :] + bias)
+                score_grad = weights * (dots - delta_ref[head:head + 1, :]) * scale
+                stages[inner - 1] = (wide, keys, query, grad, score_grad.astype(jnp.bfloat16),
+                                     weights.astype(jnp.bfloat16))
         key_flat = jnp.concatenate(key_grads, axis=1)
         value_flat = jnp.concatenate(value_grads, axis=1)
         key_out[:, span] = key_flat
@@ -276,7 +284,7 @@
         out_specs=[vmem] * (4 + ctx_size),
         out_shape=[pltpu.VMEM(loaded[2].shape, jnp.bfloat16), spread, spread, flat]
         + [total] * ctx_size,
-        compiler_params=pltpu.CompilerParams(vmem_limit_bytes=VMEM_LIMIT),
+        compiler_params=pltpu.CompilerParams(vmem_limit_bytes=LIMIT_A_TOKEN * ctx_size * rows),
         name="grads",
     )(place, *operands)
     return outs[0], outs[1], outs[2], outs[3], outs[4:]
@@ -381,7 +389,7 @@
     head_count = lse.shape[1]
     quarter = head_count // 4
     last = quarter // 2
-    counts = [quarter, head_count - quarter - last, last] if quarter >= GROUP else [head_count]
+    counts = [quarter, head_count - quarter - last, last] if last else [head_count]
     chunk_pieces = []
     for chunk, count in enumerate(counts):
         chunk_pieces.append(chunk_weights(flat, key_flat, value_flat, dp_size * ctx_size,

time: 49.6 us -> 46.9 us (0.946)
  Pallas kernels: 16.5 us -> 13.8 us
    pallas_call x1, Pallas kernels: 7.51 us -> 4.81 us  [all_grads(): pl.pallas_call(functools.partial(grads_body, ctx_size=ctx_size, group=mat...]
where the time goes in v5:
time: 46.9 us; the launch traced here: 46.7 us
  starting transfers between devices  16.7 us (36%)
  waiting for transfers between devices  15.4 us (33%)
  Pallas kernels  13.8 us (29%)
  between operations  0.76 us (2%)
    ppermute x9, starting transfers between devices, on_device(): arrivals.append(lax.ppermute(value, ('dp', 'ctx'), pairs))  9.24 us
    ppermute x3, waiting for transfers between devices, shifted(): lax.ppermute(value, axis, [(s, (s + steps) % count) for s in range(count)])  8.2 us
    ppermute x9, waiting for transfers between devices, on_device(): arrivals.append(lax.ppermute(value, ('dp', 'ctx'), pairs))  7.17 us
    pallas_call x1, Pallas kernels, all_grads(): pl.pallas_call(functools.partial(grads_body, ctx_size=ctx_size, group=mat...  4.81 us
    ppermute x2, starting transfers between devices, on_device(): other = lax.ppermute(mine, 'head', [(s, s ^ bit) for s in range(head_size)])  3.99 us
    pallas_call x1, Pallas kernels, load(): pl.pallas_call(functools.partial(load_body, ctx_size=ctx_size), in_specs=...  3.78 us
    ppermute x3, starting transfers between devices, shifted(): lax.ppermute(value, axis, [(s, (s + steps) % count) for s in range(count)])  3.44 us
    pallas_call x3, Pallas kernels, chunk_weights(): pl.pallas_call(functools.partial(weights_body, start=start * DN), in_spec...  2 us
  transfers between devices with their start and end apart: 14, of which 5 were waited for; matrix products, arithmetic and copies ran while one was open for 0% of the time, Pallas kernels for 14%

profile of v5, /device:TPU:1, one launch (start us, length us, event | category | flops | bytes accessed | tf_op | source)
XLA Modules:
  0.0 46.7 jit_solution(7085443766968832723)
XLA Ops:
  0.6 2.1 %collective-permute-start = (bf16[128,512]{1,0:T(8,128)(2,1)}, bf16[128,512]{1,0:T(8,128)(2,1)S(1)}, u32[]{:S(2)}, u32[]{:S(2)}) collective-permute-start(bf16[128,512]{1,0:T(8,128)(2,1)} %bitcast.20), channel_id=1, source_target_pairs={{0,4},{4,0},{1,5},{5,1},{2,6},{6,2},{3,7},{7,3},{8,12},{12,8},{9,1... | collective-permute-start | bytes 393224 | tf_op jit(solution)/shard_map/ppermute | solution.py:373
  2.8 0.1 collective-permute-start.1
  2.8 0.1 pad_add_fusion.place_ref
  2.9 3.8 %load.1 = (bf16[128,512]{1,0:T(8,128)(2,1)S(1)}, bf16[64,128]{1,0:T(8,128)(2,1)S(1)}, bf16[128,3072]{1,0:T(8,128)(2,1)S(1)}, bf16[128,2048]{1,0:T(8,128)(2,1)S(1...) custom-call(s32[2]{0:T(128)S(1)} %pad_add_fusion.place_ref, ...), custom_call_target="tpu_custom_call" | custom-call | tf_op jit(solution)/shard_map/load/pallas_call | solution.py:260
  6.7 4.8 %grads.1 = (bf16[128,3072]{1,0:T(8,128)(2,1)S(1)}, bf16[256,2048]{1,0:T(8,128)(2,1)S(1)}, bf16[256,2048]{1,0:T(8,128)(2,1)S(1)}, bf16[512,256]{1,0:T(8,128)(2,1)...) custom-call(s32[2]{0:T(128)S(1)} %pad_add_fusion.place_ref, s32[8,1,512]{2,1,0:T(1,128)S(1)} %copy-done, ...), custom_call_target="tpu_custom_call" | custom-call | tf_op jit(solution)/shard_map/grads/pallas_call | solution.py:281
  11.6 1.2 %weights.4 = (bf16[2,256,1280]{2,1,0:T(8,128)(2,1)S(1)}, bf16[2,128,1280]{2,1,0:T(8,128)(2,1)S(1)}, bf16[2,64,1280]{2,1,0:T(8,128)(2,1)S(1)}, bf16[2,64,1280]{2,1,0:T(8,128)(2,1)S(1)}) custom-call(bf16[512,256]{1,0:T(8,128)(2,1)S(1)} %get-tuple-element.56.flat_ref, bf16[256,2048]{1,0:T(8,128)(2,1)S(1)} %get-tuple-element.57.key_ref, ...), custom_call_target="tpu_custom_call" | custom-call | tf_op jit(solution)/shard_map/weights/pallas_call | solution.py:235
  12.7 1.1 %collective-permute-start.8 = (bf16[2,256,1280]{2,1,0:T(8,128)(2,1)S(1)}, bf16[2,256,1280]{2,1,0:T(8,128)(2,1)S(1)}, u32[]{:S(2)}, u32[]{:S(2)}) collective-permute-start(bf16[2,256,1280]{2,1,0:T(8,128)(2,1)S(1)} %get-tuple-element.64), channel_id=1, source_target_pairs={{0,8},{4,12},{8,0},{12,4},{16,24},{20,28},{24,16},{28,20},{1,9},{5... | collective-permute-start | bytes 3932168 | tf_op jit(solution)/shard_map/ppermute | solution.py:414
  13.8 2.7 %collective-permute-done.8.refs_1_ = bf16[2,256,1280]{2,1,0:T(8,128)(2,1)S(1)} collective-permute-done((bf16[2,256,1280]{2,1,0:T(8,128)(2,1)S(1)}, bf16[2,256,1280]{2,1,0:T(8,128)(2,1)S(1)}, u32[]{:S(2)}, u32[]{:S(2)}) %collective-permute-start.8) | collective-permute-done | bytes 1310752 | tf_op jit(solution)/shard_map/ppermute | solution.py:414
  16.5 0.2 add.28
  16.6 1.6 %collective-permute-start.9 = (bf16[2,128,1280]{2,1,0:T(8,128)(2,1)S(1)}, bf16[2,128,1280]{2,1,0:T(8,128)(2,1)S(1)}, u32[]{:S(2)}, u32[]{:S(2)}) collective-permute-start(bf16[2,128,1280]{2,1,0:T(8,128)(2,1)S(1)} %add.28), channel_id=1, source_target_pairs={{0,16},{4,20},{8,12},{12,8},{16,0},{20,4},{24,28},{28,24},{1,17},{... | collective-permute-start | bytes 1966088 | tf_op jit(solution)/shard_map/ppermute | solution.py:414
  18.3 0.5 %weights.3 = (bf16[2,256,512]{2,1,0:T(8,128)(2,1)S(1)}, bf16[2,128,512]{2,1,0:T(8,128)(2,1)S(1)}, bf16[2,64,512]{2,1,0:T(8,128)(2,1)S(1)}, bf16[2,64,512]{2,1,0:T(8,128)(2,1)S(1)}) custom-call(bf16[512,256]{1,0:T(8,128)(2,1)S(1)} %get-tuple-element.56.flat_ref, bf16[256,2048]{1,0:T(8,128)(2,1)S(1)} %get-tuple-element.57.key_ref, ...), custom_call_target="tpu_custom_call" | custom-call | tf_op jit(solution)/shard_map/weights/pallas_call | solution.py:235
  18.8 0.7 %collective-permute-start.5 = (bf16[2,256,512]{2,1,0:T(8,128)(2,1)S(1)}, bf16[2,256,512]{2,1,0:T(8,128)(2,1)S(1)}, u32[]{:S(2)}, u32[]{:S(2)}) collective-permute-start(bf16[2,256,512]{2,1,0:T(8,128)(2,1)S(1)} %get-tuple-element.60), channel_id=1, source_target_pairs={{0,8},{4,12},{8,0},{12,4},{16,24},{20,28},{24,16},{28,20},{1,9},{5... | collective-permute-start | bytes 1572872 | tf_op jit(solution)/shard_map/ppermute | solution.py:414
  19.5 1.2 %collective-permute-start.2 = (bf16[144,512]{1,0:T(8,128)(2,1)S(1)}, bf16[144,512]{1,0:T(8,128)(2,1)S(1)}, u32[]{:S(2)}, u32[]{:S(2)}) collective-permute-start(bf16[144,512]{1,0:T(8,128)(2,1)S(1)} %get-tuple-element.53), channel_id=1, source_target_pairs={{0,4},{4,0},{1,5},{5,1},{2,6},{6,2},{3,7},{7,3},{8,12},{12,8},{9,1... | collective-permute-start | bytes 442376 | tf_op jit(solution)/shard_map/ppermute | solution.py:373
  20.8 0.3 weights.5
  21.1 0.4 collective-permute-start.11
  21.5 8.2 %collective-permute-done.2 = bf16[144,512]{1,0:T(8,128)(2,1)S(1)} collective-permute-done((bf16[144,512]{1,0:T(8,128)(2,1)S(1)}, bf16[144,512]{1,0:T(8,128)(2,1)S(1)}, u32[]{:S(2)}, u32[]{:S(2)}) %collective-permute-start.2) | collective-permute-done | bytes 147488 | tf_op jit(solution)/shard_map/ppermute | solution.py:373
  29.8 1.6 %collective-permute-start.3 = (bf16[144,512]{1,0:T(8,128)(2,1)S(1)}, bf16[144,512]{1,0:T(8,128)(2,1)S(1)}, u32[]{:S(2)}, u32[]{:S(2)}) collective-permute-start(bf16[144,512]{1,0:T(8,128)(2,1)S(1)} %add_convert_fusion.1), channel_id=1, source_target_pairs={{0,1},{1,0},{2,3},{3,2},{4,5},{5,4},{6,7},{7,6},{8,9},{9,8},{10,11... | collective-permute-start | bytes 442376 | tf_op jit(solution)/shard_map/ppermute | solution.py:404
  31.4 0.1 add.25
  31.4 1.3 %collective-permute-start.6 = (bf16[2,128,512]{2,1,0:T(8,128)(2,1)S(1)}, bf16[2,128,512]{2,1,0:T(8,128)(2,1)S(1)}, u32[]{:S(2)}, u32[]{:S(2)}) collective-permute-start(bf16[2,128,512]{2,1,0:T(8,128)(2,1)S(1)} %add.25), channel_id=1, source_target_pairs={{0,16},{4,20},{8,12},{12,8},{16,0},{20,4},{24,28},{28,24},{1,17},{... | collective-permute-start | bytes 786440 | tf_op jit(solution)/shard_map/ppermute | solution.py:414
  32.8 0.3 collective-permute-start.12
  33.1 0.1 add.30
  33.2 1.3 %collective-permute-start.10 = (bf16[2,64,1280]{2,1,0:T(8,128)(2,1)S(1)}, bf16[2,64,1280]{2,1,0:T(8,128)(2,1)S(1)}, u32[]{:S(2)}, u32[]{:S(2)}) collective-permute-start(bf16[2,64,1280]{2,1,0:T(8,128)(2,1)S(1)} %add.30), channel_id=1, source_target_pairs={{0,4},{4,0},{8,24},{12,28},{16,20},{20,16},{24,8},{28,12},{1,5},{5... | collective-permute-start | bytes 983048 | tf_op jit(solution)/shard_map/ppermute | solution.py:414
  34.5 2.4 %collective-permute-start.4 = (bf16[144,512]{1,0:T(8,128)(2,1)S(1)}, bf16[144,512]{1,0:T(8,128)(2,1)S(1)}, u32[]{:S(2)}, u32[]{:S(2)}) collective-permute-start(bf16[144,512]{1,0:T(8,128)(2,1)S(1)} %add_convert_fusion.mine_ref), channel_id=1, source_target_pairs={{0,2},{1,3},{2,0},{3,1},{4,6},{5,7},{6,4},{7,5},{8,10},{9,11},{10,... | collective-permute-start | bytes 442376 | tf_op jit(solution)/shard_map/ppermute | solution.py:404
  36.9 2.9 %collective-permute-done.6.refs_2_ = bf16[2,128,512]{2,1,0:T(8,128)(2,1)S(1)} collective-permute-done((bf16[2,128,512]{2,1,0:T(8,128)(2,1)S(1)}, bf16[2,128,512]{2,1,0:T(8,128)(2,1)S(1)}, u32[]{:S(2)}, u32[]{:S(2)}) %collective-permute-start.6) | collective-permute-done | bytes 262176 | tf_op jit(solution)/shard_map/ppermute | solution.py:414
  39.9 1.3 %collective-permute-start.7 = (bf16[2,64,512]{2,1,0:T(8,128)(2,1)S(1)}, bf16[2,64,512]{2,1,0:T(8,128)(2,1)S(1)}, u32[]{:S(2)}, u32[]{:S(2)}) collective-permute-start(bf16[2,64,512]{2,1,0:T(8,128)(2,1)S(1)} %add.27), channel_id=1, source_target_pairs={{0,4},{4,0},{8,24},{12,28},{16,20},{20,16},{24,8},{28,12},{1,5},{5... | collective-permute-start | bytes 393224 | tf_op jit(solution)/shard_map/ppermute | solution.py:414
  41.1 1.5 %collective-permute-done.12.refs_2_ = bf16[2,128,256]{2,1,0:T(8,128)(2,1)S(1)} collective-permute-done((bf16[2,128,256]{2,1,0:T(8,128)(2,1)S(1)}, bf16[2,128,256]{2,1,0:T(8,128)(2,1)S(1)}, u32[]{:S(2)}, u32[]{:S(2)}) %collective-permute-start.12) | collective-permute-done | bytes 131104 | tf_op jit(solution)/shard_map/ppermute | solution.py:414
  42.7 1.3 %collective-permute-start.13 = (bf16[2,64,256]{2,1,0:T(8,128)(2,1)S(1)}, bf16[2,64,256]{2,1,0:T(8,128)(2,1)S(1)}, u32[]{:S(2)}, u32[]{:S(2)}) collective-permute-start(bf16[2,64,256]{2,1,0:T(8,128)(2,1)S(1)} %add.33), channel_id=1, source_target_pairs={{0,4},{4,0},{8,24},{12,28},{16,20},{20,16},{24,8},{28,12},{1,5},{5... | collective-permute-start | bytes 196616 | tf_op jit(solution)/shard_map/ppermute | solution.py:414
  43.9 0.9 %store.1 = bf16[128,3072]{1,0:T(8,128)(2,1)} custom-call(bf16[128,3072]{1,0:T(8,128)(2,1)S(1)} %get-tuple-element.51.source_ref), custom_call_target="tpu_custom_call" | custom-call | tf_op jit(solution)/shard_map/store/pallas_call | solution.py:212
  44.9 0.7 %finish.1 = (f32[128,512]{1,0:T(8,128)}, f32[64,128]{1,0:T(8,128)}) custom-call(bf16[144,512]{1,0:T(8,128)(2,1)S(1)} %add_convert_fusion.mine_ref, bf16[144,512]{1,0:T(8,128)(2,1)S(1)} %collective-permute-done.4.other_ref), custom_call_target="tpu_custom_call" | custom-call | tf_op jit(solution)/shard_map/finish/pallas_call | solution.py:316
  45.6 0.1 add.29.refs_2_
  45.8 0.1 collective-permute-done.13.refs_5_
  45.8 0.9 %last.1 = (bf16[64,2048]{1,0:T(8,128)(2,1)}, bf16[64,2048]{1,0:T(8,128)(2,1)}) custom-call(bf16[2,64,512]{2,1,0:T(8,128)(2,1)S(1)} %add.26.refs_0_, bf16[2,64,512]{2,1,0:T(8,128)(2,1)S(1)} %collective-permute-done.7.refs_1_, bf16[2,64,1280]{2,1,0:T(8,128)(2,1)S(1)} %add.29.refs_2_, bf16[2,64,1280]{2,1,0:T(8,128)(2,1)S(1)} %collective-permute-done.10.refs_3_, ...), custom_call_target="tpu_custom_call" | custom-call | tf_op jit(solution)/shard_map/last/pallas_call | solution.py:361
  (18 shorter events, 0.3 us)
Async XLA Ops:
  0.6 6.1 %collective-permute-start = (bf16[128,512]{1,0:T(8,128)(2,1)}, bf16[128,512]{1,0:T(8,128)(2,1)S(1)}, u32[]{:S(2)}, u32[]{:S(2)}) collective-permute-start(bf16[128,512]{1,0:T(8,128)(2,1)} %bitcast.20), channel_id=1, source_target_pairs={{0,4},{4,0},{1,5},{5,1},{2,6},{6,2},{3,7},{7,3},{8,12},{12,8},{9,1... | collective-permute-start | bytes 393224 | tf_op jit(solution)/shard_map/ppermute | solution.py:373
  2.8 4.0 %collective-permute-start.1 = (bf16[64,128]{1,0:T(8,128)(2,1)}, bf16[64,128]{1,0:T(8,128)(2,1)S(1)}, u32[]{:S(2)}, u32[]{:S(2)}) collective-permute-start(bf16[64,128]{1,0:T(8,128)(2,1)} %bitcast.22), channel_id=1, source_target_pairs={{0,4},{4,0},{1,5},{5,1},{2,6},{6,2},{3,7},{7,3},{8,12},{12,8},{9,1... | collective-permute-start | bytes 49160 | tf_op jit(solution)/shard_map/ppermute | solution.py:373
  2.9 3.8 %copy-start = (s32[8,1,512]{2,1,0:T(1,128)S(1)}, s32[8,1,512]{2,1,0:T(1,128)}, u32[]{:S(2)}) copy-start(s32[8,1,512]{2,1,0:T(1,128)} %constant.22.order_ref) | copy-start | bytes 49156
  12.7 3.7 %collective-permute-start.8 = (bf16[2,256,1280]{2,1,0:T(8,128)(2,1)S(1)}, bf16[2,256,1280]{2,1,0:T(8,128)(2,1)S(1)}, u32[]{:S(2)}, u32[]{:S(2)}) collective-permute-start(bf16[2,256,1280]{2,1,0:T(8,128)(2,1)S(1)} %get-tuple-element.64), channel_id=1, source_target_pairs={{0,8},{4,12},{8,0},{12,4},{16,24},{20,28},{24,16},{28,20},{1,9},{5... | collective-permute-start | bytes 3932168 | tf_op jit(solution)/shard_map/ppermute | solution.py:414
  16.6 16.4 %collective-permute-start.9 = (bf16[2,128,1280]{2,1,0:T(8,128)(2,1)S(1)}, bf16[2,128,1280]{2,1,0:T(8,128)(2,1)S(1)}, u32[]{:S(2)}, u32[]{:S(2)}) collective-permute-start(bf16[2,128,1280]{2,1,0:T(8,128)(2,1)S(1)} %add.28), channel_id=1, source_target_pairs={{0,16},{4,20},{8,12},{12,8},{16,0},{20,4},{24,28},{28,24},{1,17},{... | collective-permute-start | bytes 1966088 | tf_op jit(solution)/shard_map/ppermute | solution.py:414
  18.8 12.5 %collective-permute-start.5 = (bf16[2,256,512]{2,1,0:T(8,128)(2,1)S(1)}, bf16[2,256,512]{2,1,0:T(8,128)(2,1)S(1)}, u32[]{:S(2)}, u32[]{:S(2)}) collective-permute-start(bf16[2,256,512]{2,1,0:T(8,128)(2,1)S(1)} %get-tuple-element.60), channel_id=1, source_target_pairs={{0,8},{4,12},{8,0},{12,4},{16,24},{20,28},{24,16},{28,20},{1,9},{5... | collective-permute-start | bytes 1572872 | tf_op jit(solution)/shard_map/ppermute | solution.py:414
  19.5 10.2 %collective-permute-start.2 = (bf16[144,512]{1,0:T(8,128)(2,1)S(1)}, bf16[144,512]{1,0:T(8,128)(2,1)S(1)}, u32[]{:S(2)}, u32[]{:S(2)}) collective-permute-start(bf16[144,512]{1,0:T(8,128)(2,1)S(1)} %get-tuple-element.53), channel_id=1, source_target_pairs={{0,4},{4,0},{1,5},{5,1},{2,6},{6,2},{3,7},{7,3},{8,12},{12,8},{9,1... | collective-permute-start | bytes 442376 | tf_op jit(solution)/shard_map/ppermute | solution.py:373
  21.1 11.6 %collective-permute-start.11 = (bf16[2,256,256]{2,1,0:T(8,128)(2,1)S(1)}, bf16[2,256,256]{2,1,0:T(8,128)(2,1)S(1)}, u32[]{:S(2)}, u32[]{:S(2)}) collective-permute-start(bf16[2,256,256]{2,1,0:T(8,128)(2,1)S(1)} %get-tuple-element.68), channel_id=1, source_target_pairs={{0,8},{4,12},{8,0},{12,4},{16,24},{20,28},{24,16},{28,20},{1,9},{5... | collective-permute-start | bytes 786440 | tf_op jit(solution)/shard_map/ppermute | solution.py:414
  29.8 4.7 %collective-permute-start.3 = (bf16[144,512]{1,0:T(8,128)(2,1)S(1)}, bf16[144,512]{1,0:T(8,128)(2,1)S(1)}, u32[]{:S(2)}, u32[]{:S(2)}) collective-permute-start(bf16[144,512]{1,0:T(8,128)(2,1)S(1)} %add_convert_fusion.1), channel_id=1, source_target_pairs={{0,1},{1,0},{2,3},{3,2},{4,5},{5,4},{6,7},{7,6},{8,9},{9,8},{10,11... | collective-permute-start | bytes 442376 | tf_op jit(solution)/shard_map/ppermute | solution.py:404
  31.4 8.4 %collective-permute-start.6 = (bf16[2,128,512]{2,1,0:T(8,128)(2,1)S(1)}, bf16[2,128,512]{2,1,0:T(8,128)(2,1)S(1)}, u32[]{:S(2)}, u32[]{:S(2)}) collective-permute-start(bf16[2,128,512]{2,1,0:T(8,128)(2,1)S(1)} %add.25), channel_id=1, source_target_pairs={{0,16},{4,20},{8,12},{12,8},{16,0},{20,4},{24,28},{28,24},{1,17},{... | collective-permute-start | bytes 786440 | tf_op jit(solution)/shard_map/ppermute | solution.py:414
  32.8 9.9 %collective-permute-start.12 = (bf16[2,128,256]{2,1,0:T(8,128)(2,1)S(1)}, bf16[2,128,256]{2,1,0:T(8,128)(2,1)S(1)}, u32[]{:S(2)}, u32[]{:S(2)}) collective-permute-start(bf16[2,128,256]{2,1,0:T(8,128)(2,1)S(1)} %add.31), channel_id=1, source_target_pairs={{0,16},{4,20},{8,12},{12,8},{16,0},{20,4},{24,28},{28,24},{1,17},{... | collective-permute-start | bytes 393224 | tf_op jit(solution)/shard_map/ppermute | solution.py:414
  33.2 12.7 %collective-permute-start.10 = (bf16[2,64,1280]{2,1,0:T(8,128)(2,1)S(1)}, bf16[2,64,1280]{2,1,0:T(8,128)(2,1)S(1)}, u32[]{:S(2)}, u32[]{:S(2)}) collective-permute-start(bf16[2,64,1280]{2,1,0:T(8,128)(2,1)S(1)} %add.30), channel_id=1, source_target_pairs={{0,4},{4,0},{8,24},{12,28},{16,20},{20,16},{24,8},{28,12},{1,5},{5... | collective-permute-start | bytes 983048 | tf_op jit(solution)/shard_map/ppermute | solution.py:414
  34.5 10.4 %collective-permute-start.4 = (bf16[144,512]{1,0:T(8,128)(2,1)S(1)}, bf16[144,512]{1,0:T(8,128)(2,1)S(1)}, u32[]{:S(2)}, u32[]{:S(2)}) collective-permute-start(bf16[144,512]{1,0:T(8,128)(2,1)S(1)} %add_convert_fusion.mine_ref), channel_id=1, source_target_pairs={{0,2},{1,3},{2,0},{3,1},{4,6},{5,7},{6,4},{7,5},{8,10},{9,11},{10,... | collective-permute-start | bytes 442376 | tf_op jit(solution)/shard_map/ppermute | solution.py:404
  39.9 6.0 %collective-permute-start.7 = (bf16[2,64,512]{2,1,0:T(8,128)(2,1)S(1)}, bf16[2,64,512]{2,1,0:T(8,128)(2,1)S(1)}, u32[]{:S(2)}, u32[]{:S(2)}) collective-permute-start(bf16[2,64,512]{2,1,0:T(8,128)(2,1)S(1)} %add.27), channel_id=1, source_target_pairs={{0,4},{4,0},{8,24},{12,28},{16,20},{20,16},{24,8},{28,12},{1,5},{5... | collective-permute-start | bytes 393224 | tf_op jit(solution)/shard_map/ppermute | solution.py:414
  42.7 3.2 %collective-permute-start.13 = (bf16[2,64,256]{2,1,0:T(8,128)(2,1)S(1)}, bf16[2,64,256]{2,1,0:T(8,128)(2,1)S(1)}, u32[]{:S(2)}, u32[]{:S(2)}) collective-permute-start(bf16[2,64,256]{2,1,0:T(8,128)(2,1)S(1)} %add.33), channel_id=1, source_target_pairs={{0,4},{4,0},{8,24},{12,28},{16,20},{20,16},{24,8},{28,12},{1,5},{5... | collective-permute-start | bytes 196616 | tf_op jit(solution)/shard_map/ppermute | solution.py:414

commit v6 on v5

--- a/solution.py
+++ b/solution.py
@@ -16,9 +16,9 @@
 DQ = DN + DR
 
 MASKED = -1e30
-GROUP = 8
+GROUP = 16
 VMEM_LIMIT = 6 << 20
-LIMIT_A_TOKEN = 24 << 10
+LIMIT_A_TOKEN = 4 << 10
 LOAD_LIMIT = 4 << 20
 ADD_LIMIT = 2 << 20
 NT = (((1,), (1,)), ((), ()))
@@ -80,9 +80,9 @@
               lse_ref, wuk_ref, wuv_ref, latent_out, rope_out, query_out, grad_out, lse_out,
               delta_out, wuk_out, wuv_out, keys_out, values_out, flat_out, bias_out,
               pos, order, attn, sems, *, ctx_size):
-    pairs = [(latent_ref, latent_out), (order_ref, order), (pos_ref, pos), (rope_ref, rope_out),
-             (wuk_ref, wuk_out), (wuv_ref, wuv_out), (grad_ref, grad_out), (out_ref, attn),
-             (lse_ref, lse_out), (query_ref, query_out)]
+    pairs = [(latent_ref, latent_out), (order_ref, order), (pos_ref, pos), (grad_ref, grad_out),
+             (out_ref, attn), (wuk_ref, wuk_out), (wuv_ref, wuv_out), (query_ref, query_out),
+             (rope_ref, rope_out), (lse_ref, lse_out)]
     copies = [pltpu.make_async_copy(a, b, sems.at[k]) for k, (a, b) in enumerate(pairs)]
     for copy in copies:
         copy.start()
@@ -97,18 +97,18 @@
         bias_out[chunk * rows:(chunk + 1) * rows, :] = jnp.where(key_col <= own_pos, 0.0, MASKED)
     latent = latent_out[...]
     flat_out[...] = rows_first(latent, order[place_ref[0]])
+    copies[3].wait()
     copies[4].wait()
-    keys_out[...] = dot(latent, wuk_out[...]).astype(jnp.bfloat16)
-    copies[5].wait()
-    values_out[...] = dot(latent, wuv_out[...]).astype(jnp.bfloat16)
-    copies[6].wait()
-    copies[7].wait()
     for head in range(delta_out.shape[0]):
         cols = slice(head * DV, (head + 1) * DV)
         product = grad_out[:, cols].astype(jnp.float32) * attn[:, cols].astype(jnp.float32)
         delta_out[head:head + 1, :] = jnp.sum(product.T, axis=0, keepdims=True)
-    for k in (3, 8, 9):
-        copies[k].wait()
+    copies[5].wait()
+    keys_out[...] = dot(latent, wuk_out[...]).astype(jnp.bfloat16)
+    copies[6].wait()
+    values_out[...] = dot(latent, wuv_out[...]).astype(jnp.bfloat16)
+    for copy in copies[7:]:
+        copy.wait()
 
 
 def rows_first(latent, order):
@@ -284,7 +284,7 @@
         out_specs=[vmem] * (4 + ctx_size),
         out_shape=[pltpu.VMEM(loaded[2].shape, jnp.bfloat16), spread, spread, flat]
         + [total] * ctx_size,
-        compiler_params=pltpu.CompilerParams(vmem_limit_bytes=LIMIT_A_TOKEN * ctx_size * rows),
+        compiler_params=pltpu.CompilerParams(vmem_limit_bytes=LIMIT_A_TOKEN * ctx_size * rows * head_count),
         name="grads",
     )(place, *operands)
     return outs[0], outs[1], outs[2], outs[3], outs[4:]
@@ -389,6 +389,7 @@
     head_count = lse.shape[1]
     quarter = head_count // 4
     last = quarter // 2
+    last += last // 2
     counts = [quarter, head_count - quarter - last, last] if last else [head_count]
     chunk_pieces = []
     for chunk, count in enumerate(counts):

time: 46.9 us -> 47.3 us (level)
  waiting for transfers between devices: 15.4 us -> 14.5 us
  starting transfers between devices: 16.7 us -> 17.5 us
    ppermute x3, waiting for transfers between devices: 8.2 us -> 6.96 us  [shifted(): lax.ppermute(value, axis, [(s, (s + steps) % count) for s in range(count)])]
    ppermute x9, starting transfers between devices: 9.24 us -> 10.1 us  [on_device(): arrivals.append(lax.ppermute(value, ('dp', 'ctx'), pairs))]
    pallas_call x3, Pallas kernels: 2 us -> 2.6 us  [chunk_weights(): pl.pallas_call(functools.partial(weights_body, start=start * DN), in_spec...]
  transfers between devices with their start and end apart: 14 -> 14, of which waited for: 5 -> 5; matrix products, arithmetic and copies ran while one was open for 0% -> 0% of each run, Pallas kernels for 14% -> 15%
where the time goes in v6:
time: 47.3 us; the launch traced here: 47.2 us
  starting transfers between devices  17.5 us (37%)
  waiting for transfers between devices  14.5 us (31%)
  Pallas kernels  14.2 us (30%)
  between operations  0.76 us (2%)
    ppermute x9, starting transfers between devices, on_device(): arrivals.append(lax.ppermute(value, ('dp', 'ctx'), pairs))  10.1 us
    ppermute x9, waiting for transfers between devices, on_device(): arrivals.append(lax.ppermute(value, ('dp', 'ctx'), pairs))  7.55 us
    ppermute x3, waiting for transfers between devices, shifted(): lax.ppermute(value, axis, [(s, (s + steps) % count) for s in range(count)])  6.96 us
    pallas_call x1, Pallas kernels, all_grads(): pl.pallas_call(functools.partial(grads_body, ctx_size=ctx_size, group=mat...  4.71 us
    ppermute x2, starting transfers between devices, on_device(): other = lax.ppermute(mine, 'head', [(s, s ^ bit) for s in range(head_size)])  3.95 us
    pallas_call x1, Pallas kernels, load(): pl.pallas_call(functools.partial(load_body, ctx_size=ctx_size), in_specs=...  3.73 us
    ppermute x3, starting transfers between devices, shifted(): lax.ppermute(value, axis, [(s, (s + steps) % count) for s in range(count)])  3.42 us
    pallas_call x3, Pallas kernels, chunk_weights(): pl.pallas_call(functools.partial(weights_body, start=start * DN), in_spec...  2.6 us
  transfers between devices with their start and end apart: 14, of which 5 were waited for; matrix products, arithmetic and copies ran while one was open for 0% of the time, Pallas kernels for 15%

profile of v6, /device:TPU:1, one launch (start us, length us, event | category | flops | bytes accessed | tf_op | source)
XLA Modules:
  0.0 47.2 jit_solution(13823918322176841673)
XLA Ops:
  0.6 2.1 %collective-permute-start = (bf16[128,512]{1,0:T(8,128)(2,1)}, bf16[128,512]{1,0:T(8,128)(2,1)S(1)}, u32[]{:S(2)}, u32[]{:S(2)}) collective-permute-start(bf16[128,512]{1,0:T(8,128)(2,1)} %bitcast.20), channel_id=1, source_target_pairs={{0,4},{4,0},{1,5},{5,1},{2,6},{6,2},{3,7},{7,3},{8,12},{12,8},{9,1... | collective-permute-start | bytes 393224 | tf_op jit(solution)/shard_map/ppermute | solution.py:373
  2.8 0.1 collective-permute-start.1
  2.8 0.1 pad_add_fusion.place_ref
  2.9 3.7 %load.1 = (bf16[128,512]{1,0:T(8,128)(2,1)S(1)}, bf16[64,128]{1,0:T(8,128)(2,1)S(1)}, bf16[128,3072]{1,0:T(8,128)(2,1)S(1)}, bf16[128,2048]{1,0:T(8,128)(2,1)S(1...) custom-call(s32[2]{0:T(128)S(1)} %pad_add_fusion.place_ref, ...), custom_call_target="tpu_custom_call" | custom-call | tf_op jit(solution)/shard_map/load/pallas_call | solution.py:260
  6.7 4.7 %grads.1 = (bf16[128,3072]{1,0:T(8,128)(2,1)S(1)}, bf16[256,2048]{1,0:T(8,128)(2,1)S(1)}, bf16[256,2048]{1,0:T(8,128)(2,1)S(1)}, bf16[512,256]{1,0:T(8,128)(2,1)...) custom-call(s32[2]{0:T(128)S(1)} %pad_add_fusion.place_ref, s32[8,1,512]{2,1,0:T(1,128)S(1)} %copy-done, ...), custom_call_target="tpu_custom_call" | custom-call | tf_op jit(solution)/shard_map/grads/pallas_call | solution.py:281
  11.4 1.5 %weights.4 = (bf16[2,256,1152]{2,1,0:T(8,128)(2,1)S(1)}, bf16[2,128,1152]{2,1,0:T(8,128)(2,1)S(1)}, bf16[2,64,1152]{2,1,0:T(8,128)(2,1)S(1)}, bf16[2,64,1152]{2,1,0:T(8,128)(2,1)S(1)}) custom-call(bf16[512,256]{1,0:T(8,128)(2,1)S(1)} %get-tuple-element.56.flat_ref, bf16[256,2048]{1,0:T(8,128)(2,1)S(1)} %get-tuple-element.57.key_ref, ...), custom_call_target="tpu_custom_call" | custom-call | tf_op jit(solution)/shard_map/weights/pallas_call | solution.py:235
  12.9 1.2 %collective-permute-start.8 = (bf16[2,256,1152]{2,1,0:T(8,128)(2,1)S(1)}, bf16[2,256,1152]{2,1,0:T(8,128)(2,1)S(1)}, u32[]{:S(2)}, u32[]{:S(2)}) collective-permute-start(bf16[2,256,1152]{2,1,0:T(8,128)(2,1)S(1)} %get-tuple-element.64), channel_id=1, source_target_pairs={{0,8},{4,12},{8,0},{12,4},{16,24},{20,28},{24,16},{28,20},{1,9},{5... | collective-permute-start | bytes 3538952 | tf_op jit(solution)/shard_map/ppermute | solution.py:415
  14.0 2.5 %collective-permute-done.8.refs_1_ = bf16[2,256,1152]{2,1,0:T(8,128)(2,1)S(1)} collective-permute-done((bf16[2,256,1152]{2,1,0:T(8,128)(2,1)S(1)}, bf16[2,256,1152]{2,1,0:T(8,128)(2,1)S(1)}, u32[]{:S(2)}, u32[]{:S(2)}) %collective-permute-start.8) | collective-permute-done | bytes 1179680 | tf_op jit(solution)/shard_map/ppermute | solution.py:415
  16.5 0.2 add.28
  16.7 1.6 %collective-permute-start.9 = (bf16[2,128,1152]{2,1,0:T(8,128)(2,1)S(1)}, bf16[2,128,1152]{2,1,0:T(8,128)(2,1)S(1)}, u32[]{:S(2)}, u32[]{:S(2)}) collective-permute-start(bf16[2,128,1152]{2,1,0:T(8,128)(2,1)S(1)} %add.28), channel_id=1, source_target_pairs={{0,16},{4,20},{8,12},{12,8},{16,0},{20,4},{24,28},{28,24},{1,17},{... | collective-permute-start | bytes 1769480 | tf_op jit(solution)/shard_map/ppermute | solution.py:415
  18.3 0.5 %weights.3 = (bf16[2,256,512]{2,1,0:T(8,128)(2,1)S(1)}, bf16[2,128,512]{2,1,0:T(8,128)(2,1)S(1)}, bf16[2,64,512]{2,1,0:T(8,128)(2,1)S(1)}, bf16[2,64,512]{2,1,0:T(8,128)(2,1)S(1)}) custom-call(bf16[512,256]{1,0:T(8,128)(2,1)S(1)} %get-tuple-element.56.flat_ref, bf16[256,2048]{1,0:T(8,128)(2,1)S(1)} %get-tuple-element.57.key_ref, ...), custom_call_target="tpu_custom_call" | custom-call | tf_op jit(solution)/shard_map/weights/pallas_call | solution.py:235
  18.8 0.7 %collective-permute-start.5 = (bf16[2,256,512]{2,1,0:T(8,128)(2,1)S(1)}, bf16[2,256,512]{2,1,0:T(8,128)(2,1)S(1)}, u32[]{:S(2)}, u32[]{:S(2)}) collective-permute-start(bf16[2,256,512]{2,1,0:T(8,128)(2,1)S(1)} %get-tuple-element.60), channel_id=1, source_target_pairs={{0,8},{4,12},{8,0},{12,4},{16,24},{20,28},{24,16},{28,20},{1,9},{5... | collective-permute-start | bytes 1572872 | tf_op jit(solution)/shard_map/ppermute | solution.py:415
  19.5 1.2 %collective-permute-start.2 = (bf16[144,512]{1,0:T(8,128)(2,1)S(1)}, bf16[144,512]{1,0:T(8,128)(2,1)S(1)}, u32[]{:S(2)}, u32[]{:S(2)}) collective-permute-start(bf16[144,512]{1,0:T(8,128)(2,1)S(1)} %get-tuple-element.53), channel_id=1, source_target_pairs={{0,4},{4,0},{1,5},{5,1},{2,6},{6,2},{3,7},{7,3},{8,12},{12,8},{9,1... | collective-permute-start | bytes 442376 | tf_op jit(solution)/shard_map/ppermute | solution.py:373
  20.7 0.6 %weights.5 = (bf16[2,256,384]{2,1,0:T(8,128)(2,1)S(1)}, bf16[2,128,384]{2,1,0:T(8,128)(2,1)S(1)}, bf16[2,64,384]{2,1,0:T(8,128)(2,1)S(1)}, bf16[2,64,384]{2,1,0:T(8,128)(2,1)S(1)}) custom-call(bf16[512,256]{1,0:T(8,128)(2,1)S(1)} %get-tuple-element.56.flat_ref, bf16[256,2048]{1,0:T(8,128)(2,1)S(1)} %get-tuple-element.57.key_ref, ...), custom_call_target="tpu_custom_call" | custom-call | tf_op jit(solution)/shard_map/weights/pallas_call | solution.py:235
  21.3 0.4 collective-permute-start.11
  21.8 7.0 %collective-permute-done.2 = bf16[144,512]{1,0:T(8,128)(2,1)S(1)} collective-permute-done((bf16[144,512]{1,0:T(8,128)(2,1)S(1)}, bf16[144,512]{1,0:T(8,128)(2,1)S(1)}, u32[]{:S(2)}, u32[]{:S(2)}) %collective-permute-start.2) | collective-permute-done | bytes 147488 | tf_op jit(solution)/shard_map/ppermute | solution.py:373
  28.8 1.6 %collective-permute-start.3 = (bf16[144,512]{1,0:T(8,128)(2,1)S(1)}, bf16[144,512]{1,0:T(8,128)(2,1)S(1)}, u32[]{:S(2)}, u32[]{:S(2)}) collective-permute-start(bf16[144,512]{1,0:T(8,128)(2,1)S(1)} %add_convert_fusion.1), channel_id=1, source_target_pairs={{0,1},{1,0},{2,3},{3,2},{4,5},{5,4},{6,7},{7,6},{8,9},{9,8},{10,11... | collective-permute-start | bytes 442376 | tf_op jit(solution)/shard_map/ppermute | solution.py:405
  30.3 0.1 add.25
  30.4 1.3 %collective-permute-start.6 = (bf16[2,128,512]{2,1,0:T(8,128)(2,1)S(1)}, bf16[2,128,512]{2,1,0:T(8,128)(2,1)S(1)}, u32[]{:S(2)}, u32[]{:S(2)}) collective-permute-start(bf16[2,128,512]{2,1,0:T(8,128)(2,1)S(1)} %add.25), channel_id=1, source_target_pairs={{0,16},{4,20},{8,12},{12,8},{16,0},{20,4},{24,28},{28,24},{1,17},{... | collective-permute-start | bytes 786440 | tf_op jit(solution)/shard_map/ppermute | solution.py:415
  31.8 0.3 collective-permute-start.12
  32.1 0.1 add.30
  32.2 1.4 %collective-permute-start.10 = (bf16[2,64,1152]{2,1,0:T(8,128)(2,1)S(1)}, bf16[2,64,1152]{2,1,0:T(8,128)(2,1)S(1)}, u32[]{:S(2)}, u32[]{:S(2)}) collective-permute-start(bf16[2,64,1152]{2,1,0:T(8,128)(2,1)S(1)} %add.30), channel_id=1, source_target_pairs={{0,4},{4,0},{8,24},{12,28},{16,20},{20,16},{24,8},{28,12},{1,5},{5... | collective-permute-start | bytes 884744 | tf_op jit(solution)/shard_map/ppermute | solution.py:415
  33.6 2.4 %collective-permute-start.4 = (bf16[144,512]{1,0:T(8,128)(2,1)S(1)}, bf16[144,512]{1,0:T(8,128)(2,1)S(1)}, u32[]{:S(2)}, u32[]{:S(2)}) collective-permute-start(bf16[144,512]{1,0:T(8,128)(2,1)S(1)} %add_convert_fusion.mine_ref), channel_id=1, source_target_pairs={{0,2},{1,3},{2,0},{3,1},{4,6},{5,7},{6,4},{7,5},{8,10},{9,11},{10,... | collective-permute-start | bytes 442376 | tf_op jit(solution)/shard_map/ppermute | solution.py:405
  36.0 2.4 %collective-permute-done.6.refs_2_ = bf16[2,128,512]{2,1,0:T(8,128)(2,1)S(1)} collective-permute-done((bf16[2,128,512]{2,1,0:T(8,128)(2,1)S(1)}, bf16[2,128,512]{2,1,0:T(8,128)(2,1)S(1)}, u32[]{:S(2)}, u32[]{:S(2)}) %collective-permute-start.6) | collective-permute-done | bytes 262176 | tf_op jit(solution)/shard_map/ppermute | solution.py:415
  38.4 1.6 %collective-permute-start.7 = (bf16[2,64,512]{2,1,0:T(8,128)(2,1)S(1)}, bf16[2,64,512]{2,1,0:T(8,128)(2,1)S(1)}, u32[]{:S(2)}, u32[]{:S(2)}) collective-permute-start(bf16[2,64,512]{2,1,0:T(8,128)(2,1)S(1)} %add.27), channel_id=1, source_target_pairs={{0,4},{4,0},{8,24},{12,28},{16,20},{20,16},{24,8},{28,12},{1,5},{5... | collective-permute-start | bytes 393224 | tf_op jit(solution)/shard_map/ppermute | solution.py:415
  40.0 2.5 %collective-permute-done.12.refs_2_ = bf16[2,128,384]{2,1,0:T(8,128)(2,1)S(1)} collective-permute-done((bf16[2,128,384]{2,1,0:T(8,128)(2,1)S(1)}, bf16[2,128,384]{2,1,0:T(8,128)(2,1)S(1)}, u32[]{:S(2)}, u32[]{:S(2)}) %collective-permute-start.12) | collective-permute-done | bytes 196640 | tf_op jit(solution)/shard_map/ppermute | solution.py:415
  42.6 1.6 %collective-permute-start.13 = (bf16[2,64,384]{2,1,0:T(8,128)(2,1)S(1)}, bf16[2,64,384]{2,1,0:T(8,128)(2,1)S(1)}, u32[]{:S(2)}, u32[]{:S(2)}) collective-permute-start(bf16[2,64,384]{2,1,0:T(8,128)(2,1)S(1)} %add.33), channel_id=1, source_target_pairs={{0,4},{4,0},{8,24},{12,28},{16,20},{20,16},{24,8},{28,12},{1,5},{5... | collective-permute-start | bytes 294920 | tf_op jit(solution)/shard_map/ppermute | solution.py:415
  44.2 0.9 %store.1 = bf16[128,3072]{1,0:T(8,128)(2,1)} custom-call(bf16[128,3072]{1,0:T(8,128)(2,1)S(1)} %get-tuple-element.51.source_ref), custom_call_target="tpu_custom_call" | custom-call | tf_op jit(solution)/shard_map/store/pallas_call | solution.py:212
  45.1 0.7 %finish.1 = (f32[128,512]{1,0:T(8,128)}, f32[64,128]{1,0:T(8,128)}) custom-call(bf16[144,512]{1,0:T(8,128)(2,1)S(1)} %add_convert_fusion.mine_ref, bf16[144,512]{1,0:T(8,128)(2,1)S(1)} %collective-permute-done.4.other_ref), custom_call_target="tpu_custom_call" | custom-call | tf_op jit(solution)/shard_map/finish/pallas_call | solution.py:316
  46.0 0.1 add.29.refs_2_
  46.1 0.1 collective-permute-done.13.refs_5_
  46.3 0.9 %last.1 = (bf16[64,2048]{1,0:T(8,128)(2,1)}, bf16[64,2048]{1,0:T(8,128)(2,1)}) custom-call(bf16[2,64,512]{2,1,0:T(8,128)(2,1)S(1)} %add.26.refs_0_, bf16[2,64,512]{2,1,0:T(8,128)(2,1)S(1)} %collective-permute-done.7.refs_1_, bf16[2,64,1152]{2,1,0:T(8,128)(2,1)S(1)} %add.29.refs_2_, bf16[2,64,1152]{2,1,0:T(8,128)(2,1)S(1)} %collective-permute-done.10.refs_3_, ...), custom_call_target="tpu_custom_call" | custom-call | tf_op jit(solution)/shard_map/last/pallas_call | solution.py:361
  (18 shorter events, 0.3 us)
Async XLA Ops:
  0.6 6.0 %collective-permute-start = (bf16[128,512]{1,0:T(8,128)(2,1)}, bf16[128,512]{1,0:T(8,128)(2,1)S(1)}, u32[]{:S(2)}, u32[]{:S(2)}) collective-permute-start(bf16[128,512]{1,0:T(8,128)(2,1)} %bitcast.20), channel_id=1, source_target_pairs={{0,4},{4,0},{1,5},{5,1},{2,6},{6,2},{3,7},{7,3},{8,12},{12,8},{9,1... | collective-permute-start | bytes 393224 | tf_op jit(solution)/shard_map/ppermute | solution.py:373
  2.8 3.9 %collective-permute-start.1 = (bf16[64,128]{1,0:T(8,128)(2,1)}, bf16[64,128]{1,0:T(8,128)(2,1)S(1)}, u32[]{:S(2)}, u32[]{:S(2)}) collective-permute-start(bf16[64,128]{1,0:T(8,128)(2,1)} %bitcast.22), channel_id=1, source_target_pairs={{0,4},{4,0},{1,5},{5,1},{2,6},{6,2},{3,7},{7,3},{8,12},{12,8},{9,1... | collective-permute-start | bytes 49160 | tf_op jit(solution)/shard_map/ppermute | solution.py:373
  2.9 3.8 %copy-start = (s32[8,1,512]{2,1,0:T(1,128)S(1)}, s32[8,1,512]{2,1,0:T(1,128)}, u32[]{:S(2)}) copy-start(s32[8,1,512]{2,1,0:T(1,128)} %constant.22.order_ref) | copy-start | bytes 49156
  12.9 3.6 %collective-permute-start.8 = (bf16[2,256,1152]{2,1,0:T(8,128)(2,1)S(1)}, bf16[2,256,1152]{2,1,0:T(8,128)(2,1)S(1)}, u32[]{:S(2)}, u32[]{:S(2)}) collective-permute-start(bf16[2,256,1152]{2,1,0:T(8,128)(2,1)S(1)} %get-tuple-element.64), channel_id=1, source_target_pairs={{0,8},{4,12},{8,0},{12,4},{16,24},{20,28},{24,16},{28,20},{1,9},{5... | collective-permute-start | bytes 3538952 | tf_op jit(solution)/shard_map/ppermute | solution.py:415
  16.7 15.4 %collective-permute-start.9 = (bf16[2,128,1152]{2,1,0:T(8,128)(2,1)S(1)}, bf16[2,128,1152]{2,1,0:T(8,128)(2,1)S(1)}, u32[]{:S(2)}, u32[]{:S(2)}) collective-permute-start(bf16[2,128,1152]{2,1,0:T(8,128)(2,1)S(1)} %add.28), channel_id=1, source_target_pairs={{0,16},{4,20},{8,12},{12,8},{16,0},{20,4},{24,28},{28,24},{1,17},{... | collective-permute-start | bytes 1769480 | tf_op jit(solution)/shard_map/ppermute | solution.py:415
  18.8 11.5 %collective-permute-start.5 = (bf16[2,256,512]{2,1,0:T(8,128)(2,1)S(1)}, bf16[2,256,512]{2,1,0:T(8,128)(2,1)S(1)}, u32[]{:S(2)}, u32[]{:S(2)}) collective-permute-start(bf16[2,256,512]{2,1,0:T(8,128)(2,1)S(1)} %get-tuple-element.60), channel_id=1, source_target_pairs={{0,8},{4,12},{8,0},{12,4},{16,24},{20,28},{24,16},{28,20},{1,9},{5... | collective-permute-start | bytes 1572872 | tf_op jit(solution)/shard_map/ppermute | solution.py:415
  19.5 9.2 %collective-permute-start.2 = (bf16[144,512]{1,0:T(8,128)(2,1)S(1)}, bf16[144,512]{1,0:T(8,128)(2,1)S(1)}, u32[]{:S(2)}, u32[]{:S(2)}) collective-permute-start(bf16[144,512]{1,0:T(8,128)(2,1)S(1)} %get-tuple-element.53), channel_id=1, source_target_pairs={{0,4},{4,0},{1,5},{5,1},{2,6},{6,2},{3,7},{7,3},{8,12},{12,8},{9,1... | collective-permute-start | bytes 442376 | tf_op jit(solution)/shard_map/ppermute | solution.py:373
  21.3 10.4 %collective-permute-start.11 = (bf16[2,256,384]{2,1,0:T(8,128)(2,1)S(1)}, bf16[2,256,384]{2,1,0:T(8,128)(2,1)S(1)}, u32[]{:S(2)}, u32[]{:S(2)}) collective-permute-start(bf16[2,256,384]{2,1,0:T(8,128)(2,1)S(1)} %get-tuple-element.68), channel_id=1, source_target_pairs={{0,8},{4,12},{8,0},{12,4},{16,24},{20,28},{24,16},{28,20},{1,9},{5... | collective-permute-start | bytes 1179656 | tf_op jit(solution)/shard_map/ppermute | solution.py:415
  28.8 4.8 %collective-permute-start.3 = (bf16[144,512]{1,0:T(8,128)(2,1)S(1)}, bf16[144,512]{1,0:T(8,128)(2,1)S(1)}, u32[]{:S(2)}, u32[]{:S(2)}) collective-permute-start(bf16[144,512]{1,0:T(8,128)(2,1)S(1)} %add_convert_fusion.1), channel_id=1, source_target_pairs={{0,1},{1,0},{2,3},{3,2},{4,5},{5,4},{6,7},{7,6},{8,9},{9,8},{10,11... | collective-permute-start | bytes 442376 | tf_op jit(solution)/shard_map/ppermute | solution.py:405
  30.4 7.9 %collective-permute-start.6 = (bf16[2,128,512]{2,1,0:T(8,128)(2,1)S(1)}, bf16[2,128,512]{2,1,0:T(8,128)(2,1)S(1)}, u32[]{:S(2)}, u32[]{:S(2)}) collective-permute-start(bf16[2,128,512]{2,1,0:T(8,128)(2,1)S(1)} %add.25), channel_id=1, source_target_pairs={{0,16},{4,20},{8,12},{12,8},{16,0},{20,4},{24,28},{28,24},{1,17},{... | collective-permute-start | bytes 786440 | tf_op jit(solution)/shard_map/ppermute | solution.py:415
  31.8 10.8 %collective-permute-start.12 = (bf16[2,128,384]{2,1,0:T(8,128)(2,1)S(1)}, bf16[2,128,384]{2,1,0:T(8,128)(2,1)S(1)}, u32[]{:S(2)}, u32[]{:S(2)}) collective-permute-start(bf16[2,128,384]{2,1,0:T(8,128)(2,1)S(1)} %add.31), channel_id=1, source_target_pairs={{0,16},{4,20},{8,12},{12,8},{16,0},{20,4},{24,28},{28,24},{1,17},{... | collective-permute-start | bytes 589832 | tf_op jit(solution)/shard_map/ppermute | solution.py:415
  32.2 14.1 %collective-permute-start.10 = (bf16[2,64,1152]{2,1,0:T(8,128)(2,1)S(1)}, bf16[2,64,1152]{2,1,0:T(8,128)(2,1)S(1)}, u32[]{:S(2)}, u32[]{:S(2)}) collective-permute-start(bf16[2,64,1152]{2,1,0:T(8,128)(2,1)S(1)} %add.30), channel_id=1, source_target_pairs={{0,4},{4,0},{8,24},{12,28},{16,20},{20,16},{24,8},{28,12},{1,5},{5... | collective-permute-start | bytes 884744 | tf_op jit(solution)/shard_map/ppermute | solution.py:415
  33.6 11.5 %collective-permute-start.4 = (bf16[144,512]{1,0:T(8,128)(2,1)S(1)}, bf16[144,512]{1,0:T(8,128)(2,1)S(1)}, u32[]{:S(2)}, u32[]{:S(2)}) collective-permute-start(bf16[144,512]{1,0:T(8,128)(2,1)S(1)} %add_convert_fusion.mine_ref), channel_id=1, source_target_pairs={{0,2},{1,3},{2,0},{3,1},{4,6},{5,7},{6,4},{7,5},{8,10},{9,11},{10,... | collective-permute-start | bytes 442376 | tf_op jit(solution)/shard_map/ppermute | solution.py:405
  38.4 7.8 %collective-permute-start.7 = (bf16[2,64,512]{2,1,0:T(8,128)(2,1)S(1)}, bf16[2,64,512]{2,1,0:T(8,128)(2,1)S(1)}, u32[]{:S(2)}, u32[]{:S(2)}) collective-permute-start(bf16[2,64,512]{2,1,0:T(8,128)(2,1)S(1)} %add.27), channel_id=1, source_target_pairs={{0,4},{4,0},{8,24},{12,28},{16,20},{20,16},{24,8},{28,12},{1,5},{5... | collective-permute-start | bytes 393224 | tf_op jit(solution)/shard_map/ppermute | solution.py:415
  42.6 3.6 %collective-permute-start.13 = (bf16[2,64,384]{2,1,0:T(8,128)(2,1)S(1)}, bf16[2,64,384]{2,1,0:T(8,128)(2,1)S(1)}, u32[]{:S(2)}, u32[]{:S(2)}) collective-permute-start(bf16[2,64,384]{2,1,0:T(8,128)(2,1)S(1)} %add.33), channel_id=1, source_target_pairs={{0,4},{4,0},{8,24},{12,28},{16,20},{20,16},{24,8},{28,12},{1,5},{5... | collective-permute-start | bytes 294920 | tf_op jit(solution)/shard_map/ppermute | solution.py:415
